TPU v7x, 32 devices: a whole 2x2x4 slice. The times are simulated.
32 devices in a mesh: fsdp: 4 (over y, core), context: 4 (over z), tensor: 2 (over x).
Axes of the slice: x: 2, y: 2, z: 4, core: 2. Of those that a mesh axis runs over, the one named last changes fastest.
Arguments:
- hidden_in: float32 [4, 512, 2560], P('fsdp', 'context'), may hold values from -6 to 6
- cotangent: float32 [4, 512, 2560], P('fsdp', 'context'), may hold values from -6 to 6
- segment_ids: int32 [4, 512], P('fsdp', 'context'), may hold values from 0 to 3, as said below
- positions: int32 [4, 512], P('fsdp', 'context'), may hold values from 0 to 511, as said below
- attn_scale: float32 [2560], P(('fsdp', 'context')), may hold values from -0.5 to 0.5
- query_weight: float32 [2560, 2560], P(('fsdp', 'context'), 'tensor')
- keyval_weight: float32 [2560, 512], P(('fsdp', 'context'))
- output_weight: float32 [2560, 2560], P('tensor', ('fsdp', 'context')), may hold values from -0.5 to 0.5
- mlp_scale: float32 [2560], P(('fsdp', 'context')), may hold values from -0.5 to 0.5
- gate_weight: float32 [2560, 7680], P(('fsdp', 'context'), 'tensor'), may hold values from -0.125 to 0.125
- up_weight: float32 [2560, 7680], P(('fsdp', 'context'), 'tensor'), may hold values from -0.125 to 0.125
- down_weight: float32 [7680, 2560], P('tensor', ('fsdp', 'context')), may hold values from -0.0625 to 0.0625
- first_attn_scale: float32 [2560], P(('fsdp', 'context')), may hold values from -40 to 40
- first_query_weight: float32 [2560, 2560], P(('fsdp', 'context'), 'tensor'), may hold values from -16 to 16
- first_keyval_weight: float32 [2560, 512], P(('fsdp', 'context')), may hold values from -80 to 80
- first_output_weight: float32 [2560, 2560], P('tensor', ('fsdp', 'context')), may hold values from -4 to 4
- first_mlp_scale: float32 [2560], P(('fsdp', 'context')), may hold values from -20 to 20
- first_gate_weight: float32 [2560, 7680], P(('fsdp', 'context'), 'tensor'), may hold values from -16 to 16
- first_up_weight: float32 [2560, 7680], P(('fsdp', 'context'), 'tensor'), may hold values from -16 to 16
- first_down_weight: float32 [7680, 2560], P('tensor', ('fsdp', 'context')), may hold values from -24 to 24
- second_attn_scale: float32 [2560], P(('fsdp', 'context')), may hold values from 0.6144 to 6.144
- second_query_weight: float32 [2560, 2560], P(('fsdp', 'context'), 'tensor'), may hold values from 0.1024 to 1.024
- second_keyval_weight: float32 [2560, 512], P(('fsdp', 'context')), may hold values from 2.4576 to 24.576
- second_output_weight: float32 [2560, 2560], P('tensor', ('fsdp', 'context')), may hold values from 0.006 to 0.06
- second_mlp_scale: float32 [2560], P(('fsdp', 'context')), may hold values from 0.2048 to 2.048
- second_gate_weight: float32 [2560, 7680], P(('fsdp', 'context'), 'tensor'), may hold values from 0.1024 to 1.024
- second_up_weight: float32 [2560, 7680], P(('fsdp', 'context'), 'tensor'), may hold values from 0.1024 to 1.024
- second_down_weight: float32 [7680, 2560], P('tensor', ('fsdp', 'context')), may hold values from 0.2048 to 2.048
Outputs:
- block_output: float32 [4, 512, 2560], P('fsdp', 'context')
- input_grad: float32 [4, 512, 2560], P('fsdp', 'context')
- grad_attn_scale: float32 [2560], P(('fsdp', 'context'))
- grad_query_weight: float32 [2560, 2560], P(('fsdp', 'context'), 'tensor')
- grad_keyval_weight: float32 [2560, 512], P(('fsdp', 'context'))
- grad_output_weight: float32 [2560, 2560], P('tensor', ('fsdp', 'context'))
- grad_mlp_scale: float32 [2560], P(('fsdp', 'context'))
- grad_gate_weight: float32 [2560, 7680], P(('fsdp', 'context'), 'tensor')
- grad_up_weight: float32 [2560, 7680], P(('fsdp', 'context'), 'tensor')
- grad_down_weight: float32 [7680, 2560], P('tensor', ('fsdp', 'context'))
- new_attn_scale: float32 [2560], P(('fsdp', 'context'))
- new_query_weight: float32 [2560, 2560], P(('fsdp', 'context'), 'tensor')
- new_keyval_weight: float32 [2560, 512], P(('fsdp', 'context'))
- new_output_weight: float32 [2560, 2560], P('tensor', ('fsdp', 'context'))
- new_mlp_scale: float32 [2560], P(('fsdp', 'context'))
- new_gate_weight: float32 [2560, 7680], P(('fsdp', 'context'), 'tensor')
- new_up_weight: float32 [2560, 7680], P(('fsdp', 'context'), 'tensor')
- new_down_weight: float32 [7680, 2560], P('tensor', ('fsdp', 'context'))
- new_first_attn_scale: float32 [2560], P(('fsdp', 'context'))
- new_first_query_weight: float32 [2560, 2560], P(('fsdp', 'context'), 'tensor')
- new_first_keyval_weight: float32 [2560, 512], P(('fsdp', 'context'))
- new_first_output_weight: float32 [2560, 2560], P('tensor', ('fsdp', 'context'))
- new_first_mlp_scale: float32 [2560], P(('fsdp', 'context'))
- new_first_gate_weight: float32 [2560, 7680], P(('fsdp', 'context'), 'tensor')
- new_first_up_weight: float32 [2560, 7680], P(('fsdp', 'context'), 'tensor')
- new_first_down_weight: float32 [7680, 2560], P('tensor', ('fsdp', 'context'))
- new_second_attn_scale: float32 [2560], P(('fsdp', 'context'))
- new_second_query_weight: float32 [2560, 2560], P(('fsdp', 'context'), 'tensor')
- new_second_keyval_weight: float32 [2560, 512], P(('fsdp', 'context'))
- new_second_output_weight: float32 [2560, 2560], P('tensor', ('fsdp', 'context'))
- new_second_mlp_scale: float32 [2560], P(('fsdp', 'context'))
- new_second_gate_weight: float32 [2560, 7680], P(('fsdp', 'context'), 'tensor')
- new_second_up_weight: float32 [2560, 7680], P(('fsdp', 'context'), 'tensor')
- new_second_down_weight: float32 [7680, 2560], P('tensor', ('fsdp', 'context'))
Inputs may be any that keep to these rules, and one draw needn't show every extreme that they name: segment_ids start at 0 and never fall along a sequence; a document is a run of equal values; the first sequence is one document, every other sequence holds four. positions count the tokens from the first token of the token's document, which has 0.
All inputs are finite; a program needn't handle non-finite values.
Results may differ from a plain program's by a relative error of at most 0.014.
Values may be sent and summed in bfloat16 or wider, within the bound.
A program may use at most 448 MiB of HBM per device.

v0:
```python
import jax
import jax.numpy as jnp
from jax import lax
from jax.sharding import PartitionSpec as P

HD = 256


norm_eps = 1e-06
beta_one = 0.9
beta_two = 0.999
adam_eps = 1e-08
learn_rate = 0.03
decay_rate = 0.1
adam_step = 4.0
rope_base = 10000.0
masked_value = -1e30

single = jnp.float32
half_type = jnp.bfloat16


def gelu_tanh(values):
    return jax.nn.gelu(values, approximate=True)


def rope_tables(positions):
    half = HD // 2
    freq = rope_base ** (-2.0 * jnp.arange(half).astype(jnp.float32) / HD)
    angle = positions.astype(jnp.float32)[..., None] * freq
    return (jnp.cos(angle), jnp.sin(angle))


def rotate(values, cosine, sine):
    half = values.shape[-1] // 2
    first = values[..., :half]
    second = values[..., half:]
    return jnp.concatenate(
        [first * cosine - second * sine, second * cosine + first * sine], axis=-1
    )


def unrotate(values, cosine, sine):
    half = values.shape[-1] // 2
    first = values[..., :half]
    second = values[..., half:]
    return jnp.concatenate(
        [first * cosine + second * sine, second * cosine - first * sine], axis=-1
    )


def rms_forward(values, scale):
    inverse = lax.rsqrt(jnp.mean(values * values, axis=-1, keepdims=True) + norm_eps)
    normed = values * inverse
    return (normed, inverse, (normed * (1.0 + scale)).astype(jnp.bfloat16))


def rms_backward(dnorm, normed, inverse, scale):
    dnormed = dnorm * (1.0 + scale)
    dvalues = inverse * (dnormed - normed * jnp.mean(dnormed * normed, axis=-1, keepdims=True))
    return (dvalues, dnorm * normed)


def adamw(weight, grad, first, second):
    first_new = beta_one * first + (1.0 - beta_one) * grad
    second_new = beta_two * second + (1.0 - beta_two) * grad * grad
    fix_one = 1.0 - beta_one**adam_step
    fix_two = 1.0 - beta_two**adam_step
    update = first_new / fix_one / (jnp.sqrt(second_new / fix_two) + adam_eps)
    return (weight - learn_rate * (update + decay_rate * weight), first_new, second_new)


def dot(a, b, dims):
    return lax.dot_general(a, b, (dims, ((), ())), preferred_element_type=single)


def small_gather(attn_scale, mlp_scale, segment_ids):
    scales = jnp.stack([attn_scale, mlp_scale]).astype(half_type)
    scales = lax.all_gather(scales, ("fsdp", "context"), axis=1, tiled=True).astype(single)
    seg_all = lax.all_gather(segment_ids, "context", axis=1, tiled=True)
    return scales[0], scales[1], seg_all


def gather_rows(block):
    return lax.all_gather(block, ("fsdp", "context"), axis=0, tiled=True)


def prepare_slice(block):
    rows, columns = block.shape
    ctx = lax.axis_size("context")
    parts = block.reshape(rows, ctx, columns // ctx).transpose(1, 0, 2)
    parts = lax.all_to_all(parts, "context", split_axis=0, concat_axis=0, tiled=True)
    full = lax.all_gather(parts, "fsdp", axis=0, tiled=True)
    return full.reshape(-1, columns // ctx)


def gather_tokens(block):
    return lax.all_gather(block, ("context", "tensor"), axis=0, tiled=True)


def scatter_tokens(part):
    return lax.psum_scatter(
        part.astype(half_type), ("context", "tensor"), scatter_dimension=0, tiled=True
    ).astype(single)


def scatter_rows(part):
    return lax.psum_scatter(
        part.astype(half_type), ("fsdp", "context"), scatter_dimension=0, tiled=True
    ).astype(single)


def return_slice(part):
    full, columns = part.shape
    ctx = lax.axis_size("context")
    fs = lax.axis_size("fsdp")
    rows = full // (ctx * fs)
    parts = part.astype(half_type).reshape(fs * ctx, rows, columns)
    parts = lax.psum_scatter(parts, "fsdp", scatter_dimension=0, tiled=True)
    parts = lax.all_to_all(parts, "context", split_axis=0, concat_axis=0, tiled=True)
    return parts.transpose(1, 0, 2).reshape(rows, ctx * columns).astype(single)


def on_device(
    hidden_in,
    cotangent,
    segment_ids,
    positions,
    attn_scale,
    query_weight,
    keyval_weight,
    output_weight,
    mlp_scale,
    gate_weight,
    up_weight,
    down_weight,
    first_attn_scale,
    first_query_weight,
    first_keyval_weight,
    first_output_weight,
    first_mlp_scale,
    first_gate_weight,
    first_up_weight,
    first_down_weight,
    second_attn_scale,
    second_query_weight,
    second_keyval_weight,
    second_output_weight,
    second_mlp_scale,
    second_gate_weight,
    second_up_weight,
    second_down_weight,
):
    ten = lax.axis_size("tensor")
    x = lax.axis_index("tensor")
    context_index = lax.axis_index("context")
    block, width = hidden_in.shape[1:]
    half_rows = block // ten
    heads_here = query_weight.shape[1] // HD
    heads_width = heads_here * HD
    hidden = hidden_in[0]
    cot = cotangent[0]
    hidden_half = lax.dynamic_slice_in_dim(hidden, x * half_rows, half_rows, 0)
    cot_half = lax.dynamic_slice_in_dim(cot, x * half_rows, half_rows, 0)

    scale_one, scale_two, seg_all = small_gather(attn_scale, mlp_scale, segment_ids)
    query_full = gather_rows(query_weight.astype(half_type))
    keyval_full = gather_rows(keyval_weight.astype(half_type))
    output_full = gather_rows(output_weight.astype(half_type).T)
    gate_slice = prepare_slice(gate_weight.astype(half_type))
    up_slice = prepare_slice(up_weight.astype(half_type))
    down_slice = prepare_slice(down_weight.astype(half_type).T)
    dy_all = gather_tokens(cot_half.astype(half_type))

    normed_one, inv_one, low_one = rms_forward(hidden, scale_one)
    query = dot(low_one, query_full, ((1,), (0,))).reshape(block, heads_here, HD)
    keyval = dot(low_one, keyval_full, ((1,), (0,)))
    cosine, sine = rope_tables(positions[0])
    query_low = (rotate(query, cosine[:, None, :], sine[:, None, :]) * HD ** (-0.5)).astype(
        half_type
    )
    key_low = rotate(keyval[:, :HD], cosine, sine).astype(half_type)
    keyval_low = jnp.concatenate([key_low, keyval[:, HD:].astype(half_type)], axis=-1)
    keyval_all = lax.all_gather(keyval_low, "context", axis=0, tiled=True)
    keys_all = keyval_all[:, :HD]
    values_all = keyval_all[:, HD:]
    rows_index = context_index * block + jnp.arange(block, dtype=jnp.int32)
    cols_index = jnp.arange(keys_all.shape[0], dtype=jnp.int32)
    allowed = (rows_index[:, None] >= cols_index[None, :]) & (
        segment_ids[0][:, None] == seg_all[0][None, :]
    )
    scores = jnp.einsum("bhd,jd->hbj", query_low, keys_all, preferred_element_type=single)
    masked = jnp.where(allowed, scores, masked_value)
    top = jnp.max(masked, axis=-1, keepdims=True)
    total = jnp.sum(jnp.where(allowed, jnp.exp(masked - top), 0.0), axis=-1, keepdims=True)
    lse = top + jnp.log(total)
    prob = jnp.where(allowed, jnp.exp(masked - lse), 0.0)
    prob_low = prob.astype(half_type)
    att_low = jnp.einsum(
        "hbj,jd->bhd", prob_low, values_all, preferred_element_type=single
    ).astype(half_type)
    att_flat = att_low.reshape(block, heads_width)
    attn_part = dot(att_flat, output_full, ((1,), (1,)))
    attn_half = lax.psum_scatter(
        attn_part.astype(half_type), "tensor", scatter_dimension=0, tiled=True
    )
    mid_half = hidden_half + attn_half.astype(single)

    normed_two, inv_two, low_two = rms_forward(mid_half, scale_two)
    low_all = gather_tokens(low_two)
    gate = dot(low_all, gate_slice, ((1,), (0,)))
    upper = dot(low_all, up_slice, ((1,), (0,)))
    dhid = dot(dy_all, down_slice, ((1,), (0,)))
    gelu_gate, gelu_back = jax.vjp(gelu_tanh, gate)
    hid_low = (gelu_gate * upper).astype(half_type)
    dgate_low = gelu_back(dhid * upper)[0].astype(half_type)
    dup_low = (dhid * gelu_gate).astype(half_type)
    dnorm_two = scatter_tokens(
        dot(dgate_low, gate_slice, ((1,), (1,))) + dot(dup_low, up_slice, ((1,), (1,)))
    )
    mlp_half = scatter_tokens(dot(hid_low, down_slice, ((1,), (1,))))
    grad_wd = return_slice(dot(dy_all, hid_low, ((0,), (0,)))).T
    grad_wg = return_slice(dot(low_all, dgate_low, ((0,), (0,))))
    grad_wu = return_slice(dot(low_all, dup_low, ((0,), (0,))))
    dmid_norm, terms_two = rms_backward(dnorm_two, normed_two, inv_two, scale_two)
    dmid_half = cot_half + dmid_norm

    dmid_low = lax.all_gather(dmid_half.astype(half_type), "tensor", axis=0, tiled=True)
    grad_out_full = dot(dmid_low, att_flat, ((0,), (0,)))
    datt_low = (
        dot(dmid_low, output_full, ((1,), (0,))).astype(half_type).reshape(block, heads_here, HD)
    )
    delta = jnp.einsum("bhd,bhd->hb", datt_low, att_low, preferred_element_type=single)
    dprob = jnp.einsum("bhd,jd->hbj", datt_low, values_all, preferred_element_type=single)
    dscore_low = (prob * (dprob - delta[..., None])).astype(half_type)
    dquery = jnp.einsum("hbj,jd->bhd", dscore_low, keys_all, preferred_element_type=single)
    dkey_part = jnp.einsum("hbj,bhd->jd", dscore_low, query_low, preferred_element_type=single)
    dvalue_part = jnp.einsum("hbj,bhd->jd", prob_low, datt_low, preferred_element_type=single)
    dkeyval_own = lax.psum_scatter(
        jnp.concatenate([dkey_part, dvalue_part], axis=-1).astype(half_type),
        "context",
        scatter_dimension=0,
        tiled=True,
    )
    dkeyval_sum = lax.psum(dkeyval_own.astype(single), "tensor")
    dquery_low = (
        (unrotate(dquery, cosine[:, None, :], sine[:, None, :]) * HD ** (-0.5))
        .astype(half_type)
        .reshape(block, heads_width)
    )
    dnorm_query = dot(dquery_low, query_full, ((1,), (1,)))
    dnorm_query = lax.psum_scatter(
        dnorm_query.astype(half_type), "tensor", scatter_dimension=0, tiled=True
    ).astype(single)
    dkeyval_low = jnp.concatenate(
        [unrotate(dkeyval_sum[:, :HD], cosine, sine), dkeyval_sum[:, HD:]], axis=-1
    ).astype(half_type)
    dkeyval_half = lax.dynamic_slice_in_dim(dkeyval_low, x * half_rows, half_rows, 0)
    dnorm_one = dnorm_query + dot(dkeyval_half, keyval_full, ((1,), (1,)))
    normed_half = lax.dynamic_slice_in_dim(normed_one, x * half_rows, half_rows, 0)
    inv_half = lax.dynamic_slice_in_dim(inv_one, x * half_rows, half_rows, 0)
    dinput_norm, terms_one = rms_backward(dnorm_one, normed_half, inv_half, scale_one)
    grad_query_full = dot(low_one, dquery_low, ((0,), (0,)))
    grad_keyval_full = dot(low_one, dkeyval_low, ((0,), (0,)))
    grad_wq = scatter_rows(grad_query_full)
    grad_wkv = scatter_rows(grad_keyval_full)
    grad_wo = scatter_rows(grad_out_full).T
    terms = jnp.stack([jnp.sum(terms_one, axis=0), jnp.sum(terms_two, axis=0)])
    terms = lax.psum_scatter(terms, ("fsdp", "context"), scatter_dimension=1, tiled=True)
    terms = lax.psum(terms, "tensor")
    grad_s1, grad_s2 = terms[0], terms[1]
    outs = jnp.stack([mid_half + mlp_half, dmid_half + dinput_norm])
    outs = lax.all_gather(outs, "tensor", axis=1, tiled=True)

    masters = (
        attn_scale,
        query_weight,
        keyval_weight,
        output_weight,
        mlp_scale,
        gate_weight,
        up_weight,
        down_weight,
    )
    grads = (grad_s1, grad_wq, grad_wkv, grad_wo, grad_s2, grad_wg, grad_wu, grad_wd)
    firsts = (
        first_attn_scale,
        first_query_weight,
        first_keyval_weight,
        first_output_weight,
        first_mlp_scale,
        first_gate_weight,
        first_up_weight,
        first_down_weight,
    )
    seconds = (
        second_attn_scale,
        second_query_weight,
        second_keyval_weight,
        second_output_weight,
        second_mlp_scale,
        second_gate_weight,
        second_up_weight,
        second_down_weight,
    )
    results = [
        adamw(weight, grad, first, second)
        for weight, grad, first, second in zip(masters, grads, firsts, seconds)
    ]
    return (
        outs[0][None],
        outs[1][None],
        *grads,
        *(entry[0] for entry in results),
        *(entry[1] for entry in results),
        *(entry[2] for entry in results),
    )


def solution(mesh):
    both = ("fsdp", "context")
    tokens = P("fsdp", "context", None)
    weights = (
        P(both),
        P(both, "tensor"),
        P(both, None),
        P("tensor", both),
        P(both),
        P(both, "tensor"),
        P(both, "tensor"),
        P("tensor", both),
    )
    return jax.shard_map(
        on_device,
        mesh=mesh,
        in_specs=(tokens, tokens, P("fsdp", "context"), P("fsdp", "context"), *(weights * 3)),
        out_specs=(tokens, tokens, *(weights * 4)),
        check_vma=False,
    )
```

profile of v0, /device:TPU:8, one launch (start us, length us, event | category | flops | bytes accessed | tf_op | source)
XLA Modules:
  0.0 1193.6 jit_solution(1834390715932010794)
XLA Ops:
  13.0 29.1 %all-gather = bf16[16,160,2]{1,2,0:T(2,128)(2,1)S(1)} all-gather(bf16[1,160,2]{1,2,0:T(2,128)(2,1)S(1)} %maximum_bitcast_fusion), channel_id=1, replica_groups=mesh['fsdp'=4,'context'=4,'tensor'=2] {'fsdp','context'}, dimensions={0}, use_global_device_ids=true | all-gather | bytes 10880 | tf_op jit(solution)/shard_map/all_gather | solution.py:79
  42.2 11.6 all_gather.42
  58.5 17.9 %all_gather.41 = bf16[512,512]{1,0:T(8,128)(2,1)S(1)} all-gather(bf16[128,512]{1,0:T(8,128)(2,1)S(1)} %pad_maximum_fusion.2), channel_id=1, replica_groups=mesh['fsdp'=4,'context'=4,'tensor'=2] {'context'}, dimensions={0}, use_global_device_ids=true | all-gather | bytes 655360 | tf_op jit(solution)/shard_map/all_gather | solution.py:184
  76.4 46.9 %all-gather.13.cloned.1.call-done = bf16[2560,1280]{1,0:T(8,128)(2,1)} async-done(((bf16[160,1280]{1,0:T(8,128)(2,1)}), bf16[2560,1280]{1,0:T(8,128)(2,1)}) %all-gather.13.cloned.1.call-update) | async-done | bytes 6553616 | tf_op jit(solution)/shard_map/all_gather | solution.py:85
  123.3 9.4 copy.192
  141.5 46.3 %all-gather.15.cloned.1.call-done = bf16[2560,1280]{1,0:T(8,128)(2,1)} async-done(((bf16[160,1280]{1,0:T(8,128)(2,1)}), bf16[2560,1280]{1,0:T(8,128)(2,1)}) %all-gather.15.cloned.1.call-update) | async-done | bytes 6553616 | tf_op jit(solution)/shard_map/all_gather | solution.py:85
  204.8 58.5 %all_to_all.30 = bf16[4,160,960]{2,1,0:T(8,128)(2,1)} all-to-all(bf16[4,160,960]{2,1,0:T(8,128)(2,1)S(1)} %copy.197), channel_id=1, replica_groups=mesh['fsdp'=4,'context'=4,'tensor'=2] {'context'}, dimensions={0} | all-to-all | bytes 2457600 | tf_op jit(solution)/shard_map/all_to_all | solution.py:92
  272.3 33.8 %all_to_all.31 = bf16[4,160,960]{2,1,0:T(8,128)(2,1)} all-to-all(bf16[4,160,960]{2,1,0:T(8,128)(2,1)S(1)} %copy.195), channel_id=1, replica_groups=mesh['fsdp'=4,'context'=4,'tensor'=2] {'context'}, dimensions={0} | all-to-all | bytes 2457600 | tf_op jit(solution)/shard_map/all_to_all | solution.py:92
  317.4 33.5 %all_to_all.32 = bf16[4,160,960]{2,1,0:T(8,128)(2,1)} all-to-all(bf16[4,160,960]{2,1,0:T(8,128)(2,1)S(1)} %copy.196), channel_id=1, replica_groups=mesh['fsdp'=4,'context'=4,'tensor'=2] {'context'}, dimensions={0} | all-to-all | bytes 2457600 | tf_op jit(solution)/shard_map/all_to_all | solution.py:92
  358.8 48.5 %all-gather.17.cloned.1.call-done = bf16[512,2560]{1,0:T(8,128)(2,1)} async-done(((bf16[64,2560]{1,0:T(8,128)(2,1)}), bf16[512,2560]{1,0:T(8,128)(2,1)}) %all-gather.17.cloned.1.call-update) | async-done | bytes 2621456 | tf_op jit(solution)/shard_map/all_gather | solution.py:98
  414.6 33.2 %all-gather.21.cloned.1.call-done = bf16[16,160,960]{2,1,0:T(8,128)(2,1)} async-done(((bf16[4,160,960]{2,1,0:T(8,128)(2,1)}), bf16[16,160,960]{2,1,0:T(8,128)(2,1)}) %all-gather.21.cloned.1.call-update) | async-done | bytes 4915216 | tf_op jit(solution)/shard_map/all_gather | solution.py:93
  447.7 9.6 multiply_convert_fusion.1
  472.3 63.3 %reduce-scatter.19.cloned.1.call-done = bf16[64,2560]{1,0:T(8,128)(2,1)} async-done(((bf16[512,2560]{1,0:T(8,128)(2,1)}), bf16[64,2560]{1,0:T(8,128)(2,1)}) %reduce-scatter.19.cloned.1.call-update) | async-done | bytes 327696 | tf_op jit(solution)/shard_map/reduce_scatter | solution.py:102
  536.9 72.4 %reduce-scatter.17.cloned.1.call-done = bf16[64,2560]{1,0:T(8,128)(2,1)} async-done(((bf16[512,2560]{1,0:T(8,128)(2,1)}), bf16[64,2560]{1,0:T(8,128)(2,1)}) %reduce-scatter.17.cloned.1.call-update) | async-done | bytes 327696 | tf_op jit(solution)/shard_map/reduce_scatter | solution.py:102
  611.7 8.8 all_gather.50
  665.8 7.9 copy.211
  674.3 12.5 %all-reduce.1 = f32[128,512]{1,0:T(8,128)S(1)} all-reduce(bf16[128,512]{1,0:T(8,128)(2,1)} %reduce-scatter.23.cloned.1.call-done), channel_id=1, replica_groups=mesh['fsdp'=4,'context'=4,'tensor'=2] {'tensor'}, use_global_device_ids=true, to_apply=%region_10.11 | all-reduce | flops 65536 | bytes 393216 | tf_op jit(solution)/shard_map/psum | solution.py:245
  736.1 43.7 %reduce-scatter.33.cloned.1.call-done = bf16[4,160,960]{2,1,0:T(8,128)(2,1)} async-done(((bf16[16,160,960]{2,1,0:T(8,128)(2,1)}), bf16[4,160,960]{2,1,0:T(8,128)(2,1)}) %reduce-scatter.33.cloned.1.call-update) | async-done | bytes 1228816 | tf_op jit(solution)/shard_map/reduce_scatter | solution.py:119
  785.0 57.4 %reduce-scatter.37.cloned.1.call-done = f32[160,2]{1,0:T(8,128)} async-done(((f32[2560,2]{1,0:T(8,128)}), f32[160,2]{1,0:T(8,128)}) %reduce-scatter.37.cloned.1.call-update) | async-done | bytes 1296
  848.3 47.1 %reduce-scatter.35.cloned.1.call-done = bf16[4,160,960]{2,1,0:T(8,128)(2,1)} async-done(((bf16[16,160,960]{2,1,0:T(8,128)(2,1)}), bf16[4,160,960]{2,1,0:T(8,128)(2,1)}) %reduce-scatter.35.cloned.1.call-update) | async-done | bytes 1228816 | tf_op jit(solution)/shard_map/reduce_scatter | solution.py:119
  901.6 34.9 %all-gather.27.cloned.1.call-done = f32[2,128,2560]{2,1,0:T(8,128)} async-done(((f32[2,64,2560]{2,1,0:T(8,128)}), f32[2,128,2560]{2,1,0:T(8,128)}) %all-gather.27.cloned.1.call-update) | async-done | bytes 2621456 | tf_op jit(solution)/shard_map/all_gather | solution.py:273
  939.9 64.2 %reduce-scatter.27.cloned.1.call-done = bf16[160,512]{1,0:T(8,128)(2,1)} async-done(((bf16[2560,512]{1,0:T(8,128)(2,1)}), bf16[160,512]{1,0:T(8,128)(2,1)}) %reduce-scatter.27.cloned.1.call-update) | async-done | bytes 163856 | tf_op jit(solution)/shard_map/reduce_scatter | solution.py:108
  1052.5 41.3 %reduce-scatter.25.cloned.1.call-done = bf16[160,1280]{1,0:T(8,128)(2,1)} async-done(((bf16[2560,1280]{1,0:T(8,128)(2,1)}), bf16[160,1280]{1,0:T(8,128)(2,1)}) %reduce-scatter.25.cloned.1.call-update) | async-done | bytes 409616 | tf_op jit(solution)/shard_map/reduce_scatter | solution.py:108
  1097.1 86.2 %reduce-scatter.29.cloned.1.call-done = bf16[160,1280]{1,0:T(8,128)(2,1)} async-done(((bf16[2560,1280]{1,0:T(8,128)(2,1)}), bf16[160,1280]{1,0:T(8,128)(2,1)}) %reduce-scatter.29.cloned.1.call-update) | async-done | bytes 409616 | tf_op jit(solution)/shard_map/reduce_scatter | solution.py:108
  (306 shorter events, 258.9 us)
Async XLA Ops:
  8.1 47.7 %all-gather.11.cloned.1.call-start = ((), (), s32[]{:S(2)}) async-start(), calls=%async_computation.18 | async-start | bytes 2785280 | tf_op jit(solution)/shard_map/all_gather | solution.py:85
  10.0 113.3 %all-gather.13.cloned.1.call-start = ((), (), s32[]{:S(2)}) async-start(), calls=%async_computation.19 | async-start | bytes 6963200 | tf_op jit(solution)/shard_map/all_gather | solution.py:85
  12.0 175.8 %all-gather.15.cloned.1.call-start = ((), (), s32[]{:S(2)}) async-start(), calls=%async_computation.20 | async-start | bytes 6963200 | tf_op jit(solution)/shard_map/all_gather | solution.py:85
  12.9 293.3 %reduce-scatter.15.cloned.1.call-start = ((), (), s32[]{:S(2)}) async-start(), calls=%async_computation.21 | async-start | bytes 983040 | tf_op jit(solution)/shard_map/reduce_scatter | solution.py:204
  193.8 157.7 %all-gather.25.cloned.1.call-start = ((), (), s32[]{:S(2)}) async-start(), calls=%async_computation.27 | async-start | bytes 2949120 | tf_op jit(solution)/shard_map/all_gather | solution.py:98
  195.7 155.8 %all-gather.23.cloned.1.call-start = ((), (), s32[]{:S(2)}) async-start(), calls=%async_computation.25 | async-start | bytes 6553600 | tf_op jit(solution)/shard_map/all_gather | solution.py:93
  263.3 95.4 %all-gather.19.cloned.1.call-start = ((), (), s32[]{:S(2)}) async-start(), calls=%async_computation.23 | async-start | bytes 6553600 | tf_op jit(solution)/shard_map/all_gather | solution.py:93
  306.1 101.1 %all-gather.17.cloned.1.call-start = ((), (), s32[]{:S(2)}) async-start(), calls=%async_computation.22 | async-start | bytes 2949120 | tf_op jit(solution)/shard_map/all_gather | solution.py:98
  308.3 139.5 %all-gather.21.cloned.1.call-start = ((), (), s32[]{:S(2)}) async-start(), calls=%async_computation.24 | async-start | bytes 6553600 | tf_op jit(solution)/shard_map/all_gather | solution.py:93
  350.9 184.7 %reduce-scatter.19.cloned.1.call-start = ((), (), s32[]{:S(2)}) async-start(), calls=%async_computation.28 | async-start | bytes 2949120 | tf_op jit(solution)/shard_map/reduce_scatter | solution.py:102
  465.0 144.4 %reduce-scatter.17.cloned.1.call-start = ((), (), s32[]{:S(2)}) async-start(), calls=%async_computation.26 | async-start | bytes 2949120 | tf_op jit(solution)/shard_map/reduce_scatter | solution.py:102
  472.3 202.1 %reduce-scatter.23.cloned.1.call-start = ((), (), s32[]{:S(2)}) async-start(), calls=%async_computation.30 | async-start | bytes 655360 | tf_op jit(solution)/shard_map/reduce_scatter | solution.py:239
  633.1 55.5 %reduce-scatter.21.cloned.1.call-start = ((), (), s32[]{:S(2)}) async-start(), calls=%async_computation.29 | async-start | bytes 983040 | tf_op jit(solution)/shard_map/reduce_scatter | solution.py:252
  643.7 82.2 %reduce-scatter.31.cloned.1.call-start = ((), (), s32[]{:S(2)}) async-start(), calls=%async_computation.35 | async-start | bytes 6553600 | tf_op jit(solution)/shard_map/reduce_scatter | solution.py:119
  658.5 121.3 %reduce-scatter.33.cloned.1.call-start = ((), (), s32[]{:S(2)}) async-start(), calls=%async_computation.36 | async-start | bytes 6553600 | tf_op jit(solution)/shard_map/reduce_scatter | solution.py:119
  673.7 168.7 %reduce-scatter.37.cloned.1.call-start = ((), (), s32[]{:S(2)}) async-start(), calls=%async_computation.38 | async-start | bytes 1392640
  693.9 201.5 %reduce-scatter.35.cloned.1.call-start = ((), (), s32[]{:S(2)}) async-start(), calls=%async_computation.37 | async-start | bytes 6553600 | tf_op jit(solution)/shard_map/reduce_scatter | solution.py:119
  709.5 227.0 %all-gather.27.cloned.1.call-start = ((), (), s32[]{:S(2)}) async-start(), calls=%async_computation.31 | async-start | bytes 3932160 | tf_op jit(solution)/shard_map/all_gather | solution.py:273
  713.2 290.8 %reduce-scatter.27.cloned.1.call-start = ((), (), s32[]{:S(2)}) async-start(), calls=%async_computation.33 | async-start | bytes 2785280 | tf_op jit(solution)/shard_map/reduce_scatter | solution.py:108
  715.8 378.0 %reduce-scatter.25.cloned.1.call-start = ((), (), s32[]{:S(2)}) async-start(), calls=%async_computation.32 | async-start | bytes 6963200 | tf_op jit(solution)/shard_map/reduce_scatter | solution.py:108
  725.9 53.9 %all-to-all-start.3 = ((bf16[4,160,960]{2,1,0:T(8,128)(2,1)}), bf16[4,160,960]{2,1,0:T(8,128)(2,1)S(1)}, u32[]{:S(2)}, u32[]{:S(2)}) async-start(bf16[4,160,960]{2,1,0:T(8,128)(2,1)} %reduce-scatter.31.cloned.1.call-done), calls=%async_computation.12 | async-start | bytes 2621440 | tf_op jit(solution)/shard_map/all_to_all | solution.py:120
  731.1 452.3 %reduce-scatter.29.cloned.1.call-start = ((), (), s32[]{:S(2)}) async-start(), calls=%async_computation.34 | async-start | bytes 6963200 | tf_op jit(solution)/shard_map/reduce_scatter | solution.py:108
  779.8 115.5 %all-to-all-start.4 = ((bf16[4,160,960]{2,1,0:T(8,128)(2,1)}), bf16[4,160,960]{2,1,0:T(8,128)(2,1)}, u32[]{:S(2)}, u32[]{:S(2)}) async-start(bf16[4,160,960]{2,1,0:T(8,128)(2,1)} %reduce-scatter.33.cloned.1.call-done), calls=%async_computation.14 | async-start | bytes 2621440 | tf_op jit(solution)/shard_map/all_to_all | solution.py:120
  895.4 127.9 %all-to-all-start.5 = ((bf16[4,160,960]{2,1,0:T(8,128)(2,1)}), bf16[4,160,960]{2,1,0:T(8,128)(2,1)}, u32[]{:S(2)}, u32[]{:S(2)}) async-start(bf16[4,160,960]{2,1,0:T(8,128)(2,1)} %reduce-scatter.35.cloned.1.call-done), calls=%async_computation.16 | async-start | bytes 2621440 | tf_op jit(solution)/shard_map/all_to_all | solution.py:120
  (74 other events, 2803.8 us)
Sparse Core Ops, SparseCore 0:
  11.8 44.0 all-gather.10
  58.7 64.5 all-gather.12
  126.2 61.5 all-gather.14
  193.9 15.0 reduce-scatter.14
  633.2 18.4 reduce-scatter.22
  654.4 17.5 reduce-scatter.20
  674.5 51.3 reduce-scatter.30
  728.5 51.3 reduce-scatter.32
  784.0 58.3 reduce-scatter.36
  844.8 50.5 reduce-scatter.34
  897.5 38.9 all-gather.26
  940.1 63.9 reduce-scatter.26
  1008.0 85.7 reduce-scatter.24
  1097.6 85.7 reduce-scatter.28
Sparse Core Ops, SparseCore 1:
  197.0 70.1 all-gather.24
  268.6 39.5 all-gather.22
  309.7 40.2 all-gather.18
  352.8 54.4 all-gather.16
  408.8 38.8 all-gather.20
  465.1 70.5 reduce-scatter.18
  539.0 70.3 reduce-scatter.16
where the time goes:
time: 1210 us; the launch traced here: 1190 us
  waiting for transfers between devices  692 us (57%)
  blocking collectives  211 us (17%)
  matrix products  107 us (9%)
  local copies, waits for them, and re-layouts  93.5 us (8%)
  other arithmetic  56.7 us (5%)
  starting transfers between devices  17.4 us (1%)
  between operations  16.8 us (1%)
    reduce_scatter x3, waiting for transfers between devices, scatter_rows(): lax.psum_scatter(part.astype(half_type), ('fsdp', 'context'), scatter_dim...  192 us
    reduce_scatter x2, waiting for transfers between devices, scatter_tokens(): lax.psum_scatter(part.astype(half_type), ('context', 'tensor'), scatter_d...  136 us
    all_to_all x3, blocking collectives, prepare_slice(): lax.all_to_all(parts, 'context', split_axis=0, concat_axis=0, tiled=True)  126 us
    dot_general x18, matrix products, dot(): lax.dot_general(a, b, (dims, ((), ())), preferred_element_type=single)  101 us
    reduce_scatter x3, waiting for transfers between devices, return_slice(): parts = lax.psum_scatter(parts, 'fsdp', scatter_dimension=0, tiled=True)  96.1 us
    all_gather x3, waiting for transfers between devices, gather_rows(): return lax.all_gather(block, ('fsdp', 'context'), axis=0, tiled=True)  94 us
    unnamed x22, waiting for transfers between devices  57.8 us
    all_gather x2, waiting for transfers between devices, gather_tokens(): return lax.all_gather(block, ('context', 'tensor'), axis=0, tiled=True)  48.5 us
  transfers between devices with their start and end apart: 24, of which 15 were waited for; matrix products, arithmetic and copies ran while one was open for 17% of the time, Pallas kernels for 0%

commit v1 on v0

v1 whole, which is shorter than its diff:
```python
import functools

import jax
import jax.numpy as jnp
from jax import lax
from jax.experimental import pallas as pl
from jax.experimental.pallas import tpu as pltpu
from jax.sharding import PartitionSpec as P

HD = 256


norm_eps = 1e-06
beta_one = 0.9
beta_two = 0.999
adam_eps = 1e-08
learn_rate = 0.03
decay_rate = 0.1
adam_step = 4.0
rope_base = 10000.0
masked_value = -1e30

single = jnp.float32
half_type = jnp.bfloat16


def gelu_tanh(values):
    return jax.nn.gelu(values, approximate=True)


def rope_tables(positions):
    half = HD // 2
    freq = rope_base ** (-2.0 * jnp.arange(half).astype(jnp.float32) / HD)
    angle = positions.astype(jnp.float32)[..., None] * freq
    return (jnp.cos(angle), jnp.sin(angle))


def rotate(values, cosine, sine):
    half = values.shape[-1] // 2
    first = values[..., :half]
    second = values[..., half:]
    return jnp.concatenate(
        [first * cosine - second * sine, second * cosine + first * sine], axis=-1
    )


def unrotate(values, cosine, sine):
    half = values.shape[-1] // 2
    first = values[..., :half]
    second = values[..., half:]
    return jnp.concatenate(
        [first * cosine + second * sine, second * cosine - first * sine], axis=-1
    )


def rms_forward(values, scale):
    inverse = lax.rsqrt(jnp.mean(values * values, axis=-1, keepdims=True) + norm_eps)
    normed = values * inverse
    return (normed, inverse, (normed * (1.0 + scale)).astype(jnp.bfloat16))


def rms_backward(dnorm, normed, inverse, scale):
    dnormed = dnorm * (1.0 + scale)
    dvalues = inverse * (dnormed - normed * jnp.mean(dnormed * normed, axis=-1, keepdims=True))
    return (dvalues, dnorm * normed)


def adamw(weight, grad, first, second):
    first_new = beta_one * first + (1.0 - beta_one) * grad
    second_new = beta_two * second + (1.0 - beta_two) * grad * grad
    fix_one = 1.0 - beta_one**adam_step
    fix_two = 1.0 - beta_two**adam_step
    update = first_new / fix_one / (jnp.sqrt(second_new / fix_two) + adam_eps)
    return (weight - learn_rate * (update + decay_rate * weight), first_new, second_new)


def dot(a, b, dims):
    return lax.dot_general(a, b, (dims, ((), ())), preferred_element_type=single)


MESH = pl.DeviceIdType.MESH
ANY = pl.BlockSpec(memory_space=pl.ANY)
VMEM = pl.BlockSpec(memory_space=pltpu.VMEM)


def greet(peers):
    barrier = pltpu.get_barrier_semaphore()
    for peer in peers:
        pl.semaphore_signal(barrier, inc=1, device_id=peer, device_id_type=MESH)
    pl.semaphore_wait(barrier, len(peers))


def remote(src, dst, send, recv, peer):
    return pltpu.make_async_remote_copy(
        src_ref=src, dst_ref=dst, send_sem=send, recv_sem=recv, device_id=peer, device_id_type=MESH
    )


def arrived(dst, recv, peer):
    remote(dst, dst, recv, recv, peer).wait_recv()


def fsdp_place(fs):
    f = lax.axis_index("fsdp")
    core = lax.rem(f, 2)
    y = lax.div(f, 2)
    twin = {"fsdp": f + 1 - 2 * core}
    across = [{"fsdp": lax.rem(y + d, fs // 2) * 2 + core} for d in range(1, fs // 2)]
    return f, y, core, twin, across


class Sends:
    def __init__(self, send):
        self.send, self.made = send, []

    def push(self, src, dst, recv, peer, *conditions):
        copy = remote(src, dst, self.send.at[len(self.made)], recv, peer)
        self.made.append((copy, conditions))
        under(conditions, copy.start)

    def drain(self):
        for copy, conditions in self.made:
            under(conditions, copy.wait_send)


def under(conditions, action):
    if not conditions:
        action()
        return
    holds = conditions[0]
    for more in conditions[1:]:
        holds = jnp.logical_and(holds, more)
    pl.when(holds)(action)


def line_steps(z, ctx):
    for s in range(1, ctx):
        yield z - s, z >= s, z + 1, z + 1 < ctx
        yield z + s, z + s < ctx, z - 1, z >= 1


def tokens_kernel(ctx, ten, src, out, local, send, recv):
    z, x = lax.axis_index("context"), lax.axis_index("tensor")
    around = [lax.rem(z + d, ctx) for d in range(ctx)]
    across = [{"tensor": lax.rem(x + d, ten)} for d in range(1, ten)]
    greet([{"context": k} for k in around[1:]] + across)
    sends = []

    def push(ref, source, peer):
        copy = remote(ref, out.at[source, x], send.at[len(sends)], recv.at[source, x], peer)
        copy.start()
        sends.append(copy)

    for d in range(1, ctx):
        push(src, z, {"context": around[d]})
    for peer in across:
        push(src, z, peer)
    keep = pltpu.make_async_copy(src, out.at[z, x], local)
    keep.start()
    back = [lax.rem(z + ctx - d, ctx) for d in range(ctx)]
    for d in range(1, ctx):
        arrived(out.at[back[d], x], recv.at[back[d], x], {"context": back[d]})
        for peer in across:
            push(out.at[back[d], x], back[d], peer)
    for d in range(ctx):
        for peer in across:
            other = peer["tensor"]
            arrived(out.at[back[d], other], recv.at[back[d], other], peer)
    keep.wait()
    for copy in sends:
        copy.wait_send()


def tokens_to_all(block, ctx, ten, ident):
    sends = (ctx - 1) + ctx * (ten - 1)
    out = pl.pallas_call(
        functools.partial(tokens_kernel, ctx, ten),
        out_shape=jax.ShapeDtypeStruct((ctx, ten, *block.shape), block.dtype),
        in_specs=[VMEM],
        out_specs=VMEM,
        scratch_shapes=[
            pltpu.SemaphoreType.DMA(()),
            pltpu.SemaphoreType.DMA((sends,)),
            pltpu.SemaphoreType.DMA((ctx, ten)),
        ],
        compiler_params=pltpu.CompilerParams(collective_id=ident, has_side_effects=True),
        name=f"tokens_{ident}",
    )(block)
    return out.reshape(-1, block.shape[-1])


def sum_tokens_kernel(ctx, ten, src, out, first, mine, second, send, recv_x, recv_z):
    z, x = lax.axis_index("context"), lax.axis_index("tensor")
    around = [lax.rem(z + d, ctx) for d in range(ctx)]
    across = [lax.rem(x + d, ten) for d in range(1, ten)]
    greet([{"context": k} for k in around[1:]] + [{"tensor": k} for k in across])
    sends = []
    order = around[1:] + around[:1]
    for owner in order:
        for k, other in enumerate(across):
            copy = remote(
                src.at[owner, other],
                first.at[k, owner],
                send.at[len(sends)],
                recv_x.at[k, owner],
                {"tensor": other},
            )
            copy.start()
            sends.append(copy)
    for d, owner in enumerate(order):
        total = src[owner, x].astype(single)
        for k, other in enumerate(across):
            arrived(first.at[k, owner], recv_x.at[k, owner], {"tensor": other})
            total = total + first[k, owner].astype(single)
        if d < ctx - 1:
            mine[d] = total.astype(half_type)
            copy = remote(
                mine.at[d],
                second.at[d],
                send.at[len(sends)],
                recv_z.at[d],
                {"context": owner},
            )
            copy.start()
            sends.append(copy)
        else:
            for e in range(ctx - 1):
                arrived(second.at[e], recv_z.at[e], {"context": around[1]})
                total = total + second[e].astype(single)
            out[...] = total
    for copy in sends:
        copy.wait_send()


def sum_tokens(part, ctx, ten, ident):
    rows, columns = part.shape[0] // (ctx * ten), part.shape[1]
    sends = ctx * (ten - 1) + ctx - 1
    return pl.pallas_call(
        functools.partial(sum_tokens_kernel, ctx, ten),
        out_shape=jax.ShapeDtypeStruct((rows, columns), single),
        in_specs=[VMEM],
        out_specs=VMEM,
        scratch_shapes=[
            pltpu.VMEM((ten - 1, ctx, rows, columns), half_type),
            pltpu.VMEM((ctx - 1, rows, columns), half_type),
            pltpu.VMEM((ctx - 1, rows, columns), half_type),
            pltpu.SemaphoreType.DMA((sends,)),
            pltpu.SemaphoreType.DMA((ten - 1, ctx)),
            pltpu.SemaphoreType.DMA((ctx - 1,)),
        ],
        compiler_params=pltpu.CompilerParams(collective_id=ident, has_side_effects=True),
        name=f"sum_tokens_{ident}",
    )(part.reshape(ctx, ten, rows, columns))


def swap_kernel(ten, src, out, local, send, recv):
    x = lax.axis_index("tensor")
    beside = [lax.rem(x + d, ten) for d in range(1, ten)]
    greet([{"tensor": k} for k in beside])
    out_sends = Sends(send)
    for other in beside:
        out_sends.push(src.at[other], out.at[x], recv.at[x], {"tensor": other})
    keep = pltpu.make_async_copy(src.at[x], out.at[x], local)
    keep.start()
    for other in beside:
        arrived(out.at[other], recv.at[other], {"tensor": other})
    keep.wait()
    out_sends.drain()


def swap(blocks, ten, ident):
    return pl.pallas_call(
        functools.partial(swap_kernel, ten),
        out_shape=jax.ShapeDtypeStruct(blocks.shape, blocks.dtype),
        in_specs=[VMEM],
        out_specs=VMEM,
        scratch_shapes=[
            pltpu.SemaphoreType.DMA(()),
            pltpu.SemaphoreType.DMA((ten - 1,)),
            pltpu.SemaphoreType.DMA((ten,)),
        ],
        compiler_params=pltpu.CompilerParams(collective_id=ident, has_side_effects=True),
        name=f"swap_{ident}",
    )(blocks)


VMEM_ALL = 67043328


def cast(v):
    return v.astype(half_type)


def spread_kernel(fs, ctx, ten, count, split, *refs):
    srcs, outs = refs[: count + 1], refs[count + 1 : 2 * count + 2]
    local, send, recv, recv_t = refs[2 * count + 2 :]
    f, y, core, twin, across = fsdp_place(fs)
    z, x = lax.axis_index("context"), lax.axis_index("tensor")
    beside = [{"tensor": lax.rem(x + d, ten)} for d in range(1, ten)]
    around = [lax.rem(z + d, ctx) for d in range(ctx)]
    back = [lax.rem(z + ctx - d, ctx) for d in range(ctx)]
    up, down = {"context": z + 1}, {"context": z - 1}
    greet([{"context": k} for k in around[1:]] + across + [twin] + beside)
    out = Sends(send)
    keeps = []
    order = [count] + list(range(count))

    def where(w, source):
        if w == count:
            return outs[w].at[source, x], recv_t.at[source, x], beside
        return outs[w].at[f, source], recv.at[w, f, source], across + [twin]

    for w in order:
        mine, sem, peers = where(w, z)
        if w < count and split[w]:
            for d in range(1, ctx):
                out.push(srcs[w].at[around[d]], mine, sem, {"context": around[d]})
            src = srcs[w].at[z]
        else:
            src = srcs[w]
            out.push(src, mine, sem, up, z + 1 < ctx)
            out.push(src, mine, sem, down, z >= 1)
        for peer in peers:
            out.push(src, mine, sem, peer)
        keeps.append(pltpu.make_async_copy(src, mine, local.at[w]))
        keeps[-1].start()
    for step, (source, exists, onward, more) in enumerate(line_steps(z, ctx)):
        for w in order:
            if w < count and split[w]:
                if step % 2:
                    continue
                block, sem, peers = where(w, back[step // 2 + 1])
                arrived(block, sem, twin)
                for peer in peers:
                    out.push(block, block, sem, peer)
                continue
            block, sem, peers = where(w, source)
            under((exists,), lambda: arrived(block, sem, twin))
            out.push(block, block, sem, {"context": onward}, exists, more)
            for peer in peers:
                out.push(block, block, sem, peer, exists)
    chain = [(z, ())] + [(source, (exists,)) for source, exists, _, _ in line_steps(z, ctx)]
    ring = [(source, ()) for source in back]
    for w in range(count):
        for source, when in ring if split[w] else chain:
            for peer in across:
                owner = peer["fsdp"]
                block, sem = outs[w].at[owner, source], recv.at[w, owner, source]
                under(when, lambda: arrived(block, sem, twin))
                out.push(block, block, sem, twin, *when)
    for source in back:
        for w in range(count):
            for step in range(fs // 2):
                owner = lax.rem(y + step, fs // 2) * 2 + 1 - core
                arrived(outs[w].at[owner, source], recv.at[w, owner, source], twin)
        for peer in beside:
            arrived(outs[count].at[source, peer["tensor"]], recv_t.at[source, peer["tensor"]], twin)
    for keep in keeps:
        keep.wait()
    out.drain()


def spread(blocks, split, tokens, fs, ctx, ten, ident):
    count = len(blocks)
    chips = fs // 2
    lines = 2 + 2 * (ctx - 1)
    sends = count * (lines + (2 * ctx - 1) * (2 * chips - 1)) + lines + (2 * ctx - 1) * (ten - 1)
    shapes = [b.shape[1:] if s else b.shape for b, s in zip(blocks, split)]
    return pl.pallas_call(
        functools.partial(spread_kernel, fs, ctx, ten, count, split),
        out_shape=[jax.ShapeDtypeStruct((fs, ctx, *s), b.dtype) for s, b in zip(shapes, blocks)]
        + [jax.ShapeDtypeStruct((ctx, ten, *tokens.shape), tokens.dtype)],
        in_specs=[ANY] * (count + 1),
        out_specs=[ANY] * (count + 1),
        scratch_shapes=[
            pltpu.SemaphoreType.DMA((count + 1,)),
            pltpu.SemaphoreType.DMA((sends,)),
            pltpu.SemaphoreType.DMA((count, fs, ctx)),
            pltpu.SemaphoreType.DMA((ctx, ten)),
        ],
        compiler_params=pltpu.CompilerParams(collective_id=ident, has_side_effects=True),
        name=f"spread_{ident}",
    )(*blocks, tokens)


def fill_product(dw, left, right, owner, ctx):
    def one(k, carry):
        dw[owner, k] = cast(
            lax.dot_general(
                left[owner, k], right[...], (((1,), (0,)), ((), ())), preferred_element_type=single
            )
        )
        return carry

    lax.fori_loop(0, ctx, one, 0)


def back_kernel(
    fs, ctx, ten, low_t, dy_t, hid, dgate, dup, dnorm, mlp, dnorm_out, mlp_out, down, gate, up, *refs
):
    dws, nears, fars = refs[0:3], refs[3:6], refs[6:9]
    firsts, mines, seconds = refs[9:11], refs[11:13], refs[13:15]
    local, send, recv_c, recv_y, recv_z, recv_tx, recv_tz = refs[15:]
    f, y, core, twin, across = fsdp_place(fs)
    z, x = lax.axis_index("context"), lax.axis_index("tensor")
    chips = fs // 2
    around = [lax.rem(z + d, ctx) for d in range(ctx)]
    beside = [lax.rem(x + d, ten) for d in range(1, ten)]
    rows_of = [lax.rem(y + d, chips) for d in range(chips)]
    chip_order = rows_of[1:] + rows_of[:1]
    order = around[1:] + around[:1]
    greet([{"context": k} for k in around[1:]] + across + [twin] + [{"tensor": k} for k in beside])
    out = Sends(send)
    outs = (down, gate, up)
    sources = (dnorm, mlp)
    results = (dnorm_out, mlp_out)

    def token_start(t):
        for owner in order:
            for k, other in enumerate(beside):
                out.push(
                    sources[t].at[owner, other],
                    firsts[t].at[k, owner],
                    recv_tx.at[t, k, owner],
                    {"tensor": other},
                )

    def token_pass(t):
        for d, owner in enumerate(order):
            total = sources[t][owner, x].astype(single)
            for k, other in enumerate(beside):
                arrived(firsts[t].at[k, owner], recv_tx.at[t, k, owner], twin)
                total = total + firsts[t][k, owner].astype(single)
            if d < ctx - 1:
                mines[t][d] = cast(total)
                out.push(mines[t].at[d], seconds[t].at[d], recv_tz.at[t, d], {"context": owner})
            else:
                results[t][...] = total

    def token_end(t):
        total = results[t][...]
        for e in range(ctx - 1):
            arrived(seconds[t].at[e], recv_tz.at[t, e], twin)
            total = total + seconds[t][e].astype(single)
        results[t][...] = total

    def products(w):
        left, right = (dy_t, low_t, low_t)[w], (hid, dgate, dup)[w]
        for row in chip_order:
            fill_product(dws[w], left, right, row * 2 + 1 - core, ctx)
            out.push(dws[w].at[row * 2 + 1 - core], nears[w].at[row], recv_c.at[w, row], twin)
        for row in chip_order:
            fill_product(dws[w], left, right, row * 2 + core, ctx)

    def over_chips(w):
        for k, row in enumerate(rows_of[1:]):
            arrived(nears[w].at[row], recv_c.at[w, row], twin)
            for d, owner in enumerate(order):
                mine = dws[w].at[row * 2 + core, owner]
                mine[...] = cast(mine[...].astype(single) + nears[w][row, owner].astype(single))
                out.push(mine, fars[w].at[k, d], recv_y.at[w, k, d], across[k])

    def over_context(w):
        arrived(nears[w].at[y], recv_c.at[w, y], twin)
        for d, owner in enumerate(order):
            mine = dws[w].at[f, owner]
            total = mine[...].astype(single) + nears[w][y, owner].astype(single)
            for k in range(chips - 1):
                arrived(fars[w].at[k, d], recv_y.at[w, k, d], twin)
                total = total + fars[w][k, d].astype(single)
            mine[...] = cast(total)
            if d < ctx - 1:
                out.push(mine, outs[w].at[z], recv_z.at[w, z], {"context": owner})
            else:
                keep = pltpu.make_async_copy(mine, outs[w].at[z], local.at[w])
                keep.start()
                keeps.append(keep)

    keeps = []
    token_start(0)
    products(0)
    token_start(1)
    over_chips(0)
    products(1)
    over_chips(1)
    token_pass(0)
    over_context(0)
    products(2)
    over_chips(2)
    token_pass(1)
    over_context(1)
    over_context(2)
    token_end(0)
    token_end(1)
    for w in range(3):
        for k in around[1:]:
            arrived(outs[w].at[k], recv_z.at[w, k], twin)
    for keep in keeps:
        keep.wait()
    out.drain()


def mlp_back(low_t, dy_t, hid, dgate, dup, dnorm, mlp, fs, ctx, ten, ident):
    rows, columns = low_t.shape[2], hid.shape[1]
    t_rows, width = dnorm.shape[2:]
    chips = fs // 2
    block = (rows, columns)
    sends = 2 * (ctx * (ten - 1) + ctx - 1) + 3 * (chips + (chips - 1) * ctx + ctx - 1)
    dma = pltpu.SemaphoreType.DMA
    return pl.pallas_call(
        functools.partial(back_kernel, fs, ctx, ten),
        out_shape=[jax.ShapeDtypeStruct((t_rows, width), single)] * 2
        + [jax.ShapeDtypeStruct((ctx, *block), half_type)] * 3,
        in_specs=[VMEM] * 7,
        out_specs=[VMEM] * 2 + [ANY] * 3,
        scratch_shapes=[pltpu.VMEM((fs, ctx, *block), half_type)] * 3
        + [pltpu.VMEM((chips, ctx, *block), half_type)] * 3
        + [pltpu.VMEM((chips - 1, ctx, *block), half_type)] * 3
        + [pltpu.VMEM((ten - 1, ctx, t_rows, width), half_type)] * 2
        + [pltpu.VMEM((ctx - 1, t_rows, width), half_type)] * 4
        + [
            dma((3,)),
            dma((sends,)),
            dma((3, chips)),
            dma((3, chips - 1, ctx)),
            dma((3, ctx)),
            dma((2, ten - 1, ctx)),
            dma((2, ctx - 1)),
        ],
        compiler_params=pltpu.CompilerParams(
            collective_id=ident, has_side_effects=True, vmem_limit_bytes=VMEM_ALL
        ),
        name=f"mlp_back_{ident}",
    )(low_t, dy_t, hid, dgate, dup, dnorm, mlp)


def attn_kernel(
    fs, ctx, ten, low_t, dmid_t, d_qkv, att, terms, give, qkv_out, o_out, s_out, kv_out, take_out, *refs
):
    dws, nears, fars = refs[0:3], refs[3:6], refs[6:9]
    ups, downs = refs[9:12], refs[12:15]
    tail, near_s, local, send, recv_c, recv_y, recv_u, recv_d, recv_x = refs[15:]
    dws[2][...] = terms[...]
    f, y, core, twin, across = fsdp_place(fs)
    z, x = lax.axis_index("context"), lax.axis_index("tensor")
    chips = fs // 2
    beside = [lax.rem(x + d, ten) for d in range(1, ten)]
    rows_of = [lax.rem(y + d, chips) for d in range(chips)]
    chip_order = rows_of[1:] + rows_of[:1]
    nxt, prv = lax.rem(z + 1, ctx), lax.rem(z + ctx - 1, ctx)
    greet([{"context": nxt}, {"context": prv}] + across + [twin] + [{"tensor": k} for k in beside])
    out = Sends(send)
    order = []
    for k in range((ctx + 1) // 2):
        order += [ctx - 1 - k] + ([k] if k != ctx - 1 - k else [])
    kinds = (cast, cast, lambda v: v)

    for k, other in enumerate(beside):
        out.push(give, take_out.at[x], recv_x.at[0, x], {"tensor": other})
    keep_give = pltpu.make_async_copy(give, take_out.at[x], local.at[0])
    keep_give.start()

    def start(w):
        for row in chip_order:
            owner = row * 2 + 1 - core
            if w < 2:
                fill_product(dws[w], (low_t, dmid_t)[w], (d_qkv, att)[w], owner, ctx)
            out.push(dws[w].at[owner], nears[w].at[row], recv_c.at[w, row], twin)
        if w < 2:
            for row in chip_order:
                fill_product(dws[w], (low_t, dmid_t)[w], (d_qkv, att)[w], row * 2 + core, ctx)

    def over_chips(w):
        for k, row in enumerate(rows_of[1:]):
            arrived(nears[w].at[row], recv_c.at[w, row], twin)
            for owner in order:
                mine = dws[w].at[row * 2 + core, owner]
                mine[...] = kinds[w](mine[...].astype(single) + nears[w][row, owner].astype(single))
                out.push(mine, fars[w].at[k, owner], recv_y.at[w, k, owner], across[k])

    def over_context(w):
        arrived(nears[w].at[y], recv_c.at[w, y], twin)
        for owner in order:
            mine = dws[w].at[f, owner]
            for k in range(chips - 1):
                arrived(fars[w].at[k, owner], recv_y.at[w, k, owner], twin)

            def gathered():
                total = mine[...].astype(single) + nears[w][y, owner].astype(single)
                for k in range(chips - 1):
                    total = total + fars[w][k, owner].astype(single)
                return total

            @pl.when(z == owner)
            def _():
                mine[...] = kinds[w](gathered())

            for toward, sem, slots, edge, past in (
                ({"context": z + 1}, recv_u, ups[w], z == 0, z < owner),
                ({"context": z - 1}, recv_d, downs[w], z == ctx - 1, z > owner),
            ):

                @pl.when(jnp.logical_and(past, edge))
                def _():
                    mine[...] = kinds[w](gathered())

                @pl.when(jnp.logical_and(past, jnp.logical_not(edge)))
                def _():
                    arrived(slots.at[owner], sem.at[w, owner], twin)
                    mine[...] = kinds[w](gathered() + slots[owner].astype(single))

                out.push(mine, slots.at[owner], sem.at[w, owner], toward, past)

    def finish(w, result):
        for sem, slots, edge in ((recv_u, ups[w], z == 0), (recv_d, downs[w], z == ctx - 1)):
            mine = dws[w].at[f, z]

            @pl.when(jnp.logical_not(edge))
            def _():
                arrived(slots.at[z], sem.at[w, z], twin)
                mine[...] = kinds[w](mine[...].astype(single) + slots[z].astype(single))

        result(dws[w][f, z])

    start(2)
    start(1)
    over_chips(2)
    over_chips(1)
    start(0)
    over_chips(0)
    over_context(2)
    over_context(1)
    over_context(0)

    columns = tail.shape[-1]

    def keep_o(v):
        o_out[...] = v.astype(single)

    def keep_qkv(v):
        qkv_out[...] = v[:, : qkv_out.shape[1]].astype(single)
        tail[x] = v[:, v.shape[1] - columns :]

    def keep_s(v):
        near_s[x] = v

    finish(2, keep_s)
    for other in beside:
        out.push(near_s.at[x], near_s.at[x], recv_x.at[1, x], {"tensor": other})
    finish(1, keep_o)
    finish(0, keep_qkv)
    for other in beside:
        out.push(tail.at[x], tail.at[x], recv_x.at[2, x], {"tensor": other})
    for other in beside:
        arrived(take_out.at[other], recv_x.at[0, other], twin)
        arrived(near_s.at[other], recv_x.at[1, other], twin)
        arrived(tail.at[other], recv_x.at[2, other], twin)
    total = near_s[0]
    for k in range(1, ten):
        total = total + near_s[k]
    s_out[...] = total
    for k in range(ten):
        kv_out[:, k * columns : (k + 1) * columns] = tail[k].astype(single)
    keep_give.wait()
    out.drain()


def attn_back(low_t, dmid_t, d_qkv, att, terms, give, q_columns, fs, ctx, ten, ident):
    rows = low_t.shape[2]
    chips = fs // 2
    tail = d_qkv.shape[1] - q_columns
    blocks = [(rows, d_qkv.shape[1]), (rows, att.shape[1]), terms.shape[2:]]
    kinds = [half_type, half_type, single]
    both = list(zip(blocks, kinds))
    sends = (
        3 * (ten - 1)
        + 3 * (chips + (chips - 1) * ctx + 2 * ctx)
    )
    dma = pltpu.SemaphoreType.DMA
    return pl.pallas_call(
        functools.partial(attn_kernel, fs, ctx, ten),
        out_shape=[
            jax.ShapeDtypeStruct((rows, q_columns), single),
            jax.ShapeDtypeStruct((rows, att.shape[1]), single),
            jax.ShapeDtypeStruct(terms.shape[2:], single),
            jax.ShapeDtypeStruct((rows, ten * tail), single),
            jax.ShapeDtypeStruct((ten, *give.shape), give.dtype),
        ],
        in_specs=[VMEM] * 6,
        out_specs=[VMEM] * 5,
        scratch_shapes=[pltpu.VMEM((fs, ctx, *b), t) for b, t in both]
        + [pltpu.VMEM((chips, ctx, *b), t) for b, t in both]
        + [pltpu.VMEM((chips - 1, ctx, *b), t) for b, t in both]
        + [pltpu.VMEM((ctx, *b), t) for b, t in both] * 2
        + [
            pltpu.VMEM((ten, rows, tail), half_type),
            pltpu.VMEM((ten, *terms.shape[2:]), single),
            dma((1,)),
            dma((sends,)),
            dma((3, chips)),
            dma((3, chips - 1, ctx)),
            dma((3, ctx)),
            dma((3, ctx)),
            dma((3, ten)),
        ],
        compiler_params=pltpu.CompilerParams(
            collective_id=ident, has_side_effects=True, vmem_limit_bytes=VMEM_ALL
        ),
        name=f"attn_back_{ident}",
    )(low_t, dmid_t, d_qkv, att, terms, give)


def own_columns(weight, ctx):
    rows, columns = weight.shape
    return cast(weight).reshape(rows, ctx, columns // ctx).transpose(1, 0, 2)


def on_device(hidden_in, cotangent, segment_ids, positions, *params):
    masters, firsts, seconds = params[:8], params[8:16], params[16:]
    (
        attn_scale,
        query_weight,
        keyval_weight,
        output_weight,
        mlp_scale,
        gate_weight,
        up_weight,
        down_weight,
    ) = masters
    fs, ctx, ten = (lax.axis_size(name) for name in ("fsdp", "context", "tensor"))
    x = lax.axis_index("tensor")
    context_index = lax.axis_index("context")
    block, width = hidden_in.shape[1:]
    rows = query_weight.shape[0]
    half_rows = block // ten
    heads_width = query_weight.shape[1]
    heads_here = heads_width // HD
    hidden = hidden_in[0]
    cot = cotangent[0]
    hidden_half = lax.dynamic_slice_in_dim(hidden, x * half_rows, half_rows, 0)
    cot_half = lax.dynamic_slice_in_dim(cot, x * half_rows, half_rows, 0)
    is_key = x == 0

    qkv_block = jnp.concatenate(
        [
            cast(query_weight),
            cast(lax.dynamic_slice_in_dim(keyval_weight, x * HD, HD, 1)),
        ],
        axis=1,
    )
    lanes = -(-max(rows, block) // 128) * 128
    small = jnp.zeros((8, lanes), single)
    small = small.at[0, :rows].set(attn_scale).at[1, :rows].set(mlp_scale)
    small = small.at[2, :block].set(segment_ids[0].astype(single))
    small_all, qkv_all, out_all, dy_all = spread(
        [small, qkv_block, cast(output_weight).T],
        (False, False, False),
        cast(cot_half),
        fs,
        ctx,
        ten,
        1,
    )
    scale_one = cast(small_all[:, :, 0, :rows].reshape(-1)).astype(single)
    scale_two = cast(small_all[:, :, 1, :rows].reshape(-1)).astype(single)
    f = lax.axis_index("fsdp")
    seg_all = lax.dynamic_index_in_dim(small_all[:, :, 2, :block], f, 0, False).reshape(-1)
    qkv_full = qkv_all.reshape(width, -1)
    out_full = out_all.reshape(width, -1)
    dy_all = dy_all.reshape(-1, width)

    normed_one, inv_one, low_one = rms_forward(hidden, scale_one)
    qkv = dot(low_one, qkv_full, ((1,), (0,)))
    query = qkv[:, :heads_width].reshape(block, heads_here, HD)
    own = qkv[:, heads_width:]
    cosine, sine = rope_tables(positions[0])
    query_low = cast(rotate(query, cosine[:, None, :], sine[:, None, :]) * HD ** (-0.5))
    own_low = cast(jnp.where(is_key, rotate(own, cosine, sine), own))
    keyval_all = tokens_to_all(own_low, ctx, ten, 2).reshape(ctx, ten, block, HD)
    keys_all = keyval_all[:, 0].reshape(-1, HD)
    values_all = keyval_all[:, 1].reshape(-1, HD)
    rows_index = context_index * block + jnp.arange(block, dtype=jnp.int32)
    cols_index = jnp.arange(keys_all.shape[0], dtype=jnp.int32)
    allowed = (rows_index[:, None] >= cols_index[None, :]) & (
        segment_ids[0].astype(single)[:, None] == seg_all[None, :]
    )
    scores = jnp.einsum("bhd,jd->hbj", query_low, keys_all, preferred_element_type=single)
    masked = jnp.where(allowed, scores, masked_value)
    top = jnp.max(masked, axis=-1, keepdims=True)
    total = jnp.sum(jnp.where(allowed, jnp.exp(masked - top), 0.0), axis=-1, keepdims=True)
    lse = top + jnp.log(total)
    prob = jnp.where(allowed, jnp.exp(masked - lse), 0.0)
    prob_low = cast(prob)
    att_low = cast(
        jnp.einsum("hbj,jd->bhd", prob_low, values_all, preferred_element_type=single)
    )
    att_flat = att_low.reshape(block, heads_width)
    attn_part = dot(att_flat, out_full, ((1,), (1,)))
    attn_half = swap(cast(attn_part).reshape(ten, half_rows, width), ten, 3)
    mid_half = hidden_half + jnp.sum(attn_half.astype(single), axis=0)

    normed_two, inv_two, low_two = rms_forward(mid_half, scale_two)
    gate_slice, up_slice, down_slice, low_all = spread(
        [
            own_columns(gate_weight, ctx),
            own_columns(up_weight, ctx),
            own_columns(down_weight.T, ctx),
        ],
        (True, True, True),
        low_two,
        fs,
        ctx,
        ten,
        4,
    )
    gate_slice, up_slice, down_slice = (
        s.reshape(width, -1) for s in (gate_slice, up_slice, down_slice)
    )
    low_all = low_all.reshape(-1, width)
    gate = dot(low_all, gate_slice, ((1,), (0,)))
    upper = dot(low_all, up_slice, ((1,), (0,)))
    dhid = dot(dy_all, down_slice, ((1,), (0,)))
    gelu_gate, gelu_back = jax.vjp(gelu_tanh, gate)
    hid_low = cast(gelu_gate * upper)
    dgate_low = cast(gelu_back(dhid * upper)[0])
    dup_low = cast(dhid * gelu_gate)
    dnorm_part = cast(
        dot(dgate_low, gate_slice, ((1,), (1,))) + dot(dup_low, up_slice, ((1,), (1,)))
    )
    mlp_part = cast(dot(hid_low, down_slice, ((1,), (1,))))
    token_blocks = (ctx, ten, half_rows, width)
    row_blocks = (fs, ctx, rows, -1)
    dnorm_two, mlp_half, grad_wd, grad_wg, grad_wu = mlp_back(
        low_all.T.reshape(row_blocks),
        dy_all.T.reshape(row_blocks),
        hid_low,
        dgate_low,
        dup_low,
        dnorm_part.reshape(token_blocks),
        mlp_part.reshape(token_blocks),
        fs,
        ctx,
        ten,
        5,
    )
    dmid_norm, terms_two = rms_backward(dnorm_two, normed_two, inv_two, scale_two)
    dmid_half = cot_half + dmid_norm

    dmid_low = swap(
        jnp.broadcast_to(cast(dmid_half)[None], (ten, half_rows, width)), ten, 6
    ).reshape(block, width)
    datt_low = cast(dot(dmid_low, out_full, ((1,), (0,)))).reshape(block, heads_here, HD)
    delta = jnp.einsum("bhd,bhd->hb", datt_low, att_low, preferred_element_type=single)
    dprob = jnp.einsum("bhd,jd->hbj", datt_low, values_all, preferred_element_type=single)
    dscore_low = cast(prob * (dprob - delta[..., None]))
    dquery = jnp.einsum("hbj,jd->bhd", dscore_low, keys_all, preferred_element_type=single)
    dkey_part = jnp.einsum("hbj,bhd->jd", dscore_low, query_low, preferred_element_type=single)
    dvalue_part = jnp.einsum("hbj,bhd->jd", prob_low, datt_low, preferred_element_type=single)
    own_part = jnp.stack(
        [cast(part).reshape(ctx, block, HD) for part in (dkey_part, dvalue_part)], axis=1
    )
    down_own = sum_tokens(own_part.reshape(-1, HD), ctx, ten, 7)
    dquery_low = cast(
        unrotate(dquery, cosine[:, None, :], sine[:, None, :]) * HD ** (-0.5)
    ).reshape(block, heads_width)
    down_own = cast(jnp.where(is_key, unrotate(down_own, cosine, sine), down_own))
    d_qkv = jnp.concatenate([dquery_low, down_own], axis=1)
    dnorm_one = dot(d_qkv, qkv_full, ((1,), (1,)))
    dnorm_one = swap(cast(dnorm_one).reshape(ten, half_rows, width), ten, 8)
    dnorm_one = jnp.sum(dnorm_one.astype(single), axis=0)
    normed_half = lax.dynamic_slice_in_dim(normed_one, x * half_rows, half_rows, 0)
    inv_half = lax.dynamic_slice_in_dim(inv_one, x * half_rows, half_rows, 0)
    dinput_norm, terms_one = rms_backward(dnorm_one, normed_half, inv_half, scale_one)
    terms = jnp.stack([jnp.sum(terms_one, axis=0), jnp.sum(terms_two, axis=0)])
    terms = terms.reshape(2, fs, ctx, rows).transpose(1, 2, 0, 3)
    terms = jnp.pad(terms, ((0, 0), (0, 0), (0, 6), (0, -rows % 128)))
    give = cast(jnp.stack([mid_half + mlp_half, dmid_half + dinput_norm]))
    grad_wq, grad_wo, grad_s, grad_wkv, outs = attn_back(
        low_one.T.reshape(row_blocks),
        dmid_low.T.reshape(row_blocks),
        d_qkv,
        att_flat,
        terms,
        give,
        heads_width,
        fs,
        ctx,
        ten,
        9,
    )
    outs = outs.transpose(1, 0, 2, 3).reshape(2, 1, block, width).astype(single)

    def joined(grad):
        return grad.transpose(1, 0, 2).reshape(rows, -1).astype(single)

    grads = (
        grad_s[0, :rows],
        grad_wq,
        grad_wkv,
        grad_wo.T,
        grad_s[1, :rows],
        joined(grad_wg),
        joined(grad_wu),
        joined(grad_wd).T,
    )
    results = [
        adamw(weight, grad, first, second)
        for weight, grad, first, second in zip(masters, grads, firsts, seconds)
    ]
    return (
        outs[0],
        outs[1],
        *grads,
        *(entry[0] for entry in results),
        *(entry[1] for entry in results),
        *(entry[2] for entry in results),
    )


def solution(mesh):
    both = ("fsdp", "context")
    tokens = P("fsdp", "context", None)
    weights = (
        P(both),
        P(both, "tensor"),
        P(both, None),
        P("tensor", both),
        P(both),
        P(both, "tensor"),
        P(both, "tensor"),
        P("tensor", both),
    )
    return jax.shard_map(
        on_device,
        mesh=mesh,
        in_specs=(tokens, tokens, P("fsdp", "context"), P("fsdp", "context"), *(weights * 3)),
        out_specs=(tokens, tokens, *(weights * 4)),
        check_vma=False,
    )
```

time: 1210 us -> 782 us (0.65)
  waiting for transfers between devices: 692 us -> 0 us
  Pallas kernels: 0 us -> 588 us
  blocking collectives: 211 us -> 0 us
  matrix products: 107 us -> 64.4 us
  local copies, waits for them, and re-layouts: 93.5 us -> 62.1 us
  starting transfers between devices: 17.4 us -> 0 us
  between operations: 16.8 us -> 2.36 us
    pallas_call x0 -> x9, Pallas kernels: none -> 588 us  [the longest x2 209 us: spread(): pl.pallas_call(functools.partial(spread_kernel, fs, ctx, ten, count, spli...]
    reduce_scatter x11 -> x0, waiting for transfers between devices: 424 us -> none  [the longest x3 192 us: scatter_rows(): lax.psum_scatter(part.astype(half_type), ('fsdp', 'context'), scatter_dim...]
    all_gather x9 -> x0, waiting for transfers between devices: 211 us -> none  [the longest x3 94 us: gather_rows(): return lax.all_gather(block, ('fsdp', 'context'), axis=0, tiled=True)]
    all_to_all x3 -> x0, blocking collectives: 126 us -> none  [prepare_slice(): lax.all_to_all(parts, 'context', split_axis=0, concat_axis=0, tiled=True)]
    all_gather x4 -> x0, blocking collectives: 67.3 us -> none  [the longest x1 29.1 us: small_gather(): lax.all_gather(scales, ('fsdp', 'context'), axis=1, tiled=True)]
    unnamed x22 -> x0, waiting for transfers between devices: 57.8 us -> none
    dot_general x18 -> x10, matrix products: 101 us -> 58.9 us  [dot(): lax.dot_general(a, b, (dims, ((), ())), preferred_element_type=single)]
    convert_element_type x11 -> x9, local copies, waits for them, and re-layouts: 44.1 us -> 15.6 us  [the longest x4 10.5 us: joined(): return grad.transpose(1, 0, 2).reshape(rows, -1).astype(single)]
  transfers between devices with their start and end apart: 24 -> 0, of which waited for: 15 -> 0; matrix products, arithmetic and copies ran while one was open for 17% -> 0% of each run, Pallas kernels for 0% -> 0%
where the time goes in v1:
time: 782 us; the launch traced here: 772 us
  Pallas kernels  588 us (75%)
  matrix products  64.4 us (8%)
  local copies, waits for them, and re-layouts  62.1 us (8%)
  other arithmetic  55.9 us (7%)
    pallas_call x2, Pallas kernels, spread(): pl.pallas_call(functools.partial(spread_kernel, fs, ctx, ten, count, spli...  209 us
    pallas_call x1, Pallas kernels, mlp_back(): pl.pallas_call(functools.partial(back_kernel, fs, ctx, ten), out_shape=[j...  185 us
    pallas_call x1, Pallas kernels, attn_back(): pl.pallas_call(functools.partial(attn_kernel, fs, ctx, ten), out_shape=[j...  120 us
    dot_general x10, matrix products, dot(): lax.dot_general(a, b, (dims, ((), ())), preferred_element_type=single)  58.9 us
    pallas_call x3, Pallas kernels, swap(): pl.pallas_call(functools.partial(swap_kernel, ten), out_shape=jax.ShapeDt...  31.9 us
    sub x8, other arithmetic, adamw(): weight - learn_rate * (update + decay_rate * weight)  30.5 us
    pallas_call x1, Pallas kernels, tokens_to_all(): pl.pallas_call(functools.partial(tokens_kernel, ctx, ten), out_shape=jax....  29 us

profile of v1, /device:TPU:8, one launch (start us, length us, event | category | flops | bytes accessed | tf_op | source)
XLA Modules:
  0.0 772.3 jit_solution(13376253571762424917)
XLA Ops:
  7.0 86.0 %spread_1.1 = (f32[4,4,8,256]{3,2,1,0:T(8,128)}, bf16[4,4,160,1536]{3,2,1,0:T(8,128)(2,1)}, bf16[4,4,160,1280]{3,2,1,0:T(8,128)(2,1)}, bf16[4,2,64,2560]{3,2,1,0:T(8,128)(2,1)}) custom-call(f32[8,256]{1,0:T(8,128)} %copy-done.53, bf16[160,1536]{1,0:T(8,128)(2,1)} %pad_maximum_fusion.2.refs_1_, bf16[160,1280]{1,0:T(8,128)(2,1)} %convert_bitcast_fusion.5.refs_2_, ...), custom_call_target="tpu_custom_call" | custom-call | tf_op jit(solution)/shard_map/spread_1/pallas_call | solution.py:369
  94.3 4.5 fusion.18
  99.9 29.0 %tokens_2.1 = bf16[4,2,128,256]{3,2,1,0:T(8,128)(2,1)} custom-call(bf16[128,256]{1,0:T(8,128)(2,1)} %fusion.29.src), custom_call_target="tpu_custom_call" | custom-call | tf_op jit(solution)/shard_map/tokens_2/pallas_call | solution.py:176
  134.9 6.1 convolution_convert_fusion.2
  141.0 11.0 %swap_3.1 = bf16[2,64,2560]{2,1,0:T(8,128)(2,1)} custom-call(bf16[2,64,2560]{2,1,0:T(8,128)(2,1)} %bitcast.165), custom_call_target="tpu_custom_call" | custom-call | tf_op jit(solution)/shard_map/swap_3/pallas_call | solution.py:272
  160.9 3.7 reshape.428
  170.6 123.3 %spread_4.1 = (bf16[4,4,160,960]{3,2,1,0:T(8,128)(2,1)}, bf16[4,4,160,960]{3,2,1,0:T(8,128)(2,1)}, bf16[4,4,160,960]{3,2,1,0:T(8,128)(2,1)}, bf16[4,2,64,2560]{3,2,1,0:T(8,128)(2,1)}) custom-call(bf16[4,160,960]{2,1,0:T(8,128)(2,1)} %bitcast.160, bf16[4,160,960]{2,1,0:T(8,128)(2,1)} %get-tuple-element.171.refs_1_, ...), custom_call_target="tpu_custom_call" | custom-call | tf_op jit(solution)/shard_map/spread_4/pallas_call | solution.py:369
  293.9 7.6 fusion.74
  301.5 4.0 fusion.73
  310.4 8.1 %multiply_convert_fusion = (bf16[512,960]{1,0:T(8,128)(2,1)S(1)}, bf16[512,960]{1,0:T(8,128)(2,1)S(1)}, bf16[512,960]{1,0:T(8,128)(2,1)S(1)}) fusion(f32[512,960]{1,0:T(8,128)} %copy.135, f32[512,960]{1,0:T(8,128)} %copy.132, f32[512,960]{1,0:T(8,128)} %fusion.74, bf16[512,2560]{1,0:T(8,128)(2,1)S(1)} %bitcast.166, bf16[2560,960]{1,0:T(8,128)(2,1)} %bitcast.201), kind=kOutput, calls=%fused_computation.21 | convolution fusion | flops 2528870400 | bytes 16384000 | tf_op jit(solution)/shard_map/dot_general | solution.py:78
  318.5 8.0 %convolution_convert_fusion = bf16[512,2560]{1,0:T(8,128)(2,1)} fusion(bf16[512,960]{1,0:T(8,128)(2,1)S(1)} %get-tuple-element.144.hid, bf16[2560,960]{1,0:T(8,128)(2,1)} %bitcast.202), kind=kOutput, calls=%fused_computation.1 | convolution fusion | flops 2517893120 | bytes 8519680 | tf_op jit(solution)/shard_map/dot_general | solution.py:78
  326.5 5.3 fusion.75
  331.9 4.4 add_convert_fusion
  336.3 4.4 copy.130
  343.3 184.6 %mlp_back_5.1 = (f32[64,2560]{1,0:T(8,128)}, f32[64,2560]{1,0:T(8,128)}, bf16[4,160,960]{2,1,0:T(8,128)(2,1)}, bf16[4,160,960]{2,1,0:T(8,128)(2,1)}, bf16[4,160,960]{2,1,0:T(8,128)(2,1)}) custom-call(bf16[4,4,160,512]{3,2,1,0:T(8,128)(2,1)} %bitcast.155, bf16[4,4,160,512]{3,2,1,0:T(8,128)(2,1)} %bitcast.156, bf16[512,960]{1,0:T(8,128)(2,1)} %copy-done.34, ...), custom_call_target="tpu_custom_call" | custom-call | tf_op jit(solution)/shard_map/mlp_back_5/pallas_call | solution.py:510
  532.8 11.6 %swap_6.1 = bf16[2,64,2560]{2,1,0:T(8,128)(2,1)} custom-call(bf16[2,64,2560]{2,1,0:T(8,128)(2,1)} %broadcast_in_dim.19.src), custom_call_target="tpu_custom_call" | custom-call | tf_op jit(solution)/shard_map/swap_6/pallas_call | solution.py:272
  544.5 4.2 convolution_convert_fusion.3
  557.8 12.9 %sum_tokens_7.1 = f32[128,256]{1,0:T(8,128)} custom-call(bf16[4,2,128,256]{3,2,1,0:T(8,128)(2,1)} %pad_maximum_fusion.1.src), custom_call_target="tpu_custom_call" | custom-call | tf_op jit(solution)/shard_map/sum_tokens_7/pallas_call | solution.py:238
  571.9 6.7 convolution_convert_fusion.1
  578.6 9.3 %swap_8.1 = bf16[2,64,2560]{2,1,0:T(8,128)(2,1)} custom-call(bf16[2,64,2560]{2,1,0:T(8,128)(2,1)} %bitcast.164), custom_call_target="tpu_custom_call" | custom-call | tf_op jit(solution)/shard_map/swap_8/pallas_call | solution.py:272
  596.0 119.9 %attn_back_9.1 = (f32[160,1280]{1,0:T(8,128)}, f32[160,1280]{1,0:T(8,128)}, f32[8,256]{1,0:T(8,128)}, f32[160,512]{1,0:T(8,128)}, bf16[2,2,64,2560]{3,2,1,0:T(8,128)(2,1)}) custom-call(bf16[4,4,160,128]{3,2,1,0:T(8,128)(2,1)} %bitcast.173, bf16[4,4,160,128]{3,2,1,0:T(8,128)(2,1)} %bitcast.172, bf16[128,1536]{1,0:T(8,128)(2,1)} %pad_maximum_fusion.3.d_qkv, ...), custom_call_target="tpu_custom_call" | custom-call | tf_op jit(solution)/shard_map/attn_back_9/pallas_call | solution.py:680
  734.0 8.2 %multiply_subtract_fusion.2 = (f32[160,3840]{1,0:T(8,128)}, f32[160,3840]{1,0:T(8,128)}, f32[160,3840]{1,0:T(8,128)}) fusion(f32[160,3840]{1,0:T(8,128)} %param.43, f32[160,3840]{1,0:T(8,128)} %reshape.442, f32[160,3840]{1,0:T(8,128)} %param.51, f32[160,3840]{1,0:T(8,128)} %param.59), kind=kLoop, calls=%fused_computation.18 | loop fusion | flops 9216000 | bytes 17203200 | tf_op jit(solution)/shard_map/sub | solution.py:74
  747.6 8.2 %multiply_subtract_fusion.1 = (f32[160,3840]{1,0:T(8,128)}, f32[160,3840]{1,0:T(8,128)}, f32[160,3840]{1,0:T(8,128)}) fusion(f32[160,3840]{1,0:T(8,128)} %param.44, f32[160,3840]{1,0:T(8,128)} %reshape.443, f32[160,3840]{1,0:T(8,128)} %param.52, f32[160,3840]{1,0:T(8,128)} %param.60), kind=kLoop, calls=%fused_computation.16 | loop fusion | flops 9216000 | bytes 17203200 | tf_op jit(solution)/shard_map/sub | solution.py:74
  761.2 8.2 %multiply_subtract_fusion = (f32[3840,160]{0,1:T(8,128)}, f32[3840,160]{0,1:T(8,128)}, f32[3840,160]{0,1:T(8,128)}) fusion(f32[3840,160]{0,1:T(8,128)} %param.45, f32[3840,160]{0,1:T(8,128)} %param.53, f32[3840,160]{0,1:T(8,128)} %param.61, f32[160,3840]{1,0:T(8,128)} %reshape.444), kind=kLoop, calls=%fused_computation.14 | loop fusion | flops 9216000 | bytes 17203200 | tf_op jit(solution)/shard_map/sub | solution.py:74
  (258 shorter events, 90.9 us)
Async XLA Ops:
  0.7 5.5 copy-start.9
  3.6 90.6 %copy-start = (f32[1,128,2560]{2,1,0:T(8,128)S(1)}, f32[1,128,2560]{2,1,0:T(8,128)}, u32[]{:S(2)}) copy-start(f32[1,128,2560]{2,1,0:T(8,128)} %param.34) | copy-start | bytes 3932164
  98.9 32.4 %copy-start.54 = (f32[128]{0:T(128)}, f32[128]{0:T(128)S(1)}, u32[]{:S(2)}) copy-start(f32[128]{0:T(128)S(1)} %convert_bitcast_fusion.6) | copy-start | bytes 1540
  98.9 32.4 %copy-start.56 = (f32[128]{0:T(128)}, f32[128]{0:T(128)S(1)}, u32[]{:S(2)}) copy-start(f32[128]{0:T(128)S(1)} %multiply_power_fusion) | copy-start | bytes 1540
  133.6 7.3 copy-start.59
  134.9 6.1 copy-start.14
  153.5 13.5 %copy-start.2 = (f32[64,2560]{1,0:T(8,128)}, f32[64,2560]{1,0:T(8,128)S(1)}, u32[]{:S(2)}) copy-start(f32[64,2560]{1,0:T(8,128)S(1)} %get-tuple-element.139) | copy-start | bytes 1966084
  293.9 7.6 copy-start.17
  293.9 7.6 copy-start.73
  318.5 8.0 %copy-start.34 = (bf16[512,960]{1,0:T(8,128)(2,1)}, bf16[512,960]{1,0:T(8,128)(2,1)S(1)}, u32[]{:S(2)}) copy-start(bf16[512,960]{1,0:T(8,128)(2,1)S(1)} %get-tuple-element.144.hid) | copy-start | bytes 2949124
  318.5 8.0 %copy-start.33 = (bf16[512,960]{1,0:T(8,128)(2,1)}, bf16[512,960]{1,0:T(8,128)(2,1)S(1)}, u32[]{:S(2)}) copy-start(bf16[512,960]{1,0:T(8,128)(2,1)S(1)} %get-tuple-element.143.dgate) | copy-start | bytes 2949124
  318.5 13.3 %copy-start.32 = (bf16[512,960]{1,0:T(8,128)(2,1)}, bf16[512,960]{1,0:T(8,128)(2,1)S(1)}, u32[]{:S(2)}) copy-start(bf16[512,960]{1,0:T(8,128)(2,1)S(1)} %get-tuple-element.142.dup) | copy-start | bytes 2949124
  318.5 13.3 %slice-start = ((s8[5242880]{0:T(1024)(128)(4,1)}), s8[4194304]{0:T(1024)(128)(4,1)S(1)}, s32[]{:S(2)}) async-start(s8[5242880]{0:T(1024)(128)(4,1)} %bitcast.196), calls=%async_computation | async-start | bytes 8388608
  326.5 5.4 slice-start.1
  544.5 5.2 copy-start.7
  554.0 16.6 %copy-start.55 = (f32[128]{0:T(128)S(1)}, f32[128]{0:T(128)}, u32[]{:S(2)}) copy-start(f32[128]{0:T(128)} %copy-done.54) | copy-start | bytes 1540
  554.0 16.6 %copy-start.57 = (f32[128]{0:T(128)S(1)}, f32[128]{0:T(128)}, u32[]{:S(2)}) copy-start(f32[128]{0:T(128)} %copy-done.56) | copy-start | bytes 1540
  578.6 10.6 %copy-start.1 = (f32[1,128,2560]{2,1,0:T(8,128)S(1)}, f32[1,128,2560]{2,1,0:T(8,128)}, u32[]{:S(2)}) copy-start(f32[1,128,2560]{2,1,0:T(8,128)} %param.34) | copy-start | bytes 3932164
  578.6 10.6 %copy-start.50 = (f32[2560]{0:T(1024)S(1)}, f32[2560]{0:T(1024)}, u32[]{:S(2)}) copy-start(f32[2560]{0:T(1024)} %copy-done.49) | copy-start | bytes 30724
  578.6 10.6 %copy-start.68 = (f32[128]{0:T(128)S(1)}, f32[128]{0:T(128)}, u32[]{:S(2)}) copy-start(f32[128]{0:T(128)} %copy-done.67) | copy-start | bytes 1540
  734.0 8.2 %copy-start.29 = (bf16[4,160,960]{2,1,0:T(8,128)(2,1)S(1)}, bf16[4,160,960]{2,1,0:T(8,128)(2,1)}, u32[]{:S(2)}) copy-start(bf16[4,160,960]{2,1,0:T(8,128)(2,1)} %get-tuple-element.104) | copy-start | bytes 3686404
  747.6 8.2 %copy-start.28 = (bf16[4,160,960]{2,1,0:T(8,128)(2,1)S(1)}, bf16[4,160,960]{2,1,0:T(8,128)(2,1)}, u32[]{:S(2)}) copy-start(bf16[4,160,960]{2,1,0:T(8,128)(2,1)} %get-tuple-element.105) | copy-start | bytes 3686404
  761.2 8.2 %copy-start.13 = (f32[160,1280]{1,0:T(8,128)S(1)}, f32[160,1280]{1,0:T(8,128)}, u32[]{:S(2)}) copy-start(f32[160,1280]{1,0:T(8,128)} %get-tuple-element.209) | copy-start | bytes 2457604
  761.2 9.1 %copy-start.22 = (f32[160,512]{1,0:T(8,128)S(1)}, f32[160,512]{1,0:T(8,128)}, u32[]{:S(2)}) copy-start(f32[160,512]{1,0:T(8,128)} %get-tuple-element.210) | copy-start | bytes 983044
  (54 other events, 155.3 us)

commit v2 on v1

v2 whole, which is shorter than its diff:
```python
import functools

import jax
import jax.numpy as jnp
from jax import lax
from jax.experimental import pallas as pl
from jax.experimental.pallas import tpu as pltpu
from jax.sharding import PartitionSpec as P

HD = 256


norm_eps = 1e-06
beta_one = 0.9
beta_two = 0.999
adam_eps = 1e-08
learn_rate = 0.03
decay_rate = 0.1
adam_step = 4.0
rope_base = 10000.0
masked_value = -1e30

single = jnp.float32
half_type = jnp.bfloat16


def gelu_tanh(values):
    return jax.nn.gelu(values, approximate=True)


def rope_tables(positions):
    half = HD // 2
    freq = rope_base ** (-2.0 * jnp.arange(half).astype(jnp.float32) / HD)
    angle = positions.astype(jnp.float32)[..., None] * freq
    return (jnp.cos(angle), jnp.sin(angle))


def rotate(values, cosine, sine):
    half = values.shape[-1] // 2
    first = values[..., :half]
    second = values[..., half:]
    return jnp.concatenate(
        [first * cosine - second * sine, second * cosine + first * sine], axis=-1
    )


def unrotate(values, cosine, sine):
    half = values.shape[-1] // 2
    first = values[..., :half]
    second = values[..., half:]
    return jnp.concatenate(
        [first * cosine + second * sine, second * cosine - first * sine], axis=-1
    )


def rms_forward(values, scale):
    inverse = lax.rsqrt(jnp.mean(values * values, axis=-1, keepdims=True) + norm_eps)
    normed = values * inverse
    return (normed, inverse, (normed * (1.0 + scale)).astype(jnp.bfloat16))


def rms_backward(dnorm, normed, inverse, scale):
    dnormed = dnorm * (1.0 + scale)
    dvalues = inverse * (dnormed - normed * jnp.mean(dnormed * normed, axis=-1, keepdims=True))
    return (dvalues, dnorm * normed)


def adamw(weight, grad, first, second):
    first_new = beta_one * first + (1.0 - beta_one) * grad
    second_new = beta_two * second + (1.0 - beta_two) * grad * grad
    fix_one = 1.0 - beta_one**adam_step
    fix_two = 1.0 - beta_two**adam_step
    update = first_new / fix_one / (jnp.sqrt(second_new / fix_two) + adam_eps)
    return (weight - learn_rate * (update + decay_rate * weight), first_new, second_new)


def dot(a, b, dims):
    return lax.dot_general(a, b, (dims, ((), ())), preferred_element_type=single)


MESH = pl.DeviceIdType.MESH
ANY = pl.BlockSpec(memory_space=pl.ANY)
VMEM = pl.BlockSpec(memory_space=pltpu.VMEM)


def greet(peers):
    barrier = pltpu.get_barrier_semaphore()
    for peer in peers:
        pl.semaphore_signal(barrier, inc=1, device_id=peer, device_id_type=MESH)
    pl.semaphore_wait(barrier, len(peers))


def remote(src, dst, send, recv, peer):
    return pltpu.make_async_remote_copy(
        src_ref=src, dst_ref=dst, send_sem=send, recv_sem=recv, device_id=peer, device_id_type=MESH
    )


def arrived(dst, recv, peer):
    remote(dst, dst, recv, recv, peer).wait_recv()


def fsdp_place(fs):
    f = lax.axis_index("fsdp")
    core = lax.rem(f, 2)
    y = lax.div(f, 2)
    twin = {"fsdp": f + 1 - 2 * core}
    across = [{"fsdp": lax.rem(y + d, fs // 2) * 2 + core} for d in range(1, fs // 2)]
    return f, y, core, twin, across


class Sends:
    def __init__(self, send):
        self.send, self.made = send, []

    def push(self, src, dst, recv, peer, *conditions):
        copy = remote(src, dst, self.send.at[len(self.made)], recv, peer)
        self.made.append((copy, conditions))
        under(conditions, copy.start)

    def drain(self):
        for copy, conditions in self.made:
            under(conditions, copy.wait_send)


def under(conditions, action):
    if not conditions:
        action()
        return
    holds = conditions[0]
    for more in conditions[1:]:
        holds = jnp.logical_and(holds, more)
    pl.when(holds)(action)


def line_steps(z, ctx):
    for s in range(1, ctx):
        yield z - s, z >= s, z + 1, z + 1 < ctx
        yield z + s, z + s < ctx, z - 1, z >= 1


def tokens_kernel(ctx, ten, src, out, local, send, recv):
    z, x = lax.axis_index("context"), lax.axis_index("tensor")
    around = [lax.rem(z + d, ctx) for d in range(ctx)]
    across = [{"tensor": lax.rem(x + d, ten)} for d in range(1, ten)]
    greet([{"context": k} for k in around[1:]] + across)
    sends = []

    def push(ref, source, peer):
        copy = remote(ref, out.at[source, x], send.at[len(sends)], recv.at[source, x], peer)
        copy.start()
        sends.append(copy)

    for d in range(1, ctx):
        push(src, z, {"context": around[d]})
    for peer in across:
        push(src, z, peer)
    keep = pltpu.make_async_copy(src, out.at[z, x], local)
    keep.start()
    back = [lax.rem(z + ctx - d, ctx) for d in range(ctx)]
    for d in range(1, ctx):
        arrived(out.at[back[d], x], recv.at[back[d], x], {"context": back[d]})
        for peer in across:
            push(out.at[back[d], x], back[d], peer)
    for d in range(ctx):
        for peer in across:
            other = peer["tensor"]
            arrived(out.at[back[d], other], recv.at[back[d], other], peer)
    keep.wait()
    for copy in sends:
        copy.wait_send()


def tokens_to_all(block, ctx, ten, ident):
    sends = (ctx - 1) + ctx * (ten - 1)
    out = pl.pallas_call(
        functools.partial(tokens_kernel, ctx, ten),
        out_shape=jax.ShapeDtypeStruct((ctx, ten, *block.shape), block.dtype),
        in_specs=[VMEM],
        out_specs=VMEM,
        scratch_shapes=[
            pltpu.SemaphoreType.DMA(()),
            pltpu.SemaphoreType.DMA((sends,)),
            pltpu.SemaphoreType.DMA((ctx, ten)),
        ],
        compiler_params=pltpu.CompilerParams(collective_id=ident, has_side_effects=True),
        name=f"tokens_{ident}",
    )(block)
    return out.reshape(-1, block.shape[-1])


VMEM_ALL = 67043328


def cast(v):
    return v.astype(half_type)


def fill_product(dw, left, right, owner, ctx):
    def one(k, carry):
        dw[owner, k] = cast(
            lax.dot_general(
                left[owner, k], right[...], (((1,), (0,)), ((), ())), preferred_element_type=single
            )
        )
        return carry

    lax.fori_loop(0, ctx, one, 0)


def split_columns(ctx, weights, parts, wide, packed, small, load, store):
    columns = small.shape[-1]
    fetches = [pltpu.make_async_copy(weights[w], wide.at[w], load.at[w]) for w in range(3)]
    for fetch in fetches:
        fetch.start()
    for w in range(3):
        fetches[w].wait()
        for k in range(ctx):
            piece = cast(wide[w, :, k * columns : (k + 1) * columns])
            if w < 2:
                packed[k, :, w * columns : (w + 1) * columns] = piece
            else:
                small[k] = piece
    puts = [pltpu.make_async_copy(v, parts[j], store.at[j]) for j, v in enumerate((packed, small))]
    for put in puts:
        put.start()
    for put in puts:
        put.wait()


def first_kernel(fs, ctx, ten, count, *refs):
    srcs, weights = refs[: count + 1], refs[count + 1 : count + 4]
    refs = refs[count + 4 :]
    outs, parts = refs[: count + 1], refs[count + 1 : count + 3]
    wide, packed, small, load, store, local, send, recv, recv_t = refs[count + 3 :]
    f, y, core, twin, across = fsdp_place(fs)
    z, x = lax.axis_index("context"), lax.axis_index("tensor")
    beside = [{"tensor": lax.rem(x + d, ten)} for d in range(1, ten)]
    back = [lax.rem(z + ctx - d, ctx) for d in range(ctx)]
    up, down = {"context": z + 1}, {"context": z - 1}
    nxt, prv = lax.rem(z + 1, ctx), back[1]
    greet([{"context": nxt}, {"context": prv}] + across + [twin] + beside)
    out = Sends(send)
    keeps = []

    def where(w, source):
        if w == count:
            return outs[w].at[source, x], recv_t.at[source, x], beside
        return outs[w].at[f, source], recv.at[w, f, source], across + [twin]

    for w in range(count + 1):
        mine, sem, peers = where(w, z)
        out.push(srcs[w], mine, sem, up, z + 1 < ctx)
        out.push(srcs[w], mine, sem, down, z >= 1)
        for peer in peers:
            out.push(srcs[w], mine, sem, peer)
        keeps.append(pltpu.make_async_copy(srcs[w], mine, local.at[w]))
        keeps[-1].start()
    split_columns(ctx, weights, parts, wide, packed, small, load, store)
    for source, exists, onward, more in line_steps(z, ctx):
        for w in range(count + 1):
            block, sem, peers = where(w, source)
            under((exists,), lambda: arrived(block, sem, twin))
            out.push(block, block, sem, {"context": onward}, exists, more)
            for peer in peers:
                out.push(block, block, sem, peer, exists)
    chain = [(z, ())] + [(source, (exists,)) for source, exists, _, _ in line_steps(z, ctx)]
    for source, when in chain:
        for w in range(count):
            for peer in across:
                owner = peer["fsdp"]
                block, sem = outs[w].at[owner, source], recv.at[w, owner, source]
                under(when, lambda: arrived(block, sem, twin))
                out.push(block, block, sem, twin, *when)
    for source in back:
        for w in range(count):
            for step in range(fs // 2):
                owner = lax.rem(y + step, fs // 2) * 2 + 1 - core
                arrived(outs[w].at[owner, source], recv.at[w, owner, source], twin)
        for peer in beside:
            arrived(outs[count].at[source, peer["tensor"]], recv_t.at[source, peer["tensor"]], twin)
    for keep in keeps:
        keep.wait()
    out.drain()


def spread(blocks, tokens, weights, fs, ctx, ten, ident):
    count = len(blocks)
    chips = fs // 2
    lines = 2 + 2 * (ctx - 1)
    sends = count * (lines + (2 * ctx - 1) * (2 * chips - 1)) + lines + (2 * ctx - 1) * (ten - 1)
    rows, wide = weights[0].shape
    part = (ctx, rows, wide // ctx)
    pair = (ctx, rows, 2 * (wide // ctx))
    dma = pltpu.SemaphoreType.DMA
    return pl.pallas_call(
        functools.partial(first_kernel, fs, ctx, ten, count),
        out_shape=[jax.ShapeDtypeStruct((fs, ctx, *b.shape), b.dtype) for b in blocks]
        + [jax.ShapeDtypeStruct((ctx, ten, *tokens.shape), tokens.dtype)]
        + [jax.ShapeDtypeStruct(pair, half_type), jax.ShapeDtypeStruct(part, half_type)],
        in_specs=[ANY] * (count + 4),
        out_specs=[ANY] * (count + 3),
        scratch_shapes=[
            pltpu.VMEM((3, rows, wide), single),
            pltpu.VMEM(pair, half_type),
            pltpu.VMEM(part, half_type),
            dma((3,)),
            dma((2,)),
            dma((count + 1,)),
            dma((sends,)),
            dma((count, fs, ctx)),
            dma((ctx, ten)),
        ],
        compiler_params=pltpu.CompilerParams(
            collective_id=ident, has_side_effects=True, vmem_limit_bytes=VMEM_ALL
        ),
        name=f"spread_{ident}",
    )(*blocks, tokens, *weights)


def line_sum(z, ctx, owner, gathered, mine, slots, sem, out, kind, done):
    @pl.when(z == owner)
    def _():
        done(gathered())

    for toward, at, edge, past in (
        ({"context": z + 1}, owner + 1, z == 0, z < owner),
        ({"context": z - 1}, owner, z == ctx - 1, z > owner),
    ):

        @pl.when(jnp.logical_and(past, edge))
        def _():
            mine[...] = kind(gathered())

        @pl.when(jnp.logical_and(past, jnp.logical_not(edge)))
        def _():
            arrived(slots.at[at], sem.at[at], toward)
            mine[...] = kind(gathered() + slots[at].astype(single))

        out.push(mine, slots.at[at], sem.at[at], toward, past)


def line_end(z, ctx, slots, sem, add):
    for at, edge in ((z + 1, z == 0), (z, z == ctx - 1)):

        @pl.when(jnp.logical_not(edge))
        def _():
            arrived(slots.at[at], sem.at[at], {"context": z})
            add(slots[at].astype(single))


def ends_first(ctx):
    order = []
    for k in range((ctx + 1) // 2):
        order += [ctx - 1 - k] + ([k] if k != ctx - 1 - k else [])
    return order


def chip_tiles(weight, held, load, use):
    chips = weight.shape[0] // 2

    def fetch(k, slot):
        return pltpu.make_async_copy(weight.at[pl.ds(2 * k, 2)], held.at[slot], load.at[slot])

    fetch(0, 0).start()

    def step(k, carry):
        slot = lax.rem(k, 2)
        fetch(k, slot).wait()

        @pl.when(k + 1 < chips)
        def _():
            fetch(k + 1, 1 - slot).start()

        use(k, held[slot].reshape(-1, held.shape[-1]))
        return carry

    lax.fori_loop(0, chips, step, 0)


def forward_kernel(fs, ctx, ten, *refs):
    attn, hidden, scale, dy, part_p, part_d = refs[:6]
    slice_p, slice_d, hid, dpair, low_t, dy_t, mid, low = refs[6:14]
    low_all, take, held_p, held_d, sums_p, sums_d = refs[14:20]
    load, local, send, recv_p, recv_d, recv_t, recv_x = refs[20:]
    f, y, core, twin, across = fsdp_place(fs)
    z, x = lax.axis_index("context"), lax.axis_index("tensor")
    rows, columns = part_d.shape[1:]
    width = low.shape[1]
    count = hid.shape[0]
    beside = [{"tensor": lax.rem(x + d, ten)} for d in range(1, ten)]
    around = [lax.rem(z + d, ctx) for d in range(ctx)]
    back = [lax.rem(z + ctx - d, ctx) for d in range(ctx)]
    greet([{"context": k} for k in around[1:]] + across + [twin] + beside)
    out = Sends(send)
    parts, slices, recvs = (part_d, part_p), (slice_d, slice_p), (recv_d, recv_p)
    for peer in beside:
        out.push(attn.at[peer["tensor"]], take.at[x], recv_x.at[x], peer)

    def block(w, owner, source):
        return slices[w].at[owner, source], recvs[w].at[owner, source]

    def to_context(w, d):
        dst, sem = block(w, f, z)
        out.push(parts[w].at[around[d]], dst, sem, {"context": around[d]})

    def from_context(w, d):
        dst, sem = block(w, f, back[d])
        arrived(dst, sem, twin)
        for peer in across + [twin]:
            out.push(dst, dst, sem, peer)

    def from_chips(w):
        for d in range(ctx):
            for peer in across:
                dst, sem = block(w, peer["fsdp"], back[d])
                arrived(dst, sem, twin)
                out.push(dst, dst, sem, twin)

    def from_twin(w):
        for d in range(ctx):
            for step in range(fs // 2):
                dst, sem = block(w, lax.rem(y + step, fs // 2) * 2 + 1 - core, back[d])
                arrived(dst, sem, twin)

    to_context(0, 1)
    keeps = []
    for w in range(2):
        dst, sem = block(w, f, z)
        for peer in across + [twin]:
            out.push(parts[w].at[z], dst, sem, peer)
        keeps.append(pltpu.make_async_copy(parts[w].at[z], dst, local.at[w]))
        keeps[-1].start()
    total = hidden[...] + attn[x].astype(single)
    for peer in beside:
        other = peer["tensor"]
        arrived(take.at[other], recv_x.at[other], twin)
        total = total + take[other].astype(single)
    mid[...] = total
    inverse = lax.rsqrt(jnp.mean(total * total, axis=-1, keepdims=True) + norm_eps)
    low_all[z, x] = cast(total * inverse * (1.0 + scale[...]))
    mine = low_all.at[z, x]
    out.push(mine, mine, recv_t.at[z, x], {"context": z + 1}, z + 1 < ctx)
    out.push(mine, mine, recv_t.at[z, x], {"context": z - 1}, z >= 1)
    for peer in beside:
        out.push(mine, mine, recv_t.at[z, x], peer)
    later = [(0, d) for d in range(2, ctx)] + [(1, d) for d in range(1, ctx)]
    for step, (source, exists, onward, more) in enumerate(line_steps(z, ctx)):
        if step % 2 == 0:
            to_context(*later.pop(0))
            from_context(0, step // 2 + 1)
        here, sem = low_all.at[source, x], recv_t.at[source, x]
        under((exists,), lambda: arrived(here, sem, twin))
        out.push(here, here, sem, {"context": onward}, exists, more)
        for peer in beside:
            out.push(here, here, sem, peer, exists)
    for more in later:
        to_context(*more)

    def turned(dst, src):
        for j in range(fs * ctx):
            piece = src[:, :, :, j * rows : (j + 1) * rows].reshape(count, rows)
            dst[j // ctx, j % ctx] = piece.T

    def product(weight, held, left, sums):
        deep = width // (fs // 2)

        def use(k, tile):
            lanes = pl.ds(pl.multiple_of(k * deep, deep), deep)
            add = jnp.dot(
                left[:, :, :, lanes].reshape(count, deep), tile, preferred_element_type=single
            )

            @pl.when(k == 0)
            def _():
                sums[...] = add

            @pl.when(k > 0)
            def _():
                sums[...] += add

        chip_tiles(weight, held, load, use)

    from_chips(0)
    turned(dy_t, dy)
    from_context(1, 1)
    for source in back:
        for peer in beside:
            other = peer["tensor"]
            arrived(low_all.at[source, other], recv_t.at[source, other], twin)
    from_twin(0)
    keeps[0].wait()
    product(slice_d, held_d, dy, sums_d)
    for d in range(2, ctx):
        from_context(1, d)
    turned(low_t, low_all)
    from_chips(1)
    from_twin(1)
    keeps[1].wait()
    product(slice_p, held_p, low_all, sums_p)
    low[...] = low_all[z, x]
    root = (2.0 / jnp.pi) ** 0.5
    part = count // ctx

    def finish(k, carry):
        here = pl.ds(pl.multiple_of(k * part, part), part)
        pair, dhid = sums_p[here, :], sums_d[here, :]
        gate, upper = pair[:, :columns], pair[:, columns:]
        square = gate * gate
        tanh = jnp.tanh(root * gate * (1.0 + 0.044715 * square))
        gelu = 0.5 * gate * (1.0 + tanh)
        slope = 0.5 * (1.0 + tanh) + 0.5 * gate * (1.0 - tanh * tanh) * root * (
            1.0 + 3.0 * 0.044715 * square
        )
        hid[here, :] = cast(gelu * upper)
        dpair[here, :columns] = cast(dhid * upper * slope)
        dpair[here, columns:] = cast(dhid * gelu)
        return carry

    lax.fori_loop(0, ctx, finish, 0)
    out.drain()


def mlp_forward(attn, hidden, scale, dy_all, part_p, part_d, fs, ctx, ten, ident):
    rows, columns = part_d.shape[1:]
    t_rows, width = hidden.shape
    count = ctx * ten * t_rows
    chips = fs // 2
    sends = 2 * (ten - 1) + 2 * ctx + 2 * (ctx - 1) * (ten - 1) + 2 * (3 * ctx - 1 + 3 * ctx * chips)
    dma = pltpu.SemaphoreType.DMA
    shape = jax.ShapeDtypeStruct
    return pl.pallas_call(
        functools.partial(forward_kernel, fs, ctx, ten),
        out_shape=[
            shape((fs, ctx, rows, 2 * columns), half_type),
            shape((fs, ctx, rows, columns), half_type),
            shape((count, columns), half_type),
            shape((count, 2 * columns), half_type),
            shape((fs, ctx, rows, count), half_type),
            shape((fs, ctx, rows, count), half_type),
            shape((t_rows, width), single),
            shape((t_rows, width), half_type),
        ],
        in_specs=[VMEM] * 4 + [ANY] * 2,
        out_specs=[ANY] * 2 + [VMEM] * 6,
        scratch_shapes=[
            pltpu.VMEM((ctx, ten, t_rows, width), half_type),
            pltpu.VMEM((ten, t_rows, width), half_type),
            pltpu.VMEM((2, 2, ctx, rows, 2 * columns), half_type),
            pltpu.VMEM((2, 2, ctx, rows, columns), half_type),
            pltpu.VMEM((count, 2 * columns), single),
            pltpu.VMEM((count, columns), single),
            dma((2,)),
            dma((2,)),
            dma((sends,)),
            dma((fs, ctx)),
            dma((fs, ctx)),
            dma((ctx, ten)),
            dma((ten,)),
        ],
        compiler_params=pltpu.CompilerParams(
            collective_id=ident, has_side_effects=True, vmem_limit_bytes=VMEM_ALL
        ),
        name=f"mlp_forward_{ident}",
    )(attn, hidden, scale, dy_all, part_p, part_d)


def token_products(source, left, weight, held, load):
    def use(k, tile):
        term = lax.dot_general(
            left[...], tile, (((1,), (1,)), ((), ())), preferred_element_type=single
        )
        deep = tile.shape[0]
        lanes = pl.ds(pl.multiple_of(k * deep, deep), deep)
        source[:, :, :, lanes] = cast(term).reshape(*source.shape[:3], deep)

    chip_tiles(weight, held, load, use)


def token_start(source, first, recv, out, beside, order):
    for owner in order:
        for k, other in enumerate(beside):
            out.push(
                source.at[owner, other], first.at[k, owner], recv.at[k, owner], {"tensor": other}
            )


def token_step(owner, source, first, recv, slots, sems, z, x, ctx, out, done):
    for k in range(first.shape[0]):
        arrived(first.at[k, owner], recv.at[k, owner], {"tensor": x})

    def gathered():
        total = source[owner, x].astype(single)
        for k in range(first.shape[0]):
            total = total + first[k, owner].astype(single)
        return total

    line_sum(z, ctx, owner, gathered, source.at[owner, x], slots, sems, out, cast, done)


def back_kernel(fs, ctx, ten, *refs):
    low_t, dy_t, hid, dpair, mid, cot, scale, slice_p = refs[:8]
    dmid, dmid_all, terms, out_p, out_d = refs[8:13]
    dws, nears, fars = refs[13:15], refs[15:17], refs[17:19]
    source, first, line, held = refs[19:23]
    load, local, send, recv_c, recv_y, recv_z, recv_tx, recv_t, recv_x = refs[23:]
    f, y, core, twin, across = fsdp_place(fs)
    z, x = lax.axis_index("context"), lax.axis_index("tensor")
    chips = fs // 2
    around = [lax.rem(z + d, ctx) for d in range(ctx)]
    beside = [lax.rem(x + d, ten) for d in range(1, ten)]
    rows_of = [lax.rem(y + d, chips) for d in range(chips)]
    chip_order = rows_of[1:] + rows_of[:1]
    order = around[1:] + around[:1]
    greet([{"context": k} for k in around[1:]] + across + [twin] + [{"tensor": k} for k in beside])
    out = Sends(send)
    outs = (out_d, out_p)
    keeps = []

    def products(w):
        left, right = (dy_t, low_t)[w], (hid, dpair)[w]
        for row in chip_order:
            fill_product(dws[w], left, right, row * 2 + 1 - core, ctx)
            out.push(dws[w].at[row * 2 + 1 - core], nears[w].at[row], recv_c.at[w, row], twin)
        for row in chip_order:
            fill_product(dws[w], left, right, row * 2 + core, ctx)

    def over_chips(w):
        for k, row in enumerate(rows_of[1:]):
            arrived(nears[w].at[row], recv_c.at[w, row], twin)
            for d, owner in enumerate(order):
                mine = dws[w].at[row * 2 + core, owner]
                mine[...] = cast(mine[...].astype(single) + nears[w][row, owner].astype(single))
                out.push(mine, fars[w].at[k, d], recv_y.at[w, k, d], across[k])

    def over_context(w, d):
        if d == 0:
            arrived(nears[w].at[y], recv_c.at[w, y], twin)
        owner = order[d]
        mine = dws[w].at[f, owner]
        total = mine[...].astype(single) + nears[w][y, owner].astype(single)
        for k in range(chips - 1):
            arrived(fars[w].at[k, d], recv_y.at[w, k, d], twin)
            total = total + fars[w][k, d].astype(single)
        mine[...] = cast(total)
        if d < ctx - 1:
            out.push(mine, outs[w].at[z], recv_z.at[w, z], {"context": owner})
        else:
            keep = pltpu.make_async_copy(mine, outs[w].at[z], local.at[w])
            keep.start()
            keeps.append(keep)

    def keep_sum(v):
        dmid[...] = v

    def add_sum(v):
        dmid[...] += v

    token_products(source, dpair, slice_p, held, load)
    ends = ends_first(ctx)
    token_start(source, first, recv_tx, out, beside, ends)
    products(0)
    over_chips(0)
    products(1)
    over_chips(1)
    for d, owner in enumerate(ends):
        token_step(owner, source, first, recv_tx, line, recv_t, z, x, ctx, out, keep_sum)
        over_context(0, d)
    line_end(z, ctx, line, recv_t, add_sum)
    dnorm = dmid[...]
    values = mid[...]
    inverse = lax.rsqrt(jnp.mean(values * values, axis=-1, keepdims=True) + norm_eps)
    normed = values * inverse
    dnormed = dnorm * (1.0 + scale[...])
    terms[...] = jnp.sum(dnorm * normed, axis=0, keepdims=True)
    total = cot[...] + inverse * (
        dnormed - normed * jnp.mean(dnormed * normed, axis=-1, keepdims=True)
    )
    dmid[...] = total
    dmid_all[x] = cast(total)
    for other in beside:
        out.push(dmid_all.at[x], dmid_all.at[x], recv_x.at[x], {"tensor": other})
    for d in range(ctx):
        over_context(1, d)
    for other in beside:
        arrived(dmid_all.at[other], recv_x.at[other], twin)
    for w in range(2):
        for k in around[1:]:
            arrived(outs[w].at[k], recv_z.at[w, k], twin)
    for keep in keeps:
        keep.wait()
    out.drain()


def mlp_back(low_t, dy_t, hid, dpair, mid, cot, scale, slice_p, fs, ctx, ten, ident):
    rows, columns = low_t.shape[2], hid.shape[1]
    t_rows, width = mid.shape
    chips = fs // 2
    blocks = [(rows, columns), (rows, 2 * columns)]
    sends = ctx * (ten - 1) + 2 * ctx + 2 * (chips + (chips - 1) * ctx + ctx - 1) + ten - 1
    dma = pltpu.SemaphoreType.DMA
    shape = jax.ShapeDtypeStruct
    return pl.pallas_call(
        functools.partial(back_kernel, fs, ctx, ten),
        out_shape=[
            shape((t_rows, width), single),
            shape((ten, t_rows, width), half_type),
            shape((1, width), single),
            shape((ctx, rows, 2 * columns), half_type),
            shape((ctx, rows, columns), half_type),
        ],
        in_specs=[VMEM] * 7 + [ANY],
        out_specs=[VMEM] * 3 + [ANY] * 2,
        scratch_shapes=[pltpu.VMEM((fs, ctx, *b), half_type) for b in blocks]
        + [pltpu.VMEM((chips, ctx, *b), half_type) for b in blocks]
        + [pltpu.VMEM((chips - 1, ctx, *b), half_type) for b in blocks]
        + [
            pltpu.VMEM((ctx, ten, t_rows, width), half_type),
            pltpu.VMEM((ten - 1, ctx, t_rows, width), half_type),
            pltpu.VMEM((ctx + 1, t_rows, width), half_type),
            pltpu.VMEM((2, 2, ctx, rows, 2 * columns), half_type),
            dma((2,)),
            dma((2,)),
            dma((sends,)),
            dma((2, chips)),
            dma((2, chips - 1, ctx)),
            dma((2, ctx)),
            dma((ten - 1, ctx)),
            dma((ctx + 1,)),
            dma((ten,)),
        ],
        compiler_params=pltpu.CompilerParams(
            collective_id=ident, has_side_effects=True, vmem_limit_bytes=VMEM_ALL
        ),
        name=f"mlp_back_{ident}",
    )(low_t, dy_t, hid, dpair, mid, cot, scale, slice_p)


def update_kernel(at, parts, weight, first, second, grad_out, weight_out, first_out, second_out):
    columns = weight.shape[1] // parts.shape[0]
    for k in range(parts.shape[0]):
        grad = parts[k, :, at * columns : (at + 1) * columns].astype(single)
        here = (slice(None), slice(k * columns, (k + 1) * columns))
        grad_out[here] = grad
        weight_out[here], first_out[here], second_out[here] = adamw(
            weight[here], grad, first[here], second[here]
        )


def update(parts, at, weight, first, second, ident):
    ctx, rows, columns = parts.shape
    step = 32 if rows % 32 == 0 else 8
    spec = pl.BlockSpec((step, weight.shape[1]), lambda i: (i, 0))
    part = pl.BlockSpec((ctx, step, columns), lambda i: (0, i, 0))
    return pl.pallas_call(
        functools.partial(update_kernel, at),
        grid=(rows // step,),
        out_shape=[jax.ShapeDtypeStruct(weight.shape, single)] * 4,
        in_specs=[part, spec, spec, spec],
        out_specs=[spec] * 4,
        compiler_params=pltpu.CompilerParams(vmem_limit_bytes=VMEM_ALL),
        name=f"update_{ident}",
    )(parts, weight, first, second)


def attn_kernel(fs, ctx, ten, *refs):
    low_t, dmid_t, d_query, att, own, cosine, sine, hidden, mid, dmid, scale, terms = refs[:12]
    hid, slice_d, slice_q = refs[12:15]
    out_q, out_o, out_s, out_kv, tokens = refs[15:20]
    dws, nears, fars, lines = refs[20:23], refs[23:26], refs[26:29], refs[29:32]
    source, first, line, first_k, line_k, sum_k, d_qkv, dnorm, take = refs[32:41]
    held_d, held_q, tail, pool, total_m, own_sums = refs[41:47]
    load, send, recv_c, recv_y, recv_z, recv_tx, recv_t, recv_kx, recv_k, recv_n, recv_x = refs[47:]
    f, y, core, twin, across = fsdp_place(fs)
    z, x = lax.axis_index("context"), lax.axis_index("tensor")
    chips = fs // 2
    rows = low_t.shape[2]
    beside = [lax.rem(x + d, ten) for d in range(1, ten)]
    rows_of = [lax.rem(y + d, chips) for d in range(chips)]
    chip_order = rows_of[1:] + rows_of[:1]
    nxt, prv = lax.rem(z + 1, ctx), lax.rem(z + ctx - 1, ctx)
    greet([{"context": nxt}, {"context": prv}] + across + [twin] + [{"tensor": k} for k in beside])
    out = Sends(send)
    order = ends_first(ctx)
    kinds = (cast, cast, lambda v: v)
    heads = d_query.shape[1]
    rights = (d_qkv, att)
    lefts = (low_t, dmid_t)

    def start(w):
        for row in chip_order:
            owner = row * 2 + 1 - core
            if w < 2:
                fill_product(dws[w], lefts[w], rights[w], owner, ctx)
            out.push(dws[w].at[owner], nears[w].at[row], recv_c.at[w, row], twin)
        if w < 2:
            for row in chip_order:
                fill_product(dws[w], lefts[w], rights[w], row * 2 + core, ctx)

    def over_chips(w):
        for k, row in enumerate(rows_of[1:]):
            arrived(nears[w].at[row], recv_c.at[w, row], twin)
            for owner in order:
                mine = dws[w].at[row * 2 + core, owner]
                mine[...] = kinds[w](mine[...].astype(single) + nears[w][row, owner].astype(single))
                out.push(mine, fars[w].at[k, owner], recv_y.at[w, k, owner], across[k])

    def over_context(w, d):
        if d == 0:
            arrived(nears[w].at[y], recv_c.at[w, y], twin)
        owner = order[d]
        mine = dws[w].at[f, owner]
        for k in range(chips - 1):
            arrived(fars[w].at[k, owner], recv_y.at[w, k, owner], twin)

        def gathered():
            total = mine[...].astype(single) + nears[w][y, owner].astype(single)
            for k in range(chips - 1):
                total = total + fars[w][k, owner].astype(single)
            return total

        def done(v):
            mine[...] = kinds[w](v)

        line_sum(
            z, ctx, owner, gathered, mine, lines[w], recv_z.at[w], out, kinds[w], done
        )

    def finish(w):
        def add(v):
            dws[w][f, z] = kinds[w](dws[w][f, z].astype(single) + v)

        line_end(z, ctx, lines[w], recv_z.at[w], add)
        return dws[w][f, z]

    own_sums[...] = own[...]
    token_start(own_sums, first_k, recv_kx, out, beside, order)
    start(1)
    token_products(source, hid, slice_d, held_d, load)
    token_start(source, first, recv_tx, out, beside, order)
    over_chips(1)

    def keep_k(v):
        sum_k[...] = v

    def add_k(v):
        sum_k[...] += v

    for owner in order:
        token_step(owner, own_sums, first_k, recv_kx, line_k, recv_k, z, x, ctx, out, keep_k)
    line_end(z, ctx, line_k, recv_k, add_k)
    summed = sum_k[...]
    half = summed.shape[1] // 2
    a, b = summed[:, :half], summed[:, half:]
    c, s = cosine[...], sine[...]
    is_key = x == 0
    d_qkv[:, :heads] = d_query[...]
    d_qkv[:, heads : heads + half] = cast(jnp.where(is_key, a * c + b * s, a))
    d_qkv[:, heads + half :] = cast(jnp.where(is_key, b * c - a * s, b))
    start(0)
    over_chips(0)
    token_products(dnorm, d_qkv, slice_q, held_q, load)
    for other in beside:
        out.push(dnorm.at[0, other], take.at[x], recv_n.at[x], {"tensor": other})

    def keep_m(v):
        total_m[...] = v

    def add_m(v):
        total_m[...] += v

    for d, owner in enumerate(order):
        token_step(owner, source, first, recv_tx, line, recv_t, z, x, ctx, out, keep_m)
        over_context(1, d)
    dnorm_one = dnorm[0, x].astype(single)
    for other in beside:
        arrived(take.at[other], recv_n.at[other], twin)
        dnorm_one = dnorm_one + take[other].astype(single)
    values = hidden[...]
    inverse = lax.rsqrt(jnp.mean(values * values, axis=-1, keepdims=True) + norm_eps)
    normed = values * inverse
    dnormed = dnorm_one * (1.0 + scale[...])
    tokens[x, 1] = cast(
        dmid[...]
        + inverse * (dnormed - normed * jnp.mean(dnormed * normed, axis=-1, keepdims=True))
    )
    sums = jnp.sum(dnorm_one * normed, axis=0, keepdims=True)
    dws[2][...] = jnp.zeros_like(dws[2])
    for j in range(fs * ctx):
        at = slice(j * rows, (j + 1) * rows)
        dws[2][j // ctx, j % ctx, 0:1, :rows] = sums[:, at]
        dws[2][j // ctx, j % ctx, 1:2, :rows] = terms[:, at]
    start(2)
    line_end(z, ctx, line, recv_t, add_m)
    tokens[x, 0] = cast(mid[...] + total_m[...])
    for other in beside:
        out.push(tokens.at[x], tokens.at[x], recv_x.at[0, x], {"tensor": other})
    over_chips(2)
    for d in range(ctx):
        over_context(2, d)
        over_context(0, d)
    pool[x] = finish(2)
    for other in beside:
        out.push(pool.at[x], pool.at[x], recv_x.at[1, x], {"tensor": other})
    grad = finish(0)
    out_q[...] = grad[:, :heads].astype(single)
    tail[x] = grad[:, heads:]
    for other in beside:
        out.push(tail.at[x], tail.at[x], recv_x.at[2, x], {"tensor": other})
    out_o[...] = finish(1).astype(single)
    for other in beside:
        arrived(tokens.at[other], recv_x.at[0, other], twin)
        arrived(pool.at[other], recv_x.at[1, other], twin)
        arrived(tail.at[other], recv_x.at[2, other], twin)
    total = pool[0]
    for k in range(1, ten):
        total = total + pool[k]
    out_s[...] = total
    columns = tail.shape[-1]
    for k in range(ten):
        out_kv[:, k * columns : (k + 1) * columns] = tail[k].astype(single)
    out.drain()


def attn_back(
    low_t, dmid_t, d_query, att, own, cosine, sine, hidden, mid, dmid, scale, terms, hid, slice_d, slice_q,
    fs, ctx, ten, ident,
):
    rows = low_t.shape[2]
    t_rows, width = mid.shape
    chips = fs // 2
    heads = d_query.shape[1]
    count, tail = own.shape[2:]
    lanes = -(-rows // 128) * 128
    both = [
        ((rows, heads + tail), half_type),
        ((rows, att.shape[1]), half_type),
        ((8, lanes), single),
    ]
    sends = (
        2 * (ctx * (ten - 1) + 2 * ctx)
        + 4 * (ten - 1)
        + 3 * (chips + (chips - 1) * ctx + 2 * ctx)
    )
    dma = pltpu.SemaphoreType.DMA
    shape = jax.ShapeDtypeStruct
    return pl.pallas_call(
        functools.partial(attn_kernel, fs, ctx, ten),
        out_shape=[
            shape((rows, heads), single),
            shape((rows, att.shape[1]), single),
            shape((8, lanes), single),
            shape((rows, ten * tail), single),
            shape((ten, 2, t_rows, width), half_type),
        ],
        in_specs=[VMEM] * 13 + [ANY] * 2,
        out_specs=[VMEM] * 5,
        scratch_shapes=[pltpu.VMEM((fs, ctx, *b), t) for b, t in both]
        + [pltpu.VMEM((chips, ctx, *b), t) for b, t in both]
        + [pltpu.VMEM((chips - 1, ctx, *b), t) for b, t in both]
        + [pltpu.VMEM((ctx + 1, *b), t) for b, t in both]
        + [
            pltpu.VMEM((ctx, ten, t_rows, width), half_type),
            pltpu.VMEM((ten - 1, ctx, t_rows, width), half_type),
            pltpu.VMEM((ctx + 1, t_rows, width), half_type),
            pltpu.VMEM((ten - 1, ctx, count, tail), half_type),
            pltpu.VMEM((ctx + 1, count, tail), half_type),
            pltpu.VMEM((count, tail), single),
            pltpu.VMEM((count, heads + tail), half_type),
            pltpu.VMEM((1, ten, t_rows, width), half_type),
            pltpu.VMEM((ten, t_rows, width), half_type),
            pltpu.VMEM((2, 2, ctx, *slice_d.shape[2:]), half_type),
            pltpu.VMEM((2, 2, ctx, *slice_q.shape[2:]), half_type),
            pltpu.VMEM((ten, rows, tail), half_type),
            pltpu.VMEM((ten, 8, lanes), single),
            pltpu.VMEM((t_rows, width), single),
            pltpu.VMEM(own.shape, half_type),
            dma((2,)),
            dma((sends,)),
            dma((3, chips)),
            dma((3, chips - 1, ctx)),
            dma((3, ctx + 1)),
            dma((ten - 1, ctx)),
            dma((ctx + 1,)),
            dma((ten - 1, ctx)),
            dma((ctx + 1,)),
            dma((ten,)),
            dma((3, ten)),
        ],
        compiler_params=pltpu.CompilerParams(
            collective_id=ident, has_side_effects=True, vmem_limit_bytes=VMEM_ALL
        ),
        name=f"attn_back_{ident}",
    )(low_t, dmid_t, d_query, att, own, cosine, sine, hidden, mid, dmid, scale, terms, hid, slice_d, slice_q)


def on_device(hidden_in, cotangent, segment_ids, positions, *params):
    masters, firsts, seconds = params[:8], params[8:16], params[16:]
    (
        attn_scale,
        query_weight,
        keyval_weight,
        output_weight,
        mlp_scale,
        gate_weight,
        up_weight,
        down_weight,
    ) = masters
    fs, ctx, ten = (lax.axis_size(name) for name in ("fsdp", "context", "tensor"))
    x = lax.axis_index("tensor")
    context_index = lax.axis_index("context")
    block, width = hidden_in.shape[1:]
    rows = query_weight.shape[0]
    half_rows = block // ten
    heads_width = query_weight.shape[1]
    heads_here = heads_width // HD
    hidden = hidden_in[0]
    cot = cotangent[0]
    hidden_half = lax.dynamic_slice_in_dim(hidden, x * half_rows, half_rows, 0)
    cot_half = lax.dynamic_slice_in_dim(cot, x * half_rows, half_rows, 0)
    is_key = x == 0

    qkv_block = jnp.concatenate(
        [
            cast(query_weight),
            cast(lax.dynamic_slice_in_dim(keyval_weight, x * HD, HD, 1)),
        ],
        axis=1,
    )
    lanes = -(-max(rows, block) // 128) * 128
    wide = [
        jnp.pad(v, (0, lanes - v.shape[0]))
        for v in (attn_scale, mlp_scale, segment_ids[0].astype(single))
    ]
    small = jnp.stack(wide + [jnp.zeros((lanes,), single)] * 5)
    small_all, qkv_all, out_all, dy_all, part_p, part_d = spread(
        [small, qkv_block, cast(output_weight.T)],
        cast(cot_half),
        [gate_weight, up_weight, down_weight.T],
        fs,
        ctx,
        ten,
        1,
    )
    scale_one = cast(small_all[:, :, 0, :rows].reshape(-1)).astype(single)
    scale_two = cast(small_all[:, :, 1, :rows].reshape(-1)).astype(single)
    f = lax.axis_index("fsdp")
    seg_all = lax.dynamic_index_in_dim(small_all[:, :, 2, :block], f, 0, False).reshape(-1)
    qkv_full = qkv_all.reshape(width, -1)
    out_full = out_all.reshape(width, -1)

    _, _, low_one = rms_forward(hidden, scale_one)
    qkv = dot(low_one, qkv_full, ((1,), (0,)))
    query = qkv[:, :heads_width].reshape(block, heads_here, HD)
    own = qkv[:, heads_width:]
    cosine, sine = rope_tables(positions[0])
    query_low = cast(rotate(query, cosine[:, None, :], sine[:, None, :]) * HD ** (-0.5))
    own_low = cast(jnp.where(is_key, rotate(own, cosine, sine), own))
    keyval_all = tokens_to_all(own_low, ctx, ten, 2).reshape(ctx, ten, block, HD)
    keys_all = keyval_all[:, 0].reshape(-1, HD)
    values_all = keyval_all[:, 1].reshape(-1, HD)
    rows_index = context_index * block + jnp.arange(block, dtype=jnp.int32)
    cols_index = jnp.arange(keys_all.shape[0], dtype=jnp.int32)
    allowed = (rows_index[:, None] >= cols_index[None, :]) & (
        segment_ids[0].astype(single)[:, None] == seg_all[None, :]
    )
    scores = jnp.einsum("bhd,jd->hbj", query_low, keys_all, preferred_element_type=single)
    masked = jnp.where(allowed, scores, masked_value)
    top = jnp.max(masked, axis=-1, keepdims=True)
    total = jnp.sum(jnp.where(allowed, jnp.exp(masked - top), 0.0), axis=-1, keepdims=True)
    lse = top + jnp.log(total)
    prob = jnp.where(allowed, jnp.exp(masked - lse), 0.0)
    prob_low = cast(prob)
    att_low = cast(
        jnp.einsum("hbj,jd->bhd", prob_low, values_all, preferred_element_type=single)
    )
    att_flat = att_low.reshape(block, heads_width)
    attn_part = dot(att_flat, out_full, ((1,), (1,)))
    slice_p, slice_d, hid, dpair, low_t, dy_t, mid_half, _ = mlp_forward(
        cast(attn_part).reshape(ten, half_rows, width),
        hidden_half,
        scale_two[None],
        dy_all,
        part_p,
        part_d,
        fs,
        ctx,
        ten,
        4,
    )
    dmid_half, dmid_low, terms_two, part_p, part_d = mlp_back(
        low_t, dy_t, hid, dpair, mid_half, cot_half, scale_two[None], slice_p, fs, ctx, ten, 5
    )

    dmid_low = dmid_low.reshape(block, width)
    datt_low = cast(dot(dmid_low, out_full, ((1,), (0,)))).reshape(block, heads_here, HD)
    delta = jnp.einsum("bhd,bhd->hb", datt_low, att_low, preferred_element_type=single)
    dprob = jnp.einsum("bhd,jd->hbj", datt_low, values_all, preferred_element_type=single)
    dscore_low = cast(prob * (dprob - delta[..., None]))
    dquery = jnp.einsum("hbj,jd->bhd", dscore_low, keys_all, preferred_element_type=single)
    dkey_part = jnp.einsum("hbj,bhd->jd", dscore_low, query_low, preferred_element_type=single)
    dvalue_part = jnp.einsum("hbj,bhd->jd", prob_low, datt_low, preferred_element_type=single)
    own_part = jnp.stack(
        [cast(part).reshape(ctx, block, HD) for part in (dkey_part, dvalue_part)], axis=1
    )
    dquery_low = cast(
        unrotate(dquery, cosine[:, None, :], sine[:, None, :]) * HD ** (-0.5)
    ).reshape(block, heads_width)
    row_blocks = (fs, ctx, rows, -1)
    grad_wq, grad_wo, grad_s, grad_wkv, outs = attn_back(
        low_one.T.reshape(row_blocks),
        dmid_low.T.reshape(row_blocks),
        dquery_low,
        att_flat,
        own_part,
        cosine,
        sine,
        hidden_half,
        mid_half,
        dmid_half,
        scale_one[None],
        terms_two,
        hid,
        slice_d,
        qkv_all,
        fs,
        ctx,
        ten,
        9,
    )
    outs = outs.transpose(1, 0, 2, 3).reshape(2, 1, block, width).astype(single)

    grads = (grad_s[0, :rows], grad_wq, grad_wkv, grad_wo.T, grad_s[1, :rows])
    results = [
        (grad, *adamw(weight, grad, first, second))
        for weight, grad, first, second in zip(masters, grads, firsts, seconds)
    ]
    results += [
        update(part_p, 0, gate_weight, firsts[5], seconds[5], 5),
        update(part_p, 1, up_weight, firsts[6], seconds[6], 6),
        [v.T for v in update(part_d, 0, down_weight.T, firsts[7].T, seconds[7].T, 7)],
    ]
    return (
        outs[0],
        outs[1],
        *(entry[0] for entry in results),
        *(entry[1] for entry in results),
        *(entry[2] for entry in results),
        *(entry[3] for entry in results),
    )


def solution(mesh):
    both = ("fsdp", "context")
    tokens = P("fsdp", "context", None)
    weights = (
        P(both),
        P(both, "tensor"),
        P(both, None),
        P("tensor", both),
        P(both),
        P(both, "tensor"),
        P(both, "tensor"),
        P("tensor", both),
    )
    return jax.shard_map(
        on_device,
        mesh=mesh,
        in_specs=(tokens, tokens, P("fsdp", "context"), P("fsdp", "context"), *(weights * 3)),
        out_specs=(tokens, tokens, *(weights * 4)),
        check_vma=False,
    )
```

time: 782 us -> 639 us (0.82)
  matrix products: 64.4 us -> 17.2 us
  local copies, waits for them, and re-layouts: 62.1 us -> 20.9 us
  other arithmetic: 55.9 us -> 19.5 us
  Pallas kernels: 588 us -> 575 us
    dot_general x10 -> x3, matrix products: 58.9 us -> 14.7 us  [dot(): lax.dot_general(a, b, (dims, ((), ())), preferred_element_type=single)]
    sub x8 -> x5, other arithmetic: 30.5 us -> 7.38 us  [adamw(): weight - learn_rate * (update + decay_rate * weight)]
    reshape x7 -> x1, local copies, waits for them, and re-layouts: 17.1 us -> 1.08 us  [on_device(): dmid_low = dmid_low.reshape(block, width)]
    convert_element_type x4 -> x2, local copies, waits for them, and re-layouts: 10.5 us -> 1.39 us  [the longest x1 0.69 us: on_device(): scale_two = cast(small_all[:, :, 1, :rows].reshape(-1)).astype(single)]
    pallas_call x8 -> x7, Pallas kernels: 559 us -> 552 us  [the longest x1 151 us: mlp_back(): pl.pallas_call(functools.partial(back_kernel, fs, ctx, ten), out_shape=[s...]
where the time goes in v2:
time: 639 us; the launch traced here: 634 us
  Pallas kernels  575 us (90%)
  local copies, waits for them, and re-layouts  20.9 us (3%)
  other arithmetic  19.5 us (3%)
  matrix products  17.2 us (3%)
    pallas_call x1, Pallas kernels, mlp_back(): pl.pallas_call(functools.partial(back_kernel, fs, ctx, ten), out_shape=[s...  151 us
    pallas_call x1, Pallas kernels, attn_back(): pl.pallas_call(functools.partial(attn_kernel, fs, ctx, ten), out_shape=[s...  145 us
    pallas_call x1, Pallas kernels, mlp_forward(): pl.pallas_call(functools.partial(forward_kernel, fs, ctx, ten), out_shape...  141 us
    pallas_call x1, Pallas kernels, spread(): pl.pallas_call(functools.partial(first_kernel, fs, ctx, ten, count), out_...  85.5 us
    pallas_call x3, Pallas kernels, update(): pl.pallas_call(functools.partial(update_kernel, at), grid=(rows // step,)...  29.2 us
    pallas_call x1, Pallas kernels, tokens_to_all(): pl.pallas_call(functools.partial(tokens_kernel, ctx, ten), out_shape=jax....  22.4 us
    dot_general x3, matrix products, dot(): lax.dot_general(a, b, (dims, ((), ())), preferred_element_type=single)  14.7 us

profile of v2, /device:TPU:8, one launch (start us, length us, event | category | flops | bytes accessed | tf_op | source)
XLA Modules:
  0.0 634.2 jit_solution(3302727594119995160)
XLA Ops:
  0.7 2.6 fusion.43
  7.1 85.5 %spread_1.1 = (f32[4,4,8,256]{3,2,1,0:T(8,128)}, bf16[4,4,160,1536]{3,2,1,0:T(8,128)(2,1)}, bf16[4,4,160,1280]{3,2,1,0:T(8,128)(2,1)}, bf16[4,2,64,2560]{3,2,1,0...) custom-call(f32[8,256]{1,0:T(8,128)} %stack.22.refs_0_, ...), custom_call_target="tpu_custom_call" | custom-call | tf_op jit(solution)/shard_map/spread_1/pallas_call | solution.py:296
  92.7 1.8 convert_reduce_fusion
  94.5 1.5 fusion.4
  96.1 4.5 fusion.13
  101.6 22.4 %tokens_2.1 = bf16[4,2,128,256]{3,2,1,0:T(8,128)(2,1)} custom-call(bf16[128,256]{1,0:T(8,128)(2,1)} %fusion.23.src), custom_call_target="tpu_custom_call" | custom-call | tf_op jit(solution)/shard_map/tokens_2/pallas_call | solution.py:176
  128.9 6.1 convolution_convert_fusion
  135.7 141.4 %mlp_forward_4.1 = (bf16[4,4,160,1920]{3,2,1,0:T(8,128)(2,1)}, bf16[4,4,160,960]{3,2,1,0:T(8,128)(2,1)}, bf16[512,960]{1,0:T(8,128)(2,1)}, bf16[512,1920]{1,0:T(...) custom-call(bf16[2,64,2560]{2,1,0:T(8,128)(2,1)} %bitcast.120, ...), custom_call_target="tpu_custom_call" | custom-call | tf_op jit(solution)/shard_map/mlp_forward_4/pallas_call | solution.py:532
  277.1 150.8 %mlp_back_5.1 = (f32[64,2560]{1,0:T(8,128)}, bf16[2,64,2560]{2,1,0:T(8,128)(2,1)}, f32[1,2560]{1,0:T(1,128)}, bf16[4,160,1920]{2,1,0:T(8,128)(2,1)}, bf16[4,160,960]{2,1,0:T(8,128)(2,1)}) custom-call(bf16[4,4,160,512]{3,2,1,0:T(8,128)(2,1)} %get-tuple-element.75.refs_0_, bf16[4,4,160,512]{3,2,1,0:T(8,128)(2,1)} %get-tuple-element.76.refs_1_, ...), custom_call_target="tpu_custom_call" | custom-call | tf_op jit(solution)/shard_map/mlp_back_5/pallas_call | solution.py:703
  428.0 4.1 convolution_convert_fusion.1
  437.9 1.1 copy.81
  440.1 1.1 copy.75
  441.9 145.2 %attn_back_9.1 = (f32[160,1280]{1,0:T(8,128)}, f32[160,1280]{1,0:T(8,128)}, f32[8,256]{1,0:T(8,128)}, f32[160,512]{1,0:T(8,128)}, bf16[2,2,64,2560]{3,2,1,0:T(8,128)(2,1)}) custom-call(bf16[4,4,160,128]{3,2,1,0:T(8,128)(2,1)} %bitcast.124, bf16[4,4,160,128]{3,2,1,0:T(8,128)(2,1)} %bitcast.123, bf16[128,1280]{1,0:T(8,128)(2,1)} %copy.89.refs_2_, ...), custom_call_target="tpu_custom_call" | custom-call | tf_op jit(solution)/shard_map/attn_back_9/pallas_call | solution.py:947
  587.1 1.6 convert_bitcast_fusion
  588.8 1.7 fusion.44
  591.6 1.8 multiply_subtract_fusion.1
  594.3 1.8 multiply_subtract_fusion
  596.2 1.1 multiply_subtract_fusion.2
  597.3 9.5 %update_7.1 = (f32[160,3840]{1,0:T(8,128)}, f32[160,3840]{1,0:T(8,128)}, f32[160,3840]{1,0:T(8,128)}, f32[160,3840]{1,0:T(8,128)}) custom-call(bf16[4,160,960]{2,1,0:T(8,128)(2,1)} %get-tuple-element.93.parts, f32[160,3840]{1,0:T(8,128)} %bitcast.116, f32[160,3840]{1,0:T(8,128)} %bitcast.126, f32[160,3840]{1,0:T(8,128)} %bitcast.127), custom_call_target="tpu_custom_call" | custom-call | tf_op jit(solution)/shard_map/update_7/pallas_call | solution.py:755
  606.9 9.8 %update_5.1 = (f32[160,3840]{1,0:T(8,128)}, f32[160,3840]{1,0:T(8,128)}, f32[160,3840]{1,0:T(8,128)}, f32[160,3840]{1,0:T(8,128)}) custom-call(bf16[4,160,1920]{2,1,0:T(8,128)(2,1)} %get-tuple-element.90.parts, f32[160,3840]{1,0:T(8,128)} %weight.2, f32[160,3840]{1,0:T(8,128)} %first.2, f32[160,3840]{1,0:T(8,128)} %second.2), custom_call_target="tpu_custom_call" | custom-call | tf_op jit(solution)/shard_map/update_5/pallas_call | solution.py:755
  616.6 9.9 %update_6.1 = (f32[160,3840]{1,0:T(8,128)}, f32[160,3840]{1,0:T(8,128)}, f32[160,3840]{1,0:T(8,128)}, f32[160,3840]{1,0:T(8,128)}) custom-call(bf16[4,160,1920]{2,1,0:T(8,128)(2,1)} %get-tuple-element.90.parts, f32[160,3840]{1,0:T(8,128)} %weight.3, f32[160,3840]{1,0:T(8,128)} %first.3, f32[160,3840]{1,0:T(8,128)} %second.3), custom_call_target="tpu_custom_call" | custom-call | tf_op jit(solution)/shard_map/update_6/pallas_call | solution.py:755
  627.4 1.3 multiply_subtract_fusion.7
  628.7 1.3 multiply_subtract_fusion.6
  630.0 2.1 copy.114
  (155 shorter events, 22.1 us)
Async XLA Ops:
  0.7 3.6 copy-start.4
  3.3 3.0 copy-start.6
  92.6 3.4 copy-start
  94.5 6.0 copy-start.37
  96.1 4.5 copy-start.46
  96.1 4.5 copy-start.51
  125.1 2.3 copy-start.14
  125.1 3.0 copy-start.35
  128.2 6.9 %copy-start.40 = (f32[5,128]{1,0:T(8,128)}, f32[5,128]{1,0:T(8,128)S(1)}, u32[]{:S(2)}) copy-start(f32[5,128]{1,0:T(8,128)S(1)} %log_add_fusion) | copy-start | bytes 7684
  128.9 6.1 copy-start.11
  427.9 4.4 copy-start.12
  427.9 4.5 copy-start.31
  428.0 4.5 copy-start.36
  437.0 2.9 copy-start.1
  437.0 2.9 copy-start.38
  437.0 2.9 copy-start.47
  588.7 2.6 copy-start.26
  588.8 2.8 copy-start.27
  591.6 2.5 copy-start.28
  591.6 2.8 copy-start.29
  626.6 5.5 copy-start.17
  626.6 6.2 copy-start.9
  627.4 6.3 copy-start.44
  627.4 6.3 copy-start.45
  (28 other events, 42.9 us)

commit v3 on v2

--- a/solution.py
+++ b/solution.py
@@ -318,42 +318,36 @@
     )(*blocks, tokens, *weights)
 
 
-def line_sum(z, ctx, owner, gathered, mine, slots, sem, out, kind, done):
-    @pl.when(z == owner)
-    def _():
-        done(gathered())
-
-    for toward, at, edge, past in (
-        ({"context": z + 1}, owner + 1, z == 0, z < owner),
-        ({"context": z - 1}, owner, z == ctx - 1, z > owner),
-    ):
-
-        @pl.when(jnp.logical_and(past, edge))
-        def _():
-            mine[...] = kind(gathered())
-
-        @pl.when(jnp.logical_and(past, jnp.logical_not(edge)))
-        def _():
-            arrived(slots.at[at], sem.at[at], toward)
-            mine[...] = kind(gathered() + slots[at].astype(single))
-
-        out.push(mine, slots.at[at], sem.at[at], toward, past)
-
-
-def line_end(z, ctx, slots, sem, add):
-    for at, edge in ((z + 1, z == 0), (z, z == ctx - 1)):
-
-        @pl.when(jnp.logical_not(edge))
-        def _():
-            arrived(slots.at[at], sem.at[at], {"context": z})
-            add(slots[at].astype(single))
-
-
-def ends_first(ctx):
-    order = []
-    for k in range((ctx + 1) // 2):
-        order += [ctx - 1 - k] + ([k] if k != ctx - 1 - k else [])
-    return order
+def flip(k, bit):
+    return k + bit - 2 * bit * lax.rem(lax.div(k, bit), 2)
+
+
+def halving(z, ctx):
+    sends, seen, base, bit = [], [], 0, 1
+    while bit < ctx:
+        count = ctx // (2 * bit)
+        for u in range(count):
+            owner = flip(z, bit) - 2 * bit * lax.div(z, 2 * bit) + 2 * bit * u
+            sends.append((owner, flip(z, bit), base + u, [at + lax.div(owner, d) for at, d in seen]))
+        seen.append((base, 2 * bit))
+        base, bit = base + count, 2 * bit
+    return sends, [at + lax.div(z, d) for at, d in seen]
+
+
+def doubling(z, ctx):
+    steps, held, bit = [], [z], ctx // 2
+    while bit:
+        got = [flip(k, bit) for k in held]
+        steps.append((flip(z, bit), list(held), got))
+        held, bit = held + got, bit // 2
+    return steps
+
+
+def collect(total, slots, sem, places, peer):
+    for at in places:
+        arrived(slots.at[at], sem.at[at], peer)
+        total = total + slots[at].astype(single)
+    return total
 
 
 def chip_tiles(weight, held, load, use):
@@ -393,7 +387,7 @@
     back = [lax.rem(z + ctx - d, ctx) for d in range(ctx)]
     greet([{"context": k} for k in around[1:]] + across + [twin] + beside)
     out = Sends(send)
-    parts, slices, recvs = (part_d, part_p), (slice_d, slice_p), (recv_d, recv_p)
+    parts, slices, recvs = (part_p, part_d), (slice_p, slice_d), (recv_p, recv_d)
     for peer in beside:
         out.push(attn.at[peer["tensor"]], take.at[x], recv_x.at[x], peer)
 
@@ -440,22 +434,30 @@
     inverse = lax.rsqrt(jnp.mean(total * total, axis=-1, keepdims=True) + norm_eps)
     low_all[z, x] = cast(total * inverse * (1.0 + scale[...]))
     mine = low_all.at[z, x]
-    out.push(mine, mine, recv_t.at[z, x], {"context": z + 1}, z + 1 < ctx)
-    out.push(mine, mine, recv_t.at[z, x], {"context": z - 1}, z >= 1)
+    later = [(0, d) for d in range(2, ctx)] + [(1, d) for d in range(1, ctx)]
+    early = [d for d in range(1, ctx)]
+    steps = doubling(z, ctx)
+    for partner, _, _ in steps:
+        out.push(mine, mine, recv_t.at[z, x], {"context": partner})
     for peer in beside:
         out.push(mine, mine, recv_t.at[z, x], peer)
-    later = [(0, d) for d in range(2, ctx)] + [(1, d) for d in range(1, ctx)]
-    for step, (source, exists, onward, more) in enumerate(line_steps(z, ctx)):
-        if step % 2 == 0:
-            to_context(*later.pop(0))
-            from_context(0, step // 2 + 1)
-        here, sem = low_all.at[source, x], recv_t.at[source, x]
-        under((exists,), lambda: arrived(here, sem, twin))
-        out.push(here, here, sem, {"context": onward}, exists, more)
-        for peer in beside:
-            out.push(here, here, sem, peer, exists)
-    for more in later:
-        to_context(*more)
+    to_context(*later.pop(0))
+    for step, (partner, _, got) in enumerate(steps):
+        for source in got:
+            here, sem = low_all.at[source, x], recv_t.at[source, x]
+            arrived(here, sem, twin)
+            for further, _, _ in steps[step + 1 :]:
+                out.push(here, here, sem, {"context": further})
+            for peer in beside:
+                out.push(here, here, sem, peer)
+            if early:
+                from_context(0, early.pop(0))
+            if later:
+                to_context(*later.pop(0))
+    while later:
+        to_context(*later.pop(0))
+    while early:
+        from_context(0, early.pop(0))
 
     def turned(dst, src):
         for j in range(fs * ctx):
@@ -490,14 +492,14 @@
             arrived(low_all.at[source, other], recv_t.at[source, other], twin)
     from_twin(0)
     keeps[0].wait()
-    product(slice_d, held_d, dy, sums_d)
+    turned(low_t, low_all)
     for d in range(2, ctx):
         from_context(1, d)
-    turned(low_t, low_all)
+    product(slice_p, held_p, low_all, sums_p)
     from_chips(1)
     from_twin(1)
     keeps[1].wait()
-    product(slice_p, held_p, low_all, sums_p)
+    product(slice_d, held_d, dy, sums_d)
     low[...] = low_all[z, x]
     root = (2.0 / jnp.pi) ** 0.5
     part = count // ctx
@@ -585,17 +587,19 @@
             )
 
 
-def token_step(owner, source, first, recv, slots, sems, z, x, ctx, out, done):
+def token_sum(owner, places, source, first, recv, slots, sem, x):
+    total = source[owner, x].astype(single)
     for k in range(first.shape[0]):
         arrived(first.at[k, owner], recv.at[k, owner], {"tensor": x})
-
-    def gathered():
-        total = source[owner, x].astype(single)
-        for k in range(first.shape[0]):
-            total = total + first[k, owner].astype(single)
-        return total
-
-    line_sum(z, ctx, owner, gathered, source.at[owner, x], slots, sems, out, cast, done)
+        total = total + first[k, owner].astype(single)
+    return collect(total, slots, sem, places, {"tensor": x})
+
+
+def token_send(send, source, first, recv, slots, sem, x, out):
+    owner, partner, slot, places = send
+    mine = source.at[owner, x]
+    mine[...] = cast(token_sum(owner, places, source, first, recv, slots, sem, x))
+    out.push(mine, slots.at[slot], sem.at[slot], {"context": partner})
 
 
 def back_kernel(fs, ctx, ten, *refs):
@@ -650,24 +654,19 @@
             keep.start()
             keeps.append(keep)
 
-    def keep_sum(v):
-        dmid[...] = v
-
-    def add_sum(v):
-        dmid[...] += v
-
-    token_products(source, dpair, slice_p, held, load)
-    ends = ends_first(ctx)
-    token_start(source, first, recv_tx, out, beside, ends)
+    sends, own_slots = halving(z, ctx)
+    owners = [send[0] for send in sends] + [z]
     products(0)
     over_chips(0)
+    token_products(source, dpair, slice_p, held, load)
+    token_start(source, first, recv_tx, out, beside, owners)
     products(1)
     over_chips(1)
-    for d, owner in enumerate(ends):
-        token_step(owner, source, first, recv_tx, line, recv_t, z, x, ctx, out, keep_sum)
+    for d, send_z in enumerate(sends):
+        token_send(send_z, source, first, recv_tx, line, recv_t, x, out)
         over_context(0, d)
-    line_end(z, ctx, line, recv_t, add_sum)
-    dnorm = dmid[...]
+    over_context(0, ctx - 1)
+    dnorm = token_sum(z, own_slots, source, first, recv_tx, line, recv_t, x)
     values = mid[...]
     inverse = lax.rsqrt(jnp.mean(values * values, axis=-1, keepdims=True) + norm_eps)
     normed = values * inverse
@@ -736,41 +735,47 @@
     )(low_t, dy_t, hid, dpair, mid, cot, scale, slice_p)
 
 
-def update_kernel(at, parts, weight, first, second, grad_out, weight_out, first_out, second_out):
-    columns = weight.shape[1] // parts.shape[0]
-    for k in range(parts.shape[0]):
-        grad = parts[k, :, at * columns : (at + 1) * columns].astype(single)
-        here = (slice(None), slice(k * columns, (k + 1) * columns))
-        grad_out[here] = grad
-        weight_out[here], first_out[here], second_out[here] = adamw(
-            weight[here], grad, first[here], second[here]
-        )
-
-
-def update(parts, at, weight, first, second, ident):
+def update_kernel(parts, *refs):
+    count = len(refs) // 7
+    for w in range(count):
+        weight, first, second = refs[3 * w : 3 * w + 3]
+        outs = refs[3 * count + 4 * w : 3 * count + 4 * w + 4]
+        columns = weight.shape[1] // parts.shape[0]
+        for k in range(parts.shape[0]):
+            grad = parts[k, :, w * columns : (w + 1) * columns].astype(single)
+            here = (slice(None), slice(k * columns, (k + 1) * columns))
+            values = (grad, *adamw(weight[here], grad, first[here], second[here]))
+            for out, value in zip(outs, values):
+                out[here] = value
+
+
+def update(parts, weights, ident):
     ctx, rows, columns = parts.shape
     step = 32 if rows % 32 == 0 else 8
-    spec = pl.BlockSpec((step, weight.shape[1]), lambda i: (i, 0))
+    wide = weights[0][0].shape[1]
+    spec = pl.BlockSpec((step, wide), lambda i: (i, 0))
     part = pl.BlockSpec((ctx, step, columns), lambda i: (0, i, 0))
-    return pl.pallas_call(
-        functools.partial(update_kernel, at),
+    count = len(weights)
+    outs = pl.pallas_call(
+        update_kernel,
         grid=(rows // step,),
-        out_shape=[jax.ShapeDtypeStruct(weight.shape, single)] * 4,
-        in_specs=[part, spec, spec, spec],
-        out_specs=[spec] * 4,
+        out_shape=[jax.ShapeDtypeStruct((rows, wide), single)] * (4 * count),
+        in_specs=[part] + [spec] * (3 * count),
+        out_specs=[spec] * (4 * count),
         compiler_params=pltpu.CompilerParams(vmem_limit_bytes=VMEM_ALL),
         name=f"update_{ident}",
-    )(parts, weight, first, second)
+    )(parts, *(v for group in weights for v in group))
+    return [outs[4 * w : 4 * w + 4] for w in range(count)]
 
 
 def attn_kernel(fs, ctx, ten, *refs):
     low_t, dmid_t, d_query, att, own, cosine, sine, hidden, mid, dmid, scale, terms = refs[:12]
     hid, slice_d, slice_q = refs[12:15]
     out_q, out_o, out_s, out_kv, tokens = refs[15:20]
-    dws, nears, fars, lines = refs[20:23], refs[23:26], refs[26:29], refs[29:32]
-    source, first, line, first_k, line_k, sum_k, d_qkv, dnorm, take = refs[32:41]
-    held_d, held_q, tail, pool, total_m, own_sums = refs[41:47]
-    load, send, recv_c, recv_y, recv_z, recv_tx, recv_t, recv_kx, recv_k, recv_n, recv_x = refs[47:]
+    dws, nears, fars, lines = refs[20:25], refs[25:30], refs[30:35], refs[35:40]
+    source, first, line, first_k, line_k, d_qkv, dnorm, take = refs[40:48]
+    held_d, held_q, tail, pool, own_sums = refs[48:53]
+    load, send, recv_c, recv_y, recv_z, recv_tx, recv_t, recv_kx, recv_k, recv_n, recv_x = refs[53:]
     f, y, core, twin, across = fsdp_place(fs)
     z, x = lax.axis_index("context"), lax.axis_index("tensor")
     chips = fs // 2
@@ -778,22 +783,29 @@
     beside = [lax.rem(x + d, ten) for d in range(1, ten)]
     rows_of = [lax.rem(y + d, chips) for d in range(chips)]
     chip_order = rows_of[1:] + rows_of[:1]
-    nxt, prv = lax.rem(z + 1, ctx), lax.rem(z + ctx - 1, ctx)
-    greet([{"context": nxt}, {"context": prv}] + across + [twin] + [{"tensor": k} for k in beside])
+    partners = [{"context": partner} for partner, _, _ in doubling(z, ctx)]
+    greet(partners + across + [twin] + [{"tensor": k} for k in beside])
     out = Sends(send)
-    order = ends_first(ctx)
-    kinds = (cast, cast, lambda v: v)
+    sends, own_slots = halving(z, ctx)
+    order = [send_z[0] for send_z in sends] + [z]
+    kinds = (cast, cast, cast, cast, lambda v: v)
     heads = d_query.shape[1]
-    rights = (d_qkv, att)
-    lefts = (low_t, dmid_t)
+    widths = [dw.shape[-1] for dw in dws[:4]]
+    rights = (
+        d_qkv.at[:, : widths[0]],
+        d_qkv.at[:, widths[0] :],
+        att.at[:, : widths[2]],
+        att.at[:, widths[2] :],
+    )
+    lefts = (low_t, low_t, dmid_t, dmid_t)
 
     def start(w):
         for row in chip_order:
             owner = row * 2 + 1 - core
-            if w < 2:
+            if w < 4:
                 fill_product(dws[w], lefts[w], rights[w], owner, ctx)
             out.push(dws[w].at[owner], nears[w].at[row], recv_c.at[w, row], twin)
-        if w < 2:
+        if w < 4:
             for row in chip_order:
                 fill_product(dws[w], lefts[w], rights[w], row * 2 + core, ctx)
 
@@ -805,51 +817,34 @@
                 mine[...] = kinds[w](mine[...].astype(single) + nears[w][row, owner].astype(single))
                 out.push(mine, fars[w].at[k, owner], recv_y.at[w, k, owner], across[k])
 
+    def summed_block(w, owner, places):
+        total = dws[w][f, owner].astype(single) + nears[w][y, owner].astype(single)
+        for k in range(chips - 1):
+            arrived(fars[w].at[k, owner], recv_y.at[w, k, owner], twin)
+            total = total + fars[w][k, owner].astype(single)
+        return collect(total, lines[w], recv_z.at[w], places, twin)
+
     def over_context(w, d):
         if d == 0:
             arrived(nears[w].at[y], recv_c.at[w, y], twin)
-        owner = order[d]
+        owner, partner, slot, places = sends[d]
         mine = dws[w].at[f, owner]
-        for k in range(chips - 1):
-            arrived(fars[w].at[k, owner], recv_y.at[w, k, owner], twin)
-
-        def gathered():
-            total = mine[...].astype(single) + nears[w][y, owner].astype(single)
-            for k in range(chips - 1):
-                total = total + fars[w][k, owner].astype(single)
-            return total
-
-        def done(v):
-            mine[...] = kinds[w](v)
-
-        line_sum(
-            z, ctx, owner, gathered, mine, lines[w], recv_z.at[w], out, kinds[w], done
-        )
+        mine[...] = kinds[w](summed_block(w, owner, places))
+        out.push(mine, lines[w].at[slot], recv_z.at[w, slot], {"context": partner})
 
     def finish(w):
-        def add(v):
-            dws[w][f, z] = kinds[w](dws[w][f, z].astype(single) + v)
-
-        line_end(z, ctx, lines[w], recv_z.at[w], add)
-        return dws[w][f, z]
+        return summed_block(w, z, own_slots)
 
     own_sums[...] = own[...]
     token_start(own_sums, first_k, recv_kx, out, beside, order)
-    start(1)
-    token_products(source, hid, slice_d, held_d, load)
-    token_start(source, first, recv_tx, out, beside, order)
-    over_chips(1)
-
-    def keep_k(v):
-        sum_k[...] = v
-
-    def add_k(v):
-        sum_k[...] += v
-
-    for owner in order:
-        token_step(owner, own_sums, first_k, recv_kx, line_k, recv_k, z, x, ctx, out, keep_k)
-    line_end(z, ctx, line_k, recv_k, add_k)
-    summed = sum_k[...]
+    start(2)
+    over_chips(2)
+    start(3)
+    over_chips(3)
+    for d, send_z in enumerate(sends):
+        token_send(send_z, own_sums, first_k, recv_kx, line_k, recv_k, x, out)
+        over_context(2, d)
+    summed = token_sum(z, own_slots, own_sums, first_k, recv_kx, line_k, recv_k, x)
     half = summed.shape[1] // 2
     a, b = summed[:, :half], summed[:, half:]
     c, s = cosine[...], sine[...]
@@ -857,21 +852,15 @@
     d_qkv[:, :heads] = d_query[...]
     d_qkv[:, heads : heads + half] = cast(jnp.where(is_key, a * c + b * s, a))
     d_qkv[:, heads + half :] = cast(jnp.where(is_key, b * c - a * s, b))
-    start(0)
-    over_chips(0)
     token_products(dnorm, d_qkv, slice_q, held_q, load)
     for other in beside:
         out.push(dnorm.at[0, other], take.at[x], recv_n.at[x], {"tensor": other})
-
-    def keep_m(v):
-        total_m[...] = v
-
-    def add_m(v):
-        total_m[...] += v
-
-    for d, owner in enumerate(order):
-        token_step(owner, source, first, recv_tx, line, recv_t, z, x, ctx, out, keep_m)
-        over_context(1, d)
+    start(0)
+    over_chips(0)
+    token_products(source, hid, slice_d, held_d, load)
+    token_start(source, first, recv_tx, out, beside, order)
+    for d in range(ctx - 1):
+        over_context(3, d)
     dnorm_one = dnorm[0, x].astype(single)
     for other in beside:
         arrived(take.at[other], recv_n.at[other], twin)
@@ -885,33 +874,49 @@
         + inverse * (dnormed - normed * jnp.mean(dnormed * normed, axis=-1, keepdims=True))
     )
     sums = jnp.sum(dnorm_one * normed, axis=0, keepdims=True)
-    dws[2][...] = jnp.zeros_like(dws[2])
+    dws[4][...] = jnp.zeros_like(dws[4])
     for j in range(fs * ctx):
         at = slice(j * rows, (j + 1) * rows)
-        dws[2][j // ctx, j % ctx, 0:1, :rows] = sums[:, at]
-        dws[2][j // ctx, j % ctx, 1:2, :rows] = terms[:, at]
-    start(2)
-    line_end(z, ctx, line, recv_t, add_m)
-    tokens[x, 0] = cast(mid[...] + total_m[...])
+        dws[4][j // ctx, j % ctx, 0:1, :rows] = sums[:, at]
+        dws[4][j // ctx, j % ctx, 1:2, :rows] = terms[:, at]
+    start(4)
+    start(1)
+    over_chips(4)
+    over_chips(1)
+
+    def hand_over(t):
+        for other in beside:
+            out.push(tokens.at[x, t], tokens.at[x, t], recv_x.at[2 + t, x], {"tensor": other})
+
+    hand_over(1)
+    for d, send_z in enumerate(sends):
+        token_send(send_z, source, first, recv_tx, line, recv_t, x, out)
+        over_context(0, d)
+    for d in range(ctx - 1):
+        over_context(4, d)
+    for d in range(ctx - 1):
+        over_context(1, d)
+        if d == 0:
+            tokens[x, 0] = cast(
+                mid[...] + token_sum(z, own_slots, source, first, recv_tx, line, recv_t, x)
+            )
+            hand_over(0)
+    pool[x] = finish(4)
     for other in beside:
-        out.push(tokens.at[x], tokens.at[x], recv_x.at[0, x], {"tensor": other})
-    over_chips(2)
-    for d in range(ctx):
-        over_context(2, d)
-        over_context(0, d)
-    pool[x] = finish(2)
+        out.push(pool.at[x], pool.at[x], recv_x.at[0, x], {"tensor": other})
+    out_o[:, : widths[2]] = finish(2)
+    out_o[:, widths[2] :] = finish(3)
+    out_q[:, : widths[0]] = finish(0)
+    grad = finish(1)
+    out_q[:, widths[0] :] = grad[:, : heads - widths[0]]
+    tail[x] = cast(grad[:, heads - widths[0] :])
     for other in beside:
-        out.push(pool.at[x], pool.at[x], recv_x.at[1, x], {"tensor": other})
-    grad = finish(0)
-    out_q[...] = grad[:, :heads].astype(single)
-    tail[x] = grad[:, heads:]
+        out.push(tail.at[x], tail.at[x], recv_x.at[1, x], {"tensor": other})
     for other in beside:
-        out.push(tail.at[x], tail.at[x], recv_x.at[2, x], {"tensor": other})
-    out_o[...] = finish(1).astype(single)
-    for other in beside:
-        arrived(tokens.at[other], recv_x.at[0, other], twin)
-        arrived(pool.at[other], recv_x.at[1, other], twin)
-        arrived(tail.at[other], recv_x.at[2, other], twin)
+        arrived(pool.at[other], recv_x.at[0, other], twin)
+        arrived(tail.at[other], recv_x.at[1, other], twin)
+        for t in range(2):
+            arrived(tokens.at[other, t], recv_x.at[2 + t, other], twin)
     total = pool[0]
     for k in range(1, ten):
         total = total + pool[k]
@@ -932,15 +937,18 @@
     heads = d_query.shape[1]
     count, tail = own.shape[2:]
     lanes = -(-rows // 128) * 128
+    cuts = [-(-total // 256) * 128 for total in (heads + tail, att.shape[1])]
     both = [
-        ((rows, heads + tail), half_type),
-        ((rows, att.shape[1]), half_type),
+        ((rows, cuts[0]), half_type),
+        ((rows, heads + tail - cuts[0]), half_type),
+        ((rows, cuts[1]), half_type),
+        ((rows, att.shape[1] - cuts[1]), half_type),
         ((8, lanes), single),
     ]
     sends = (
         2 * (ctx * (ten - 1) + 2 * ctx)
-        + 4 * (ten - 1)
-        + 3 * (chips + (chips - 1) * ctx + 2 * ctx)
+        + 5 * (ten - 1)
+        + 5 * (chips + (chips - 1) * ctx + 2 * ctx)
     )
     dma = pltpu.SemaphoreType.DMA
     shape = jax.ShapeDtypeStruct
@@ -965,7 +973,6 @@
             pltpu.VMEM((ctx + 1, t_rows, width), half_type),
             pltpu.VMEM((ten - 1, ctx, count, tail), half_type),
             pltpu.VMEM((ctx + 1, count, tail), half_type),
-            pltpu.VMEM((count, tail), single),
             pltpu.VMEM((count, heads + tail), half_type),
             pltpu.VMEM((1, ten, t_rows, width), half_type),
             pltpu.VMEM((ten, t_rows, width), half_type),
@@ -973,19 +980,18 @@
             pltpu.VMEM((2, 2, ctx, *slice_q.shape[2:]), half_type),
             pltpu.VMEM((ten, rows, tail), half_type),
             pltpu.VMEM((ten, 8, lanes), single),
-            pltpu.VMEM((t_rows, width), single),
             pltpu.VMEM(own.shape, half_type),
             dma((2,)),
             dma((sends,)),
-            dma((3, chips)),
-            dma((3, chips - 1, ctx)),
-            dma((3, ctx + 1)),
+            dma((5, chips)),
+            dma((5, chips - 1, ctx)),
+            dma((5, ctx + 1)),
             dma((ten - 1, ctx)),
             dma((ctx + 1,)),
             dma((ten - 1, ctx)),
             dma((ctx + 1,)),
             dma((ten,)),
-            dma((3, ten)),
+            dma((4, ten)),
         ],
         compiler_params=pltpu.CompilerParams(
             collective_id=ident, has_side_effects=True, vmem_limit_bytes=VMEM_ALL
@@ -1135,11 +1141,9 @@
         (grad, *adamw(weight, grad, first, second))
         for weight, grad, first, second in zip(masters, grads, firsts, seconds)
     ]
-    results += [
-        update(part_p, 0, gate_weight, firsts[5], seconds[5], 5),
-        update(part_p, 1, up_weight, firsts[6], seconds[6], 6),
-        [v.T for v in update(part_d, 0, down_weight.T, firsts[7].T, seconds[7].T, 7)],
-    ]
+    groups = list(zip(masters, firsts, seconds))
+    results += update(part_p, groups[5:7], 5)
+    results += [[v.T for v in update(part_d, [[v.T for v in groups[7]]], 7)[0]]]
     return (
         outs[0],
         outs[1],

time: 639 us -> 607 us (0.950)
  Pallas kernels: 575 us -> 540 us
    pallas_call x1, Pallas kernels: 145 us -> 131 us  [attn_back(): pl.pallas_call(functools.partial(attn_kernel, fs, ctx, ten), out_shape=[s...]
    pallas_call x1, Pallas kernels: 141 us -> 132 us  [mlp_forward(): pl.pallas_call(functools.partial(forward_kernel, fs, ctx, ten), out_shape...]
    pallas_call x1, Pallas kernels: 151 us -> 143 us  [mlp_back(): pl.pallas_call(functools.partial(back_kernel, fs, ctx, ten), out_shape=[s...]
    pallas_call x3 -> x2, Pallas kernels: 29.2 us -> 25.5 us  [update(): pl.pallas_call(update_kernel, grid=(rows // step,), out_shape=[jax.ShapeD...]
where the time goes in v3:
time: 607 us; the launch traced here: 599 us
  Pallas kernels  540 us (89%)
  local copies, waits for them, and re-layouts  20.9 us (3%)
  other arithmetic  19.5 us (3%)
  matrix products  17.2 us (3%)
    pallas_call x1, Pallas kernels, mlp_back(): pl.pallas_call(functools.partial(back_kernel, fs, ctx, ten), out_shape=[s...  143 us
    pallas_call x1, Pallas kernels, mlp_forward(): pl.pallas_call(functools.partial(forward_kernel, fs, ctx, ten), out_shape...  132 us
    pallas_call x1, Pallas kernels, attn_back(): pl.pallas_call(functools.partial(attn_kernel, fs, ctx, ten), out_shape=[s...  131 us
    pallas_call x1, Pallas kernels, spread(): pl.pallas_call(functools.partial(first_kernel, fs, ctx, ten, count), out_...  85.5 us
    pallas_call x2, Pallas kernels, update(): pl.pallas_call(update_kernel, grid=(rows // step,), out_shape=[jax.ShapeD...  25.5 us
    pallas_call x1, Pallas kernels, tokens_to_all(): pl.pallas_call(functools.partial(tokens_kernel, ctx, ten), out_shape=jax....  22.4 us
    dot_general x3, matrix products, dot(): lax.dot_general(a, b, (dims, ((), ())), preferred_element_type=single)  14.7 us

profile of v3, /device:TPU:8, one launch (start us, length us, event | category | flops | bytes accessed | tf_op | source)
XLA Modules:
  0.0 598.9 jit_solution(17711858338609989639)
XLA Ops:
  0.7 2.6 fusion.43
  7.1 85.5 %spread_1.1 = (f32[4,4,8,256]{3,2,1,0:T(8,128)}, bf16[4,4,160,1536]{3,2,1,0:T(8,128)(2,1)}, bf16[4,4,160,1280]{3,2,1,0:T(8,128)(2,1)}, bf16[4,2,64,2560]{3,2,1,0...) custom-call(f32[8,256]{1,0:T(8,128)} %stack.22.refs_0_, ...), custom_call_target="tpu_custom_call" | custom-call | tf_op jit(solution)/shard_map/spread_1/pallas_call | solution.py:296
  92.7 1.8 convert_reduce_fusion
  94.5 1.5 fusion.4
  96.1 4.5 fusion.13
  101.6 22.4 %tokens_2.1 = bf16[4,2,128,256]{3,2,1,0:T(8,128)(2,1)} custom-call(bf16[128,256]{1,0:T(8,128)(2,1)} %fusion.23.src), custom_call_target="tpu_custom_call" | custom-call | tf_op jit(solution)/shard_map/tokens_2/pallas_call | solution.py:176
  124.1 1.1 fusion.46
  128.9 6.1 %convolution_convert_fusion = bf16[128,2560]{1,0:T(8,128)(2,1)} fusion(bf16[128,1280]{0,1:T(8,128)(2,1)S(1)} %bitcast.118, bf16[2560,1280]{1,0:T(8,128)(2,1)} %bitcast.113), kind=kOutput, calls=%fused_computation | convolution fusion | flops 839188480 | bytes 7536640 | tf_op jit(solution)/shard_map/dot_general | solution.py:78
  135.7 132.3 %mlp_forward_4.1 = (bf16[4,4,160,1920]{3,2,1,0:T(8,128)(2,1)}, bf16[4,4,160,960]{3,2,1,0:T(8,128)(2,1)}, bf16[512,960]{1,0:T(8,128)(2,1)}, bf16[512,1920]{1,0:T(...) custom-call(bf16[2,64,2560]{2,1,0:T(8,128)(2,1)} %bitcast.120, ...), custom_call_target="tpu_custom_call" | custom-call | tf_op jit(solution)/shard_map/mlp_forward_4/pallas_call | solution.py:534
  268.0 143.1 %mlp_back_5.1 = (f32[64,2560]{1,0:T(8,128)}, bf16[2,64,2560]{2,1,0:T(8,128)(2,1)}, f32[1,2560]{1,0:T(1,128)}, bf16[4,160,1920]{2,1,0:T(8,128)(2,1)}, bf16[4,160,960]{2,1,0:T(8,128)(2,1)}) custom-call(bf16[4,4,160,512]{3,2,1,0:T(8,128)(2,1)} %get-tuple-element.75.refs_0_, bf16[4,4,160,512]{3,2,1,0:T(8,128)(2,1)} %get-tuple-element.76.refs_1_, ...), custom_call_target="tpu_custom_call" | custom-call | tf_op jit(solution)/shard_map/mlp_back_5/pallas_call | solution.py:702
  411.1 16.0 %update_5.1 = (f32[160,3840]{1,0:T(8,128)}, f32[160,3840]{1,0:T(8,128)}, f32[160,3840]{1,0:T(8,128)}, f32[160,3840]{1,0:T(8,128)}, f32[160,3840]{1,0:T(8,128)}, ...) custom-call(bf16[4,160,1920]{2,1,0:T(8,128)(2,1)} %get-tuple-element.90.parts, f32[160,3840]{1,0:T(8,128)} %refs_0_.1, ...), custom_call_target="tpu_custom_call" | custom-call | tf_op jit(solution)/shard_map/update_5/pallas_call | solution.py:759
  427.2 4.2 convolution_convert_fusion.1
  437.1 1.1 copy.81
  439.3 1.1 copy.75
  441.1 130.7 %attn_back_9.1 = (f32[160,1280]{1,0:T(8,128)}, f32[160,1280]{1,0:T(8,128)}, f32[8,256]{1,0:T(8,128)}, f32[160,512]{1,0:T(8,128)}, bf16[2,2,64,2560]{3,2,1,0:T(8,128)(2,1)}) custom-call(bf16[4,4,160,128]{3,2,1,0:T(8,128)(2,1)} %bitcast.124, bf16[4,4,160,128]{3,2,1,0:T(8,128)(2,1)} %bitcast.123, bf16[128,1280]{1,0:T(8,128)(2,1)} %copy.89.refs_2_, ...), custom_call_target="tpu_custom_call" | custom-call | tf_op jit(solution)/shard_map/attn_back_9/pallas_call | solution.py:955
  571.8 1.6 convert_bitcast_fusion
  573.5 1.7 fusion.44
  576.3 1.8 multiply_subtract_fusion.1
  579.1 1.8 multiply_subtract_fusion
  580.9 1.1 multiply_subtract_fusion.2
  582.0 9.5 %update_7.1 = (f32[160,3840]{1,0:T(8,128)}, f32[160,3840]{1,0:T(8,128)}, f32[160,3840]{1,0:T(8,128)}, f32[160,3840]{1,0:T(8,128)}) custom-call(bf16[4,160,960]{2,1,0:T(8,128)(2,1)} %get-tuple-element.93.parts, f32[160,3840]{1,0:T(8,128)} %bitcast.116, f32[160,3840]{1,0:T(8,128)} %bitcast.126, f32[160,3840]{1,0:T(8,128)} %bitcast.127), custom_call_target="tpu_custom_call" | custom-call | tf_op jit(solution)/shard_map/update_7/pallas_call | solution.py:759
  592.4 1.3 multiply_subtract_fusion.7
  593.7 1.3 multiply_subtract_fusion.6
  595.0 2.1 copy.114
  (154 shorter events, 21.1 us)
Async XLA Ops:
  0.7 3.6 copy-start.4
  3.3 3.0 copy-start.6
  92.6 3.4 copy-start
  94.5 6.0 %copy-start.37 = (f32[2560]{0:T(1024)}, f32[2560]{0:T(1024)S(1)}, u32[]{:S(2)}) copy-start(f32[2560]{0:T(1024)S(1)} %add.143) | copy-start | bytes 30724
  96.1 4.5 copy-start.46
  96.1 4.5 copy-start.51
  125.1 2.3 copy-start.14
  125.1 3.0 copy-start.35
  128.2 6.9 %copy-start.40 = (f32[5,128]{1,0:T(8,128)}, f32[5,128]{1,0:T(8,128)S(1)}, u32[]{:S(2)}) copy-start(f32[5,128]{1,0:T(8,128)S(1)} %log_add_fusion) | copy-start | bytes 7684
  128.9 6.1 %copy-start.11 = (bf16[256,5,128]{2,0,1:T(8,128)(2,1)}, bf16[256,5,128]{2,0,1:T(8,128)(2,1)S(1)}, u32[]{:S(2)}) copy-start(bf16[256,5,128]{2,0,1:T(8,128)(2,1)S(1)} %convolution_convert_fusion.2) | copy-start | bytes 983044
  427.2 4.4 copy-start.12
  427.2 4.5 copy-start.31
  427.2 4.5 copy-start.36
  436.2 2.9 copy-start.1
  436.2 2.9 copy-start.38
  436.2 2.9 copy-start.47
  573.5 2.6 copy-start.26
  573.5 2.8 copy-start.27
  576.3 2.5 copy-start.28
  576.3 2.8 copy-start.29
  591.5 5.5 copy-start.17
  591.5 6.2 %copy-start.9 = (f32[160,1280]{1,0:T(8,128)S(1)}, f32[160,1280]{1,0:T(8,128)}, u32[]{:S(2)}) copy-start(f32[160,1280]{1,0:T(8,128)} %get-tuple-element.89) | copy-start | bytes 2457604
  592.4 6.3 %copy-start.44 = (f32[1,160]{1,0:T(1,128)}, f32[1,160]{1,0:T(1,128)S(1)}, u32[]{:S(2)}) copy-start(f32[1,160]{1,0:T(1,128)S(1)} %get-tuple-element.136) | copy-start | bytes 1924
  592.4 6.3 %copy-start.45 = (f32[1,160]{1,0:T(1,128)}, f32[1,160]{1,0:T(1,128)S(1)}, u32[]{:S(2)}) copy-start(f32[1,160]{1,0:T(1,128)S(1)} %get-tuple-element.137) | copy-start | bytes 1924
  (28 other events, 42.9 us)

commit v4 on v3

--- a/solution.py
+++ b/solution.py
@@ -373,14 +373,14 @@
 
 
 def forward_kernel(fs, ctx, ten, *refs):
-    attn, hidden, scale, dy, part_p, part_d = refs[:6]
-    slice_p, slice_d, hid, dpair, low_t, dy_t, mid, low = refs[6:14]
-    low_all, take, held_p, held_d, sums_p, sums_d = refs[14:20]
-    load, local, send, recv_p, recv_d, recv_t, recv_x = refs[20:]
+    att, hidden, scale, dy, part_p, part_d, slice_o = refs[:7]
+    slice_p, slice_d, hid, dpair, low_t, dy_t, mid = refs[7:14]
+    low_all, attn, take, held_o, held_p, held_d, sums_p, sums_d = refs[14:22]
+    load, local, send, recv_p, recv_d, recv_t, recv_x = refs[22:]
     f, y, core, twin, across = fsdp_place(fs)
     z, x = lax.axis_index("context"), lax.axis_index("tensor")
     rows, columns = part_d.shape[1:]
-    width = low.shape[1]
+    width = hidden.shape[1]
     count = hid.shape[0]
     beside = [{"tensor": lax.rem(x + d, ten)} for d in range(1, ten)]
     around = [lax.rem(z + d, ctx) for d in range(ctx)]
@@ -388,8 +388,6 @@
     greet([{"context": k} for k in around[1:]] + across + [twin] + beside)
     out = Sends(send)
     parts, slices, recvs = (part_p, part_d), (slice_p, slice_d), (recv_p, recv_d)
-    for peer in beside:
-        out.push(attn.at[peer["tensor"]], take.at[x], recv_x.at[x], peer)
 
     def block(w, owner, source):
         return slices[w].at[owner, source], recvs[w].at[owner, source]
@@ -425,7 +423,10 @@
             out.push(parts[w].at[z], dst, sem, peer)
         keeps.append(pltpu.make_async_copy(parts[w].at[z], dst, local.at[w]))
         keeps[-1].start()
-    total = hidden[...] + attn[x].astype(single)
+    token_products(attn, att, slice_o, held_o, load)
+    for peer in beside:
+        out.push(attn.at[0, peer["tensor"]], take.at[x], recv_x.at[x], peer)
+    total = hidden[...] + attn[0, x].astype(single)
     for peer in beside:
         other = peer["tensor"]
         arrived(take.at[other], recv_x.at[other], twin)
@@ -442,6 +443,7 @@
     for peer in beside:
         out.push(mine, mine, recv_t.at[z, x], peer)
     to_context(*later.pop(0))
+    from_context(0, early.pop(0))
     for step, (partner, _, got) in enumerate(steps):
         for source in got:
             here, sem = low_all.at[source, x], recv_t.at[source, x]
@@ -500,7 +502,6 @@
     from_twin(1)
     keeps[1].wait()
     product(slice_d, held_d, dy, sums_d)
-    low[...] = low_all[z, x]
     root = (2.0 / jnp.pi) ** 0.5
     part = count // ctx
 
@@ -523,7 +524,7 @@
     out.drain()
 
 
-def mlp_forward(attn, hidden, scale, dy_all, part_p, part_d, fs, ctx, ten, ident):
+def mlp_forward(att, hidden, scale, dy_all, part_p, part_d, slice_o, fs, ctx, ten, ident):
     rows, columns = part_d.shape[1:]
     t_rows, width = hidden.shape
     count = ctx * ten * t_rows
@@ -541,13 +542,14 @@
             shape((fs, ctx, rows, count), half_type),
             shape((fs, ctx, rows, count), half_type),
             shape((t_rows, width), single),
-            shape((t_rows, width), half_type),
         ],
-        in_specs=[VMEM] * 4 + [ANY] * 2,
-        out_specs=[ANY] * 2 + [VMEM] * 6,
+        in_specs=[VMEM] * 4 + [ANY] * 3,
+        out_specs=[ANY] * 2 + [VMEM] * 5,
         scratch_shapes=[
             pltpu.VMEM((ctx, ten, t_rows, width), half_type),
+            pltpu.VMEM((1, ten, t_rows, width), half_type),
             pltpu.VMEM((ten, t_rows, width), half_type),
+            pltpu.VMEM((2, 2, ctx, *slice_o.shape[2:]), half_type),
             pltpu.VMEM((2, 2, ctx, rows, 2 * columns), half_type),
             pltpu.VMEM((2, 2, ctx, rows, columns), half_type),
             pltpu.VMEM((count, 2 * columns), single),
@@ -564,7 +566,7 @@
             collective_id=ident, has_side_effects=True, vmem_limit_bytes=VMEM_ALL
         ),
         name=f"mlp_forward_{ident}",
-    )(attn, hidden, scale, dy_all, part_p, part_d)
+    )(att, hidden, scale, dy_all, part_p, part_d, slice_o)
 
 
 def token_products(source, left, weight, held, load):
@@ -603,11 +605,11 @@
 
 
 def back_kernel(fs, ctx, ten, *refs):
-    low_t, dy_t, hid, dpair, mid, cot, scale, slice_p = refs[:8]
-    dmid, dmid_all, terms, out_p, out_d = refs[8:13]
-    dws, nears, fars = refs[13:15], refs[15:17], refs[17:19]
-    source, first, line, held = refs[19:23]
-    load, local, send, recv_c, recv_y, recv_z, recv_tx, recv_t, recv_x = refs[23:]
+    low_t, dy_t, hid, dpair, mid, cot, scale, slice_p, slice_o = refs[:9]
+    dmid, dmid_all, datt, terms, out_p, out_d = refs[9:15]
+    dws, nears, fars = refs[15:17], refs[17:19], refs[19:21]
+    source, first, line, held, held_o, sums = refs[21:27]
+    load, local, send, recv_c, recv_y, recv_z, recv_tx, recv_t, recv_x = refs[27:]
     f, y, core, twin, across = fsdp_place(fs)
     z, x = lax.axis_index("context"), lax.axis_index("tensor")
     chips = fs // 2
@@ -660,12 +662,12 @@
     over_chips(0)
     token_products(source, dpair, slice_p, held, load)
     token_start(source, first, recv_tx, out, beside, owners)
+    over_context(0, 0)
     products(1)
     over_chips(1)
     for d, send_z in enumerate(sends):
         token_send(send_z, source, first, recv_tx, line, recv_t, x, out)
-        over_context(0, d)
-    over_context(0, ctx - 1)
+        over_context(0, d + 1)
     dnorm = token_sum(z, own_slots, source, first, recv_tx, line, recv_t, x)
     values = mid[...]
     inverse = lax.rsqrt(jnp.mean(values * values, axis=-1, keepdims=True) + norm_eps)
@@ -683,6 +685,25 @@
         over_context(1, d)
     for other in beside:
         arrived(dmid_all.at[other], recv_x.at[other], twin)
+    count, width = dmid_all.shape[0] * dmid_all.shape[1], dmid_all.shape[2]
+    deep = width // chips
+
+    def use(k, tile):
+        lanes = pl.ds(pl.multiple_of(k * deep, deep), deep)
+        add = jnp.dot(
+            dmid_all[:, :, lanes].reshape(count, deep), tile, preferred_element_type=single
+        )
+
+        @pl.when(k == 0)
+        def _():
+            sums[...] = add
+
+        @pl.when(k > 0)
+        def _():
+            sums[...] += add
+
+    chip_tiles(slice_o, held_o, load, use)
+    datt[...] = cast(sums[...])
     for w in range(2):
         for k in around[1:]:
             arrived(outs[w].at[k], recv_z.at[w, k], twin)
@@ -691,7 +712,7 @@
     out.drain()
 
 
-def mlp_back(low_t, dy_t, hid, dpair, mid, cot, scale, slice_p, fs, ctx, ten, ident):
+def mlp_back(low_t, dy_t, hid, dpair, mid, cot, scale, slice_p, slice_o, fs, ctx, ten, ident):
     rows, columns = low_t.shape[2], hid.shape[1]
     t_rows, width = mid.shape
     chips = fs // 2
@@ -704,20 +725,23 @@
         out_shape=[
             shape((t_rows, width), single),
             shape((ten, t_rows, width), half_type),
+            shape((ten * t_rows, slice_o.shape[3]), half_type),
             shape((1, width), single),
             shape((ctx, rows, 2 * columns), half_type),
             shape((ctx, rows, columns), half_type),
         ],
-        in_specs=[VMEM] * 7 + [ANY],
-        out_specs=[VMEM] * 3 + [ANY] * 2,
+        in_specs=[VMEM] * 7 + [ANY] * 2,
+        out_specs=[VMEM] * 4 + [ANY] * 2,
         scratch_shapes=[pltpu.VMEM((fs, ctx, *b), half_type) for b in blocks]
         + [pltpu.VMEM((chips, ctx, *b), half_type) for b in blocks]
         + [pltpu.VMEM((chips - 1, ctx, *b), half_type) for b in blocks]
         + [
             pltpu.VMEM((ctx, ten, t_rows, width), half_type),
             pltpu.VMEM((ten - 1, ctx, t_rows, width), half_type),
-            pltpu.VMEM((ctx + 1, t_rows, width), half_type),
+            pltpu.VMEM((ctx, t_rows, width), half_type),
             pltpu.VMEM((2, 2, ctx, rows, 2 * columns), half_type),
+            pltpu.VMEM((2, 2, ctx, *slice_o.shape[2:]), half_type),
+            pltpu.VMEM((ten * t_rows, slice_o.shape[3]), single),
             dma((2,)),
             dma((2,)),
             dma((sends,)),
@@ -732,7 +756,7 @@
             collective_id=ident, has_side_effects=True, vmem_limit_bytes=VMEM_ALL
         ),
         name=f"mlp_back_{ident}",
-    )(low_t, dy_t, hid, dpair, mid, cot, scale, slice_p)
+    )(low_t, dy_t, hid, dpair, mid, cot, scale, slice_p, slice_o)
 
 
 def update_kernel(parts, *refs):
@@ -839,11 +863,17 @@
     token_start(own_sums, first_k, recv_kx, out, beside, order)
     start(2)
     over_chips(2)
+    token_products(source, hid, slice_d, held_d, load)
+    token_start(source, first, recv_tx, out, beside, order)
     start(3)
     over_chips(3)
-    for d, send_z in enumerate(sends):
-        token_send(send_z, own_sums, first_k, recv_kx, line_k, recv_k, x, out)
+    early, late = range(ctx // 2), range(ctx // 2, ctx - 1)
+    for d in early:
+        token_send(sends[d], own_sums, first_k, recv_kx, line_k, recv_k, x, out)
+    for d in early:
         over_context(2, d)
+    for d in late:
+        token_send(sends[d], own_sums, first_k, recv_kx, line_k, recv_k, x, out)
     summed = token_sum(z, own_slots, own_sums, first_k, recv_kx, line_k, recv_k, x)
     half = summed.shape[1] // 2
     a, b = summed[:, :half], summed[:, half:]
@@ -852,14 +882,21 @@
     d_qkv[:, :heads] = d_query[...]
     d_qkv[:, heads : heads + half] = cast(jnp.where(is_key, a * c + b * s, a))
     d_qkv[:, heads + half :] = cast(jnp.where(is_key, b * c - a * s, b))
+    start(0)
+    over_chips(0)
+    for d in late:
+        over_context(2, d)
     token_products(dnorm, d_qkv, slice_q, held_q, load)
     for other in beside:
         out.push(dnorm.at[0, other], take.at[x], recv_n.at[x], {"tensor": other})
-    start(0)
-    over_chips(0)
-    token_products(source, hid, slice_d, held_d, load)
-    token_start(source, first, recv_tx, out, beside, order)
-    for d in range(ctx - 1):
+    for d in early:
+        token_send(sends[d], source, first, recv_tx, line, recv_t, x, out)
+    for d in early:
+        over_context(3, d)
+    start(1)
+    for d in late:
+        token_send(sends[d], source, first, recv_tx, line, recv_t, x, out)
+    for d in late:
         over_context(3, d)
     dnorm_one = dnorm[0, x].astype(single)
     for other in beside:
@@ -880,7 +917,6 @@
         dws[4][j // ctx, j % ctx, 0:1, :rows] = sums[:, at]
         dws[4][j // ctx, j % ctx, 1:2, :rows] = terms[:, at]
     start(4)
-    start(1)
     over_chips(4)
     over_chips(1)
 
@@ -889,18 +925,21 @@
             out.push(tokens.at[x, t], tokens.at[x, t], recv_x.at[2 + t, x], {"tensor": other})
 
     hand_over(1)
-    for d, send_z in enumerate(sends):
-        token_send(send_z, source, first, recv_tx, line, recv_t, x, out)
+    for d in early:
         over_context(0, d)
-    for d in range(ctx - 1):
+    tokens[x, 0] = cast(
+        mid[...] + token_sum(z, own_slots, source, first, recv_tx, line, recv_t, x)
+    )
+    hand_over(0)
+    for d in early:
         over_context(4, d)
-    for d in range(ctx - 1):
+    for d in late:
+        over_context(0, d)
+    for d in early:
         over_context(1, d)
-        if d == 0:
-            tokens[x, 0] = cast(
-                mid[...] + token_sum(z, own_slots, source, first, recv_tx, line, recv_t, x)
-            )
-            hand_over(0)
+    for w in (4, 1):
+        for d in late:
+            over_context(w, d)
     pool[x] = finish(4)
     for other in beside:
         out.push(pool.at[x], pool.at[x], recv_x.at[0, x], {"tensor": other})
@@ -1053,7 +1092,6 @@
     f = lax.axis_index("fsdp")
     seg_all = lax.dynamic_index_in_dim(small_all[:, :, 2, :block], f, 0, False).reshape(-1)
     qkv_full = qkv_all.reshape(width, -1)
-    out_full = out_all.reshape(width, -1)
 
     _, _, low_one = rms_forward(hidden, scale_one)
     qkv = dot(low_one, qkv_full, ((1,), (0,)))
@@ -1081,25 +1119,25 @@
         jnp.einsum("hbj,jd->bhd", prob_low, values_all, preferred_element_type=single)
     )
     att_flat = att_low.reshape(block, heads_width)
-    attn_part = dot(att_flat, out_full, ((1,), (1,)))
-    slice_p, slice_d, hid, dpair, low_t, dy_t, mid_half, _ = mlp_forward(
-        cast(attn_part).reshape(ten, half_rows, width),
+    slice_p, slice_d, hid, dpair, low_t, dy_t, mid_half = mlp_forward(
+        att_flat,
         hidden_half,
         scale_two[None],
         dy_all,
         part_p,
         part_d,
+        out_all,
         fs,
         ctx,
         ten,
         4,
     )
-    dmid_half, dmid_low, terms_two, part_p, part_d = mlp_back(
-        low_t, dy_t, hid, dpair, mid_half, cot_half, scale_two[None], slice_p, fs, ctx, ten, 5
+    dmid_half, dmid_low, datt, terms_two, part_p, part_d = mlp_back(
+        low_t, dy_t, hid, dpair, mid_half, cot_half, scale_two[None], slice_p, out_all, fs, ctx, ten, 5
     )
 
     dmid_low = dmid_low.reshape(block, width)
-    datt_low = cast(dot(dmid_low, out_full, ((1,), (0,)))).reshape(block, heads_here, HD)
+    datt_low = datt.reshape(block, heads_here, HD)
     delta = jnp.einsum("bhd,bhd->hb", datt_low, att_low, preferred_element_type=single)
     dprob = jnp.einsum("bhd,jd->hbj", datt_low, values_all, preferred_element_type=single)
     dscore_low = cast(prob * (dprob - delta[..., None]))

time: 607 us -> 580 us (0.956)
  Pallas kernels: 540 us -> 520 us
  matrix products: 17.2 us -> 7.97 us
    dot_general x3 -> x1, matrix products: 14.7 us -> 4.48 us  [dot(): lax.dot_general(a, b, (dims, ((), ())), preferred_element_type=single)]
    pallas_call x1, Pallas kernels: 132 us -> 125 us  [mlp_forward(): pl.pallas_call(functools.partial(forward_kernel, fs, ctx, ten), out_shape...]
    pallas_call x1, Pallas kernels: 143 us -> 136 us  [mlp_back(): pl.pallas_call(functools.partial(back_kernel, fs, ctx, ten), out_shape=[s...]
where the time goes in v4:
time: 580 us; the launch traced here: 571 us
  Pallas kernels  520 us (90%)
  local copies, waits for them, and re-layouts  21 us (4%)
  other arithmetic  20.4 us (4%)
  matrix products  7.97 us (1%)
    pallas_call x1, Pallas kernels, mlp_back(): pl.pallas_call(functools.partial(back_kernel, fs, ctx, ten), out_shape=[s...  136 us
    pallas_call x1, Pallas kernels, attn_back(): pl.pallas_call(functools.partial(attn_kernel, fs, ctx, ten), out_shape=[s...  125 us
    pallas_call x1, Pallas kernels, mlp_forward(): pl.pallas_call(functools.partial(forward_kernel, fs, ctx, ten), out_shape...  125 us
    pallas_call x1, Pallas kernels, spread(): pl.pallas_call(functools.partial(first_kernel, fs, ctx, ten, count), out_...  85.5 us
    pallas_call x2, Pallas kernels, update(): pl.pallas_call(update_kernel, grid=(rows // step,), out_shape=[jax.ShapeD...  25.3 us
    pallas_call x1, Pallas kernels, tokens_to_all(): pl.pallas_call(functools.partial(tokens_kernel, ctx, ten), out_shape=jax....  22.4 us

profile of v4, /device:TPU:8, one launch (start us, length us, event | category | flops | bytes accessed | tf_op | source)
XLA Modules:
  0.0 571.1 jit_solution(17174668258805659864)
XLA Ops:
  0.7 2.6 fusion.43
  3.3 1.0 dynamic-slice_convert_fusion
  7.1 85.5 %spread_1.1 = (f32[4,4,8,256]{3,2,1,0:T(8,128)}, bf16[4,4,160,1536]{3,2,1,0:T(8,128)(2,1)}, bf16[4,4,160,1280]{3,2,1,0:T(8,128)(2,1)}, bf16[4,2,64,2560]{3,2,1,0...) custom-call(f32[8,256]{1,0:T(8,128)} %stack.22.refs_0_, ...), custom_call_target="tpu_custom_call" | custom-call | tf_op jit(solution)/shard_map/spread_1/pallas_call | solution.py:296
  92.7 1.8 convert_reduce_fusion
  94.5 1.5 fusion.4
  96.1 4.5 fusion.13
  101.6 22.4 %tokens_2.1 = bf16[4,2,128,256]{3,2,1,0:T(8,128)(2,1)} custom-call(bf16[128,256]{1,0:T(8,128)(2,1)} %fusion.23.src), custom_call_target="tpu_custom_call" | custom-call | tf_op jit(solution)/shard_map/tokens_2/pallas_call | solution.py:176
  124.1 1.1 fusion.46
  126.8 0.9 slice.61
  131.8 125.0 %mlp_forward_4.1 = (bf16[4,4,160,1920]{3,2,1,0:T(8,128)(2,1)}, bf16[4,4,160,960]{3,2,1,0:T(8,128)(2,1)}, bf16[512,960]{1,0:T(8,128)(2,1)}, bf16[512,1920]{1,0:T(...) custom-call(bf16[128,1280]{1,0:T(8,128)(2,1)} %copy.81.refs_0_.refs_3_, ...), custom_call_target="tpu_custom_call" | custom-call | tf_op jit(solution)/shard_map/mlp_forward_4/pallas_call | solution.py:535
  256.8 136.3 %mlp_back_5.1 = (f32[64,2560]{1,0:T(8,128)}, bf16[2,64,2560]{2,1,0:T(8,128)(2,1)}, bf16[128,1280]{1,0:T(8,128)(2,1)}, f32[1,2560]{1,0:T(1,128)}, bf16[4,160,1920...) custom-call(bf16[4,4,160,512]{3,2,1,0:T(8,128)(2,1)} %get-tuple-element.76.refs_0_, ...), custom_call_target="tpu_custom_call" | custom-call | tf_op jit(solution)/shard_map/mlp_back_5/pallas_call | solution.py:723
  393.1 15.8 %update_5.1 = (f32[160,3840]{1,0:T(8,128)}, f32[160,3840]{1,0:T(8,128)}, f32[160,3840]{1,0:T(8,128)}, f32[160,3840]{1,0:T(8,128)}, f32[160,3840]{1,0:T(8,128)}, ...) custom-call(bf16[4,160,1920]{2,1,0:T(8,128)(2,1)} %get-tuple-element.92.parts, f32[160,3840]{1,0:T(8,128)} %refs_0_.1, ...), custom_call_target="tpu_custom_call" | custom-call | tf_op jit(solution)/shard_map/update_5/pallas_call | solution.py:783
  408.9 1.3 copy.83
  410.2 1.1 fusion.18
  411.3 1.5 fusion.3
  416.7 1.1 copy.82
  417.9 1.1 copy.75
  419.7 125.4 %attn_back_9.1 = (f32[160,1280]{1,0:T(8,128)}, f32[160,1280]{1,0:T(8,128)}, f32[8,256]{1,0:T(8,128)}, f32[160,512]{1,0:T(8,128)}, bf16[2,2,64,2560]{3,2,1,0:T(8,128)(2,1)}) custom-call(bf16[4,4,160,128]{3,2,1,0:T(8,128)(2,1)} %bitcast.111, bf16[4,4,160,128]{3,2,1,0:T(8,128)(2,1)} %bitcast.110, bf16[128,1280]{1,0:T(8,128)(2,1)} %copy.90.refs_2_, ...), custom_call_target="tpu_custom_call" | custom-call | tf_op jit(solution)/shard_map/attn_back_9/pallas_call | solution.py:994
  545.2 1.6 convert_bitcast_fusion
  546.8 1.7 fusion.44
  549.6 1.8 multiply_subtract_fusion.1
  552.4 1.8 multiply_subtract_fusion
  554.2 9.5 %update_7.1 = (f32[160,3840]{1,0:T(8,128)}, f32[160,3840]{1,0:T(8,128)}, f32[160,3840]{1,0:T(8,128)}, f32[160,3840]{1,0:T(8,128)}) custom-call(bf16[4,160,960]{2,1,0:T(8,128)(2,1)} %get-tuple-element.95.parts, f32[160,3840]{1,0:T(8,128)} %bitcast.108, f32[160,3840]{1,0:T(8,128)} %bitcast.113, f32[160,3840]{1,0:T(8,128)} %bitcast.114), custom_call_target="tpu_custom_call" | custom-call | tf_op jit(solution)/shard_map/update_7/pallas_call | solution.py:783
  563.8 2.5 multiply_subtract_fusion.2
  (154 shorter events, 20.6 us)
Async XLA Ops:
  0.7 3.6 copy-start.4
  3.3 3.0 copy-start.6
  92.6 3.4 copy-start
  94.5 6.0 %copy-start.32 = (f32[2560]{0:T(1024)}, f32[2560]{0:T(1024)S(1)}, u32[]{:S(2)}) copy-start(f32[2560]{0:T(1024)S(1)} %add.143) | copy-start | bytes 30724
  96.1 4.5 copy-start.43
  96.1 4.5 copy-start.52
  125.1 2.8 copy-start.12
  125.1 3.5 copy-start.31
  128.7 2.4 copy-start.35
  546.8 2.6 copy-start.24
  546.8 2.8 copy-start.25
  549.6 2.5 copy-start.26
  549.6 2.8 copy-start.27
  563.7 3.4 copy-start.38
  563.7 3.4 copy-start.47
  563.7 3.4 copy-start.48
  563.8 3.9 copy-start.40
  563.8 3.9 copy-start.49
  563.8 3.9 copy-start.50
  563.8 4.5 copy-start.11
  566.3 2.9 copy-start.14
  566.3 3.7 copy-start.9
  567.1 3.7 copy-start.41
  567.1 3.7 copy-start.42
  (29 other events, 45.2 us)

commit v5 on v4

--- a/solution.py
+++ b/solution.py
@@ -383,8 +383,9 @@
     width = hidden.shape[1]
     count = hid.shape[0]
     beside = [{"tensor": lax.rem(x + d, ten)} for d in range(1, ten)]
-    around = [lax.rem(z + d, ctx) for d in range(ctx)]
-    back = [lax.rem(z + ctx - d, ctx) for d in range(ctx)]
+    shifts = sorted(range(ctx), key=lambda d: (min(d, ctx - d), d))
+    around = [lax.rem(z + d, ctx) for d in shifts]
+    back = [lax.rem(z + ctx - d, ctx) for d in shifts]
     greet([{"context": k} for k in around[1:]] + across + [twin] + beside)
     out = Sends(send)
     parts, slices, recvs = (part_p, part_d), (slice_p, slice_d), (recv_p, recv_d)
@@ -775,7 +776,7 @@
 
 def update(parts, weights, ident):
     ctx, rows, columns = parts.shape
-    step = 32 if rows % 32 == 0 else 8
+    step = 80 if rows % 80 == 0 else 8
     wide = weights[0][0].shape[1]
     spec = pl.BlockSpec((step, wide), lambda i: (i, 0))
     part = pl.BlockSpec((ctx, step, columns), lambda i: (0, i, 0))

time: 580 us -> 571 us (0.984)
  Pallas kernels: 520 us -> 510 us
where the time goes in v5:
time: 571 us; the launch traced here: 562 us
  Pallas kernels  510 us (89%)
  local copies, waits for them, and re-layouts  21 us (4%)
  other arithmetic  20.4 us (4%)
  matrix products  7.97 us (1%)
    pallas_call x1, Pallas kernels, mlp_back(): pl.pallas_call(functools.partial(back_kernel, fs, ctx, ten), out_shape=[s...  138 us
    pallas_call x1, Pallas kernels, attn_back(): pl.pallas_call(functools.partial(attn_kernel, fs, ctx, ten), out_shape=[s...  125 us
    pallas_call x1, Pallas kernels, mlp_forward(): pl.pallas_call(functools.partial(forward_kernel, fs, ctx, ten), out_shape...  120 us
    pallas_call x1, Pallas kernels, spread(): pl.pallas_call(functools.partial(first_kernel, fs, ctx, ten, count), out_...  85.5 us
    pallas_call x1, Pallas kernels, tokens_to_all(): pl.pallas_call(functools.partial(tokens_kernel, ctx, ten), out_shape=jax....  22.5 us
    pallas_call x2, Pallas kernels, update(): pl.pallas_call(update_kernel, grid=(rows // step,), out_shape=[jax.ShapeD...  19.7 us

profile of v5, /device:TPU:8, one launch (start us, length us, event | category | flops | bytes accessed | tf_op | source)
XLA Modules:
  0.0 561.5 jit_solution(14340946550320228652)
XLA Ops:
  0.7 2.6 fusion.43
  3.3 1.0 dynamic-slice_convert_fusion
  7.1 85.5 %spread_1.1 = (f32[4,4,8,256]{3,2,1,0:T(8,128)}, bf16[4,4,160,1536]{3,2,1,0:T(8,128)(2,1)}, bf16[4,4,160,1280]{3,2,1,0:T(8,128)(2,1)}, bf16[4,2,64,2560]{3,2,1,0...) custom-call(f32[8,256]{1,0:T(8,128)} %stack.22.refs_0_, ...), custom_call_target="tpu_custom_call" | custom-call | tf_op jit(solution)/shard_map/spread_1/pallas_call | solution.py:296
  92.7 1.8 convert_reduce_fusion
  94.5 1.5 fusion.4
  96.1 4.5 fusion.13
  101.6 22.5 %tokens_2.1 = bf16[4,2,128,256]{3,2,1,0:T(8,128)(2,1)} custom-call(bf16[128,256]{1,0:T(8,128)(2,1)} %fusion.23.src), custom_call_target="tpu_custom_call" | custom-call | tf_op jit(solution)/shard_map/tokens_2/pallas_call | solution.py:176
  124.1 1.1 fusion.46
  126.8 0.9 slice.61
  131.8 120.4 %mlp_forward_4.1 = (bf16[4,4,160,1920]{3,2,1,0:T(8,128)(2,1)}, bf16[4,4,160,960]{3,2,1,0:T(8,128)(2,1)}, bf16[512,960]{1,0:T(8,128)(2,1)}, bf16[512,1920]{1,0:T(...) custom-call(bf16[128,1280]{1,0:T(8,128)(2,1)} %copy.81.refs_0_.refs_3_, ...), custom_call_target="tpu_custom_call" | custom-call | tf_op jit(solution)/shard_map/mlp_forward_4/pallas_call | solution.py:536
  252.2 137.7 %mlp_back_5.1 = (f32[64,2560]{1,0:T(8,128)}, bf16[2,64,2560]{2,1,0:T(8,128)(2,1)}, bf16[128,1280]{1,0:T(8,128)(2,1)}, f32[1,2560]{1,0:T(1,128)}, bf16[4,160,1920...) custom-call(bf16[4,4,160,512]{3,2,1,0:T(8,128)(2,1)} %get-tuple-element.76.refs_0_, ...), custom_call_target="tpu_custom_call" | custom-call | tf_op jit(solution)/shard_map/mlp_back_5/pallas_call | solution.py:724
  389.9 12.5 %update_5.1 = (f32[160,3840]{1,0:T(8,128)}, f32[160,3840]{1,0:T(8,128)}, f32[160,3840]{1,0:T(8,128)}, f32[160,3840]{1,0:T(8,128)}, f32[160,3840]{1,0:T(8,128)}, ...) custom-call(bf16[4,160,1920]{2,1,0:T(8,128)(2,1)} %get-tuple-element.92.parts, f32[160,3840]{1,0:T(8,128)} %refs_0_.1, ...), custom_call_target="tpu_custom_call" | custom-call | tf_op jit(solution)/shard_map/update_5/pallas_call | solution.py:784
  402.4 1.3 copy.83
  403.7 1.1 fusion.18
  404.8 1.5 fusion.3
  410.2 1.1 copy.82
  411.5 1.1 copy.75
  413.2 124.7 %attn_back_9.1 = (f32[160,1280]{1,0:T(8,128)}, f32[160,1280]{1,0:T(8,128)}, f32[8,256]{1,0:T(8,128)}, f32[160,512]{1,0:T(8,128)}, bf16[2,2,64,2560]{3,2,1,0:T(8,128)(2,1)}) custom-call(bf16[4,4,160,128]{3,2,1,0:T(8,128)(2,1)} %bitcast.111, bf16[4,4,160,128]{3,2,1,0:T(8,128)(2,1)} %bitcast.110, bf16[128,1280]{1,0:T(8,128)(2,1)} %copy.90.refs_2_, ...), custom_call_target="tpu_custom_call" | custom-call | tf_op jit(solution)/shard_map/attn_back_9/pallas_call | solution.py:995
  538.0 1.6 convert_bitcast_fusion
  539.6 1.7 fusion.44
  542.4 1.8 multiply_subtract_fusion.1
  545.2 1.8 multiply_subtract_fusion
  547.0 7.2 %update_7.1 = (f32[160,3840]{1,0:T(8,128)}, f32[160,3840]{1,0:T(8,128)}, f32[160,3840]{1,0:T(8,128)}, f32[160,3840]{1,0:T(8,128)}) custom-call(bf16[4,160,960]{2,1,0:T(8,128)(2,1)} %get-tuple-element.95.parts, f32[160,3840]{1,0:T(8,128)} %bitcast.108, f32[160,3840]{1,0:T(8,128)} %bitcast.113, f32[160,3840]{1,0:T(8,128)} %bitcast.114), custom_call_target="tpu_custom_call" | custom-call | tf_op jit(solution)/shard_map/update_7/pallas_call | solution.py:784
  554.3 2.5 multiply_subtract_fusion.2
  (154 shorter events, 20.6 us)
Async XLA Ops:
  0.7 3.6 copy-start.4
  3.3 3.0 copy-start.6
  92.6 3.4 copy-start
  94.5 6.0 %copy-start.32 = (f32[2560]{0:T(1024)}, f32[2560]{0:T(1024)S(1)}, u32[]{:S(2)}) copy-start(f32[2560]{0:T(1024)S(1)} %add.143) | copy-start | bytes 30724
  96.1 4.5 copy-start.43
  96.1 4.5 copy-start.52
  125.1 2.8 copy-start.12
  125.1 3.5 copy-start.31
  128.7 2.4 copy-start.35
  539.6 2.6 copy-start.24
  539.6 2.8 copy-start.25
  542.4 2.5 copy-start.26
  542.4 2.8 copy-start.27
  554.2 3.4 copy-start.38
  554.2 3.4 copy-start.47
  554.2 3.4 copy-start.48
  554.3 3.9 copy-start.40
  554.3 3.9 copy-start.49
  554.3 3.9 copy-start.50
  554.3 4.5 copy-start.11
  556.8 2.9 copy-start.14
  556.8 3.7 copy-start.9
  557.6 3.7 copy-start.41
  557.6 3.7 copy-start.42
  (29 other events, 45.2 us)
